TPU v7x, 8 devices: a whole 2x2x1 slice. The times are simulated.
8 devices in a mesh: dp: 1 (over z), y: 2 (over y), x: 4 (over x, core).
Axes of the slice: x: 2, y: 2, z: 1, core: 2. Of those that a mesh axis runs over, the one named last changes fastest.
Arguments:
- tokens: int32 [3, 256], P(None, 'dp')
- lengths: int32 [256], P('dp')
- choices: int32 [3, 256, 8], P(None, 'dp')
- emb_table: bfloat16 [49155, 1536], P(None, 'x')
- k_cache: bfloat16 [256, 256, 8, 64], P('dp', None, 'y')
- v_cache: bfloat16 [256, 256, 8, 64], P('dp', None, 'y')
- g_attn: bfloat16 [1536], P('x')
- w_q: bfloat16 [1536, 1536], P('x', 'y')
- w_k: bfloat16 [1536, 512], P('x', 'y')
- w_v: bfloat16 [1536, 512], P('x', 'y')
- w_o: bfloat16 [1536, 1536], P('y', 'x')
- g_ffn: bfloat16 [1536], P('x')
- w_router: bfloat16 [1536, 40], P('x')
- w_act: bfloat16 [40, 1536, 512], P(None, 'x', 'y')
- w_lin: bfloat16 [40, 1536, 512], P(None, 'x', 'y')
- w_down: bfloat16 [40, 512, 1536], P(None, 'y', 'x')
Outputs:
- output 1: bfloat16 [3, 256, 1536], P(None, 'dp', 'x')
- output 2: bfloat16 [256, 256, 8, 64], P('dp', None, 'y')
- output 3: bfloat16 [256, 256, 8, 64], P('dp', None, 'y')
All inputs are finite; a program needn't handle non-finite values.
Results may differ from a plain program's by a relative error of at most 0.0112615.
Values are sent between devices in bfloat16 or wider.
A program may use at most 1 GiB of HBM per device.

v0:
```python
import jax
import jax.numpy as jnp
from jax import lax
from jax.sharding import PartitionSpec as P

EPS = 1e-5
ROPE_BASE = 1.0e6


def shard_norm(x_val, gain_vec, width_full):
    x_f32 = x_val.astype(jnp.float32)
    sq_total = lax.psum(jnp.sum(x_f32 * x_f32, axis=-1, keepdims=True), 'x')
    return (x_f32 * lax.rsqrt(sq_total / width_full + EPS) * gain_vec.astype(jnp.float32)).astype(jnp.bfloat16)


def rotate(vectors, positions):
    head_dim = vectors.shape[-1]
    half_dim = head_dim // 2
    inv_freq = ROPE_BASE ** (-(jnp.arange(half_dim, dtype=jnp.float32) * 2.0 / head_dim))
    angle_shape = (vectors.shape[0],) + (1,) * (vectors.ndim - 2) + (half_dim,)
    angles = (positions.astype(jnp.float32)[:, None] * inv_freq[None, :]).reshape(angle_shape)
    cosine = jnp.cos(angles)
    sine_val = jnp.sin(angles)
    first_half = vectors[..., :half_dim].astype(jnp.float32)
    second_half = vectors[..., half_dim:].astype(jnp.float32)
    return jnp.concatenate([first_half * cosine - second_half * sine_val, second_half * cosine + first_half * sine_val], axis=-1).astype(jnp.bfloat16)


def write_slot(cache_arr, new_rows, positions):
    hit_mask = (jnp.arange(cache_arr.shape[1])[None, :] == positions[:, None])[:, :, None, None]
    return jnp.where(hit_mask, new_rows[:, None], cache_arr)


def attention(queries, key_cache, val_cache, positions):
    head_dim = queries.shape[-1]
    scores = jnp.einsum('bkgh,bskh->bkgs', queries, key_cache, preferred_element_type=jnp.float32) * head_dim ** -0.5
    valid_mask = (jnp.arange(key_cache.shape[1])[None, :] <= positions[:, None])[:, None, None, :]
    scores = jnp.where(valid_mask, scores, -1.0e30)
    peak_val = jnp.max(scores, axis=-1, keepdims=True)
    weight = jnp.where(valid_mask, jnp.exp(scores - peak_val), 0.0)
    total_w = jnp.sum(weight, axis=-1, keepdims=True)
    mixed_out = jnp.einsum('bkgs,bskh->bkgh', weight.astype(jnp.bfloat16), val_cache, preferred_element_type=jnp.float32)
    return (mixed_out / total_w).astype(jnp.bfloat16)


def mixing(logits, choice_row, experts):
    gate_val = jax.nn.softmax(jnp.take_along_axis(logits, choice_row, axis=1), axis=-1)
    onehot = choice_row[:, :, None] == jnp.arange(experts)[None, None, :]
    return jnp.sum(jnp.where(onehot, gate_val[:, :, None], 0.0), axis=1)


def solution(mesh):
    x_count = mesh.shape['x']
    cache_spec = P('dp', None, 'y', None)
    in_specs = (P(None, 'dp'), P('dp'), P(None, 'dp', None), P(None, 'x'), cache_spec, cache_spec, P('x'), P('x', 'y'), P('x', 'y'), P('x', 'y'), P('y', 'x'), P('x'), P('x', None), P(None, 'x', 'y'), P(None, 'x', 'y'), P(None, 'y', 'x'))
    out_specs = (P(None, 'dp', 'x'), cache_spec, cache_spec)

    def per_device(tokens, lengths, choices, emb_table, k_cache, v_cache, g_attn, w_q, w_k, w_v, w_o, g_ffn, w_router, w_act, w_lin, w_down):
        n_batch = tokens.shape[1]
        kv_local, head_dim = k_cache.shape[2], k_cache.shape[3]
        q_cols = w_q.shape[1]
        kv_cols = w_k.shape[1]
        group_size = q_cols // head_dim // kv_local
        width_full = emb_table.shape[1] * x_count
        experts = w_act.shape[0]
        key_cache, val_cache = k_cache, v_cache
        step_outs = []
        for step_idx in range(tokens.shape[0]):
            positions = lengths + step_idx
            x_in = jnp.take(emb_table, tokens[step_idx], axis=0)
            normed = shard_norm(x_in, g_attn, width_full)
            proj_part = jnp.concatenate([jnp.dot(normed, w_q, preferred_element_type=jnp.float32), jnp.dot(normed, w_k, preferred_element_type=jnp.float32), jnp.dot(normed, w_v, preferred_element_type=jnp.float32)], axis=1).astype(jnp.bfloat16)
            proj_sum = lax.psum(proj_part, 'x')
            queries = rotate(proj_sum[:, :q_cols].reshape(n_batch, kv_local, group_size, head_dim), positions)
            new_keys = rotate(proj_sum[:, q_cols:q_cols + kv_cols].reshape(n_batch, kv_local, head_dim), positions)
            new_vals = proj_sum[:, q_cols + kv_cols:].reshape(n_batch, kv_local, head_dim)
            key_cache = write_slot(key_cache, new_keys, positions)
            val_cache = write_slot(val_cache, new_vals, positions)
            mixed = attention(queries, key_cache, val_cache, positions).reshape(n_batch, q_cols)
            attn_sum = lax.psum(jnp.dot(mixed, w_o, preferred_element_type=jnp.float32).astype(jnp.bfloat16), 'y')
            x_mid = (x_in.astype(jnp.float32) + attn_sum.astype(jnp.float32)).astype(jnp.bfloat16)
            normed2 = shard_norm(x_mid, g_ffn, width_full)
            logits = lax.psum(jnp.dot(normed2, w_router, preferred_element_type=jnp.float32), 'x')
            coef = mixing(logits, choices[step_idx], experts)
            hidden_part = jnp.stack([jnp.einsum('bd,edf->ebf', normed2, w_act, preferred_element_type=jnp.float32), jnp.einsum('bd,edf->ebf', normed2, w_lin, preferred_element_type=jnp.float32)]).astype(jnp.bfloat16)
            hidden_sum = lax.psum(hidden_part, 'x')
            unit_bf16 = (coef.T[:, :, None] * jax.nn.silu(hidden_sum[0].astype(jnp.float32)) * hidden_sum[1].astype(jnp.float32)).astype(jnp.bfloat16)
            moe_sum = lax.psum(jnp.einsum('ebf,efd->bd', unit_bf16, w_down, preferred_element_type=jnp.float32).astype(jnp.bfloat16), 'y')
            step_outs.append((x_mid.astype(jnp.float32) + moe_sum.astype(jnp.float32)).astype(jnp.bfloat16))
        return jnp.stack(step_outs), key_cache, val_cache

    return jax.shard_map(per_device, mesh=mesh, in_specs=in_specs, out_specs=out_specs, check_vma=False)
```

profile of v0, /device:TPU:0, one launch (start us, length us, event | category | flops | bytes accessed | tf_op | source)
XLA Modules:
  0.0 990.6 jit_solution(9352087793308539571)
XLA Ops:
  8.2 2.7 gather_fusion.4
  10.9 2.7 gather_fusion.2
  13.6 2.7 gather_fusion
  17.0 8.8 all-reduce.2
  26.4 1.2 convolution_convert_fusion.6
  27.6 1.2 convolution_convert_fusion.7
  28.8 1.2 convolution_convert_fusion.8
  37.1 41.6 %all-reduce.17.cloned.1.call-done = (bf16[256,1280]{1,0:T(8,128)(2,1)}, bf16[256,1280]{1,0:T(8,128)(2,1)}, bf16[256,1280]{1,0:T(8,128)(2,1)}) async-done(((bf16[256,1280]{1,0:T(8,128)(2,1)}, bf16[256,1280]{1,0:T(8,128)(2,1)}, bf16[256,1280]{1,0:T(8,128)(2,1)}), (bf16[256,1280]{1,0:T(8,128)(2,1)}, bf16[256,1280]{1,0:T(8,128)(2,1)}, bf16[256,1280]{1,0:T(8,128)(2,1)})) %all-reduce.17.cloned.1.call-update) | async-done | bytes 1966096 | tf_op jit(solution)/shard_map/psum | solution.py:73
  79.7 1.0 slice.162
  81.7 1.0 slice.144
  83.7 1.0 slice.153
  87.1 1.9 copy.163
  88.9 22.7 %broadcast_select_fusion.29 = bf16[256,256,4,64]{1,3,2,0:T(8,128)(2,1)} fusion(pred[256,256]{1,0:T(8,128)(4,1)S(1)} %get-tuple-element.97, bf16[256,256,4,64]{1,3,2,0:T(8,128)(2,1)} %param.25, pred[256,256]{1,0:T(8,128)(4,1)S(1)} %get-tuple-element.79, bf16[256,4,64]{2,1,0:T(4,128)(2,1)S(1)} %copy.154, ...), kind=kLoop, calls=%fused_computation.11.clone.1.clone.clone.clone.1 | loop fusion | flops 33554432 | bytes 67502080 | tf_op jit(solution)/shard_map/bkgs,bskh->bkgh/dot_general | solution.py:42
  111.7 60.2 %broadcast_select_fusion.1 = (bf16[256,256,4,64]{1,3,2,0:T(8,128)(2,1)}, bf16[256,256,4,64]{1,3,2,0:T(8,128)(2,1)}) fusion(pred[256,256]{1,0:T(8,128)(4,1)S(1)} %get-tuple-element.81, bf16[256,256,4,64]{1,3,2,0:T(8,128)(2,1)} %param.24, pred[256,256]{1,0:T(8,128)(4,1)S(1)} %get-tuple-element.79, pred[256,256]{1,0:T(8,128)(4,1)S(1)} %get-tuple-element.97, ...), kind=kLoop, calls=%fused_computation.10 | loop fusion | flops 100663296 | bytes 135200768 | tf_op jit(solution)/shard_map/jit(_where)/select_n | solution.py:31
  171.9 15.4 %fusion.183 = (f32[256,4,3]{2,1,0:T(4,128)S(1)}, bf16[256,4,3,256]{3,2,1,0:T(4,128)(2,1)}) fusion(pred[256,256]{1,0:T(8,128)(4,1)S(1)} %copy-done.20, bf16[256,4,3,64]{3,2,1,0:T(4,128)(2,1)} %copy.163, bf16[256,256,4,64]{1,3,2,0:T(8,128)(2,1)} %get-tuple-element.50), kind=kOutput, calls=%fused_computation.302 | convolution fusion | flops 105382144 | bytes 35598336 | tf_op jit(solution)/shard_map/sub | solution.py:40
  187.4 15.9 %fusion.52 = bf16[256,4,3,64]{3,2,1,0:T(4,128)(2,1)} fusion(bf16[256,256,4,64]{1,3,2,0:T(8,128)(2,1)} %get-tuple-element.51, bf16[256,4,3,256]{3,2,1,0:T(4,128)(2,1)} %get-tuple-element.92, f32[256,4,3]{2,1,0:T(4,128)S(1)} %get-tuple-element.91), kind=kOutput, calls=%fused_computation.91 | convolution fusion | flops 101056512 | bytes 35532800 | tf_op jit(solution)/shard_map/bkgs,bskh->bkgh/dot_general | solution.py:42
  203.3 2.2 copy.166
  207.2 18.5 %fusion.184 = (f32[256,4,3]{2,1,0:T(4,128)}, bf16[256,4,3,256]{3,2,1,0:T(4,128)(2,1)}) fusion(pred[256,256]{1,0:T(8,128)(4,1)S(1)} %copy-done.18, bf16[256,4,3,64]{3,2,1,0:T(4,128)(2,1)S(1)} %copy.141, bf16[256,256,4,64]{1,3,2,0:T(8,128)(2,1)} %param.24, pred[256,256]{1,0:T(8,128)(4,1)S(1)} %get-tuple-element.79, bf16[256,4,64]{2,1,0:T(4,128)(2,1)S(1)} %copy.140), kind=kOutput, calls=%fused_computation.303 | convolution fusion | flops 122159360 | bytes 35794944 | tf_op jit(solution)/shard_map/sub | solution.py:40
  225.7 16.0 %divide_convert_fusion.1 = bf16[256,4,3,64]{3,2,1,0:T(4,128)(2,1)S(1)} fusion(f32[256,4,3]{2,1,0:T(4,128)} %get-tuple-element.93, bf16[256,256,4,64]{1,3,2,0:T(8,128)(2,1)} %param.25, pred[256,256]{1,0:T(8,128)(4,1)S(1)} %get-tuple-element.79, bf16[256,4,64]{2,1,0:T(4,128)(2,1)S(1)} %copy.143, bf16[256,4,3,256]{3,2,1,0:T(4,128)(2,1)} %get-tuple-element.94), kind=kOutput, calls=%fused_computation.87 | convolution fusion | flops 117833728 | bytes 35729408 | tf_op jit(solution)/shard_map/bkgs,bskh->bkgh/dot_general | solution.py:42
  241.8 1.1 copy.144
  242.9 2.1 convolution_convert_fusion.3
  245.0 2.1 convolution_convert_fusion.5
  248.2 26.3 %fusion.185 = (f32[256,4,3]{2,1,0:T(4,128)}, bf16[256,4,3,256]{3,2,1,0:T(4,128)(2,1)}) fusion(pred[256,256]{1,0:T(8,128)(4,1)S(1)} %copy-done.19, bf16[256,4,3,64]{3,2,1,0:T(4,128)(2,1)S(1)} %copy.152, pred[256,256]{1,0:T(8,128)(4,1)S(1)} %get-tuple-element.97, bf16[256,256,4,64]{1,3,2,0:T(8,128)(2,1)} %param.24, ...), kind=kOutput, calls=%fused_computation.304 | convolution fusion | flops 138936576 | bytes 35991552 | tf_op jit(solution)/shard_map/sub | solution.py:40
  274.6 15.0 %divide_convert_fusion = bf16[256,4,3,64]{3,2,1,0:T(4,128)(2,1)S(1)} fusion(f32[256,4,3]{2,1,0:T(4,128)} %get-tuple-element.95, bf16[256,4,3,256]{3,2,1,0:T(4,128)(2,1)} %get-tuple-element.96, bf16[256,256,4,64]{1,3,2,0:T(8,128)(2,1)} %broadcast_select_fusion.29), kind=kOutput, calls=%fused_computation.86 | convolution fusion | flops 101056512 | bytes 35532800 | tf_op jit(solution)/shard_map/bkgs,bskh->bkgh/dot_general | solution.py:42
  290.3 1.1 convolution_convert_fusion.4
  291.5 24.5 %all-reduce.21.cloned.1.call-done = (bf16[256,384]{1,0:T(8,128)(2,1)}, bf16[256,384]{1,0:T(8,128)(2,1)}, bf16[256,384]{1,0:T(8,128)(2,1)}) async-done(((bf16[256,384]{1,0:T(8,128)(2,1)}, bf16[256,384]{1,0:T(8,128)(2,1)}, bf16[256,384]{1,0:T(8,128)(2,1)}), (bf16[256,384]{1,0:T(8,128)(2,1)}, bf16[256,384]{1,0:T(8,128)(2,1)}, bf16[256,384]{1,0:T(8,128)(2,1)})) %all-reduce.21.cloned.1.call-update) | async-done | bytes 589840 | tf_op jit(solution)/shard_map/psum | solution.py:80
  316.0 1.2 fusion.109
  317.2 1.2 fusion.93
  318.4 1.2 fusion.101
  319.7 6.3 all-reduce.1
  326.0 8.1 convert_bitcast_fusion
  334.1 8.1 convert_bitcast_fusion.1
  342.3 4.8 convert_bitcast_fusion.2
  347.1 4.9 convert_bitcast_fusion.3
  352.0 4.7 convert_bitcast_fusion.4
  356.7 4.7 convert_bitcast_fusion.5
  364.0 9.0 pad_maximum_fusion.2
  373.0 8.8 pad_maximum_fusion.1
  381.9 9.0 pad_maximum_fusion
  392.4 15.5 %all-reduce.13.cloned.1.call-done = (f32[256,40]{0,1:T(8,128)}, f32[256,40]{0,1:T(8,128)}, f32[256,40]{0,1:T(8,128)}) async-done(((f32[256,40]{0,1:T(8,128)}, f32[256,40]{0,1:T(8,128)}, f32[256,40]{0,1:T(8,128)}), (f32[256,40]{0,1:T(8,128)}, f32[256,40]{0,1:T(8,128)}, f32[256,40]{0,1:T(8,128)})) %all-reduce.13.cloned.1.call-update) | async-done | bytes 122896 | tf_op jit(solution)/shard_map/psum | solution.py:83
  407.9 15.2 %gather_fusion.1 = f32[2048]{0:T(1024)S(1)} fusion(f32[256,40]{0,1:T(8,128)} %get-tuple-element.11, s32[2048]{0:T(1024)S(1)} %reshape.605), kind=kCustom, calls=%fused_computation.1.clone | custom fusion | bytes 32768 | tf_op jit(solution)/shard_map/jit(take_along_axis)/gather | solution.py:47
  423.9 16.8 %gather_fusion.5 = f32[2048]{0:T(1024)S(1)} fusion(f32[256,40]{0,1:T(8,128)S(1)} %copy-done.3, s32[2048]{0:T(1024)S(1)} %reshape.619), kind=kCustom, calls=%fused_computation.5.clone | custom fusion | bytes 32768 | tf_op jit(solution)/shard_map/jit(take_along_axis)/gather | solution.py:47
  441.5 16.8 %gather_fusion.3 = f32[2048]{0:T(1024)S(1)} fusion(f32[256,40]{0,1:T(8,128)S(1)} %copy-done.2, s32[2048]{0:T(1024)S(1)} %reshape.612), kind=kCustom, calls=%fused_computation.4.clone | custom fusion | bytes 32768 | tf_op jit(solution)/shard_map/jit(take_along_axis)/gather | solution.py:47
  458.7 470.4 %all-reduce.15.cloned.1.call-done = (bf16[2,40,256,256]{3,2,1,0:T(8,128)(2,1)}, bf16[2,40,256,256]{3,2,1,0:T(8,128)(2,1)}, bf16[2,40,256,256]{3,2,1,0:T(8,128)(2,1)}) async-done(((bf16[2,40,256,256]{3,2,1,0:T(8,128)(2,1)}, bf16[2,40,256,256]{3,2,1,0:T(8,128)(2,1)}, bf16[2,40,256,256]{3,2,1,0:T(8,128)(2,1)}), (bf16[2,40,256,256]{3,2,1,0:T(8,128)(2,1)}, bf16[2,40,256,256]{3,2,1,0:T(8,128)(2,1)}, ...) | async-done | bytes 31457296 | tf_op jit(solution)/shard_map/psum | solution.py:86
  929.1 10.2 %fusion.70 = bf16[256,384]{1,0:T(8,128)(2,1)} fusion(bf16[40,256,384]{2,1,0:T(8,128)(2,1)} %param.35, bf16[2,40,256,256]{3,2,1,0:T(8,128)(2,1)} %get-tuple-element.20, f32[40,256]{1,0:T(8,128)S(1)} %bitcast.249), kind=kOutput, calls=%fused_computation.103 | convolution fusion | flops 2036957184 | bytes 18587648 | tf_op jit(solution)/shard_map/ebf,efd->bd/dot_general | solution.py:88
  939.3 11.0 %fusion.67 = bf16[256,384]{1,0:T(8,128)(2,1)} fusion(bf16[40,256,384]{2,1,0:T(8,128)(2,1)} %param.35, bf16[2,40,256,256]{3,2,1,0:T(8,128)(2,1)S(1)} %copy-done.29, f32[40,256]{1,0:T(8,128)S(1)} %bitcast.250), kind=kOutput, calls=%fused_computation.102 | convolution fusion | flops 2036957184 | bytes 18587648 | tf_op jit(solution)/shard_map/ebf,efd->bd/dot_general | solution.py:88
  950.4 4.8 fusion.64
  955.2 24.8 %all-reduce.19.cloned.1.call-done = (bf16[256,384]{1,0:T(8,128)(2,1)}, bf16[256,384]{1,0:T(8,128)(2,1)}, bf16[256,384]{1,0:T(8,128)(2,1)}) async-done(((bf16[256,384]{1,0:T(8,128)(2,1)}, bf16[256,384]{1,0:T(8,128)(2,1)}, bf16[256,384]{1,0:T(8,128)(2,1)}), (bf16[256,384]{1,0:T(8,128)(2,1)}, bf16[256,384]{1,0:T(8,128)(2,1)}, bf16[256,384]{1,0:T(8,128)(2,1)})) %all-reduce.19.cloned.1.call-update) | async-done | bytes 589840 | tf_op jit(solution)/shard_map/psum | solution.py:88
  (193 shorter events, 27.7 us)
Async XLA Ops:
  7.2 23.2 %copy-start = (bf16[384,768]{1,0:T(8,128)(2,1)S(1)}, bf16[384,768]{1,0:T(8,128)(2,1)}, u32[]{:S(2)}) copy-start(bf16[384,768]{1,0:T(8,128)(2,1)} %param.27) | copy-start | bytes 1769476
  7.2 24.0 %copy-start.31 = (bf16[384,256]{1,0:T(8,128)(2,1)S(1)}, bf16[384,256]{1,0:T(8,128)(2,1)}, u32[]{:S(2)}) copy-start(bf16[384,256]{1,0:T(8,128)(2,1)} %param.29) | copy-start | bytes 589828
  7.2 22.9 %copy-start.32 = (bf16[384,256]{1,0:T(8,128)(2,1)S(1)}, bf16[384,256]{1,0:T(8,128)(2,1)}, u32[]{:S(2)}) copy-start(bf16[384,256]{1,0:T(8,128)(2,1)} %param.28) | copy-start | bytes 589828
  7.2 71.5 %all-reduce.17.cloned.1.call-start = ((), (), s32[]{:S(2)}) async-start(), calls=%async_computation.2 | async-start | bytes 3932160 | tf_op jit(solution)/shard_map/psum | solution.py:73
  8.1 25.0 %copy-start.24 = (pred[256]{0:T(512)(128)(4,1)}, pred[256]{0:T(512)(128)(4,1)S(1)}, u32[]{:S(2)}) copy-start(pred[256]{0:T(512)(128)(4,1)S(1)} %compare_and_fusion) | copy-start | bytes 772
  8.1 25.0 %copy-start.22 = (pred[256]{0:T(512)(128)(4,1)}, pred[256]{0:T(512)(128)(4,1)S(1)}, u32[]{:S(2)}) copy-start(pred[256]{0:T(512)(128)(4,1)S(1)} %compare_and_fusion.1) | copy-start | bytes 772
  8.2 25.0 %copy-start.26 = (pred[256]{0:T(512)(128)(4,1)}, pred[256]{0:T(512)(128)(4,1)S(1)}, u32[]{:S(2)}) copy-start(pred[256]{0:T(512)(128)(4,1)S(1)} %compare_and_fusion.2) | copy-start | bytes 772
  10.9 24.0 %copy-start.12 = (bf16[256,384]{1,0:T(8,128)(2,1)}, bf16[256,384]{1,0:T(8,128)(2,1)S(1)}, u32[]{:S(2)}) copy-start(bf16[256,384]{1,0:T(8,128)(2,1)S(1)} %gather_fusion.4) | copy-start | bytes 589828
  13.6 21.3 %copy-start.10 = (bf16[256,384]{1,0:T(8,128)(2,1)}, bf16[256,384]{1,0:T(8,128)(2,1)S(1)}, u32[]{:S(2)}) copy-start(bf16[256,384]{1,0:T(8,128)(2,1)S(1)} %gather_fusion.2) | copy-start | bytes 589828
  16.3 20.8 %copy-start.14 = (bf16[256,384]{1,0:T(8,128)(2,1)}, bf16[256,384]{1,0:T(8,128)(2,1)S(1)}, u32[]{:S(2)}) copy-start(bf16[256,384]{1,0:T(8,128)(2,1)S(1)} %gather_fusion) | copy-start | bytes 589828
  16.3 18.7 %copy-start.21 = (s32[256]{0:T(256)S(1)}, s32[256]{0:T(256)}, u32[]{:S(2)}) copy-start(s32[256]{0:T(256)} %param.21) | copy-start | bytes 3076
  34.9 281.0 %all-reduce.21.cloned.1.call-start = ((), (), s32[]{:S(2)}) async-start(), calls=%async_computation.4 | async-start | bytes 1179648 | tf_op jit(solution)/shard_map/psum | solution.py:80
  111.7 60.2 %copy-start.20 = (pred[256,256]{1,0:T(8,128)(4,1)S(1)}, pred[256,256]{1,0:T(8,128)(4,1)}, u32[]{:S(2)}) copy-start(pred[256,256]{1,0:T(8,128)(4,1)} %get-tuple-element.80) | copy-start | bytes 196612
  187.3 19.8 %copy-start.18 = (pred[256,256]{1,0:T(8,128)(4,1)S(1)}, pred[256,256]{1,0:T(8,128)(4,1)}, u32[]{:S(2)}) copy-start(pred[256,256]{1,0:T(8,128)(4,1)} %get-tuple-element.78) | copy-start | bytes 196612
  225.7 17.2 %copy-start.17 = (bf16[256,4,3,64]{0,3,2,1:T(8,128)(2,1)S(1)}, bf16[256,4,3,64]{0,3,2,1:T(8,128)(2,1)}, u32[]{:S(2)}) copy-start(bf16[256,4,3,64]{0,3,2,1:T(8,128)(2,1)} %copy.166) | copy-start | bytes 1179652
  225.7 22.5 %copy-start.19 = (pred[256,256]{1,0:T(8,128)(4,1)S(1)}, pred[256,256]{1,0:T(8,128)(4,1)}, u32[]{:S(2)}) copy-start(pred[256,256]{1,0:T(8,128)(4,1)} %get-tuple-element.98) | copy-start | bytes 196612
  274.5 15.8 %copy-start.30 = (bf16[768,384]{1,0:T(8,128)(2,1)S(1)}, bf16[768,384]{1,0:T(8,128)(2,1)}, u32[]{:S(2)}) copy-start(bf16[768,384]{1,0:T(8,128)(2,1)} %param.30) | copy-start | bytes 1769476
  274.5 17.0 %copy-start.28 = (bf16[384]{0:T(512)(128)(2,1)S(1)}, bf16[384]{0:T(512)(128)(2,1)}, u32[]{:S(2)}) copy-start(bf16[384]{0:T(512)(128)(2,1)} %param.31) | copy-start | bytes 2308
  274.5 41.5 %copy-start.13 = (bf16[256,384]{1,0:T(8,128)(2,1)S(1)}, bf16[256,384]{1,0:T(8,128)(2,1)}, u32[]{:S(2)}) copy-start(bf16[256,384]{1,0:T(8,128)(2,1)} %copy-done.12) | copy-start | bytes 589828
  274.5 41.5 %copy-start.25 = (pred[256]{0:T(512)(128)(4,1)S(1)}, pred[256]{0:T(512)(128)(4,1)}, u32[]{:S(2)}) copy-start(pred[256]{0:T(512)(128)(4,1)} %copy-done.24) | copy-start | bytes 772
  274.5 42.6 %copy-start.15 = (bf16[256,384]{1,0:T(8,128)(2,1)S(1)}, bf16[256,384]{1,0:T(8,128)(2,1)}, u32[]{:S(2)}) copy-start(bf16[256,384]{1,0:T(8,128)(2,1)} %copy-done.14) | copy-start | bytes 589828
  274.5 42.6 %copy-start.27 = (pred[256]{0:T(512)(128)(4,1)S(1)}, pred[256]{0:T(512)(128)(4,1)}, u32[]{:S(2)}) copy-start(pred[256]{0:T(512)(128)(4,1)} %copy-done.26) | copy-start | bytes 772
  274.5 43.9 %copy-start.11 = (bf16[256,384]{1,0:T(8,128)(2,1)S(1)}, bf16[256,384]{1,0:T(8,128)(2,1)}, u32[]{:S(2)}) copy-start(bf16[256,384]{1,0:T(8,128)(2,1)} %copy-done.10) | copy-start | bytes 589828
  274.6 43.9 %copy-start.23 = (pred[256]{0:T(512)(128)(4,1)S(1)}, pred[256]{0:T(512)(128)(4,1)}, u32[]{:S(2)}) copy-start(pred[256]{0:T(512)(128)(4,1)} %copy-done.22) | copy-start | bytes 772
  291.4 116.5 %all-reduce.13.cloned.1.call-start = ((), (), s32[]{:S(2)}) async-start(), calls=%async_computation | async-start | bytes 245760 | tf_op jit(solution)/shard_map/psum | solution.py:83
  317.1 45.1 %copy-start.6 = (bf16[256,384]{1,0:T(8,128)(2,1)}, bf16[256,384]{1,0:T(8,128)(2,1)S(1)}, u32[]{:S(2)}) copy-start(bf16[256,384]{1,0:T(8,128)(2,1)S(1)} %get-tuple-element.37) | copy-start | bytes 589828
  318.4 43.0 %copy-start.4 = (bf16[256,384]{1,0:T(8,128)(2,1)}, bf16[256,384]{1,0:T(8,128)(2,1)S(1)}, u32[]{:S(2)}) copy-start(bf16[256,384]{1,0:T(8,128)(2,1)S(1)} %get-tuple-element.35) | copy-start | bytes 589828
  319.7 43.5 %copy-start.8 = (bf16[256,384]{1,0:T(8,128)(2,1)}, bf16[256,384]{1,0:T(8,128)(2,1)S(1)}, u32[]{:S(2)}) copy-start(bf16[256,384]{1,0:T(8,128)(2,1)S(1)} %get-tuple-element.33) | copy-start | bytes 589828
  326.0 16.3 %slice-start = ((s8[7864320]{0:T(1024)(128)(4,1)}), s8[4194304]{0:T(1024)(128)(4,1)S(1)}, s32[]{:S(2)}) async-start(s8[7864320]{0:T(1024)(128)(4,1)} %bitcast.233), calls=%async_computation.5 | async-start | bytes 8388608
  334.1 8.2 slice-start.1
  334.1 13.0 %slice-start.2 = ((s8[7864320]{0:T(1024)(128)(4,1)}), s8[4194304]{0:T(1024)(128)(4,1)S(1)}, s32[]{:S(2)}) async-start(s8[7864320]{0:T(1024)(128)(4,1)} %bitcast.235), calls=%async_computation.7 | async-start | bytes 8388608
  342.3 4.8 slice-start.3
  356.7 4.7 copy-start.33
  381.9 547.2 %all-reduce.15.cloned.1.call-start = ((), (), s32[]{:S(2)}) async-start(), calls=%async_computation.1 | async-start | bytes 62914560 | tf_op jit(solution)/shard_map/psum | solution.py:86
  390.9 0.7 copy-start.16
  390.9 589.1 %all-reduce.19.cloned.1.call-start = ((), (), s32[]{:S(2)}) async-start(), calls=%async_computation.3 | async-start | bytes 1179648 | tf_op jit(solution)/shard_map/psum | solution.py:88
  423.2 0.8 copy-start.3
  440.7 0.8 copy-start.2
  929.1 10.2 %copy-start.29 = (bf16[2,40,256,256]{3,2,1,0:T(8,128)(2,1)S(1)}, bf16[2,40,256,256]{3,2,1,0:T(8,128)(2,1)}, u32[]{:S(2)}) copy-start(bf16[2,40,256,256]{3,2,1,0:T(8,128)(2,1)} %get-tuple-element.21) | copy-start | bytes 31457284
  929.1 21.2 %slice-start.4 = ((s8[10485760]{0:T(1024)(128)(4,1)}), s8[4194304]{0:T(1024)(128)(4,1)S(1)}, s32[]{:S(2)}) async-start(s8[10485760]{0:T(1024)(128)(4,1)} %bitcast.282), calls=%async_computation.9 | async-start | bytes 8388608
  929.1 21.2 %slice-start.5 = ((s8[10485760]{0:T(1024)(128)(4,1)}), s8[4194304]{0:T(1024)(128)(4,1)S(1)}, s32[]{:S(2)}) async-start(s8[10485760]{0:T(1024)(128)(4,1)} %bitcast.282), calls=%async_computation.10 | async-start | bytes 8388608
  929.1 21.2 %slice-start.7 = ((s8[7864320]{0:T(1024)(128)(4,1)}), s8[4194304]{0:T(1024)(128)(4,1)S(1)}, s32[]{:S(2)}) async-start(s8[7864320]{0:T(1024)(128)(4,1)} %bitcast.284), calls=%async_computation.12 | async-start | bytes 8388608
  939.3 11.0 %slice-start.6 = ((s8[10485760]{0:T(1024)(128)(4,1)}), s8[2097152]{0:T(1024)(128)(4,1)S(1)}, s32[]{:S(2)}) async-start(s8[10485760]{0:T(1024)(128)(4,1)} %bitcast.282), calls=%async_computation.11 | async-start | bytes 4194304
  939.3 11.0 %slice-start.8 = ((s8[7864320]{0:T(1024)(128)(4,1)}), s8[3670016]{0:T(1024)(128)(4,1)S(1)}, s32[]{:S(2)}) async-start(s8[7864320]{0:T(1024)(128)(4,1)} %bitcast.284), calls=%async_computation.13 | async-start | bytes 7340032
  950.4 29.6 %copy-start.7 = (bf16[256,384]{1,0:T(8,128)(2,1)S(1)}, bf16[256,384]{1,0:T(8,128)(2,1)}, u32[]{:S(2)}) copy-start(bf16[256,384]{1,0:T(8,128)(2,1)} %copy-done.6) | copy-start | bytes 589828
  950.4 30.6 %copy-start.9 = (bf16[256,384]{1,0:T(8,128)(2,1)S(1)}, bf16[256,384]{1,0:T(8,128)(2,1)}, u32[]{:S(2)}) copy-start(bf16[256,384]{1,0:T(8,128)(2,1)} %copy-done.8) | copy-start | bytes 589828
  950.4 31.6 %copy-start.5 = (bf16[256,384]{1,0:T(8,128)(2,1)S(1)}, bf16[256,384]{1,0:T(8,128)(2,1)}, u32[]{:S(2)}) copy-start(bf16[256,384]{1,0:T(8,128)(2,1)} %copy-done.4) | copy-start | bytes 589828
  950.4 33.5 %copy-start.1 = (bf16[384,768]{1,0:T(8,128)(2,1)S(1)}, bf16[384,768]{1,0:T(8,128)(2,1)}, u32[]{:S(2)}) copy-start(bf16[384,768]{1,0:T(8,128)(2,1)} %param.27) | copy-start | bytes 1769476
Sparse Core Ops, SparseCore 0:
  35.0 43.6 all-reduce.16
  291.5 24.3 all-reduce.20
  382.0 25.8 all-reduce.12
  410.5 518.5 all-reduce.14
  955.4 24.5 all-reduce.18
where the time goes:
time: 999 us; the launch traced here: 991 us
  waiting for transfers between devices  577 us (58%)
  matrix products  182 us (18%)
  other arithmetic  124 us (12%)
  local copies, waits for them, and re-layouts  77 us (8%)
  blocking collectives  15.1 us (2%)
  between operations  14.9 us (1%)
    psum x1, waiting for transfers between devices, per_device(): hidden_sum = lax.psum(hidden_part, 'x')  470 us
    sub x3, matrix products, attention(): weight = jnp.where(valid_mask, jnp.exp(scores - peak_val), 0.0)  60.3 us
    select_n x1, other arithmetic, write_slot(): return jnp.where(hit_mask, new_rows[:, None], cache_arr)  60.2 us
    gather x15, local copies, waits for them, and re-layouts, mixing(): jnp.take_along_axis(logits, choice_row, axis=1)  50 us
    dot_general x3, matrix products, attention(): jnp.einsum('bkgs,bskh->bkgh', weight.astype(jnp.bfloat16), val_cache, pre...  47 us
    psum x1, waiting for transfers between devices, per_device(): proj_sum = lax.psum(proj_part, 'x')  41.6 us
    another operation x3, other arithmetic, per_device(): jnp.stack([jnp.einsum('bd,edf->ebf', normed2, w_act, preferred_element_ty...  26.8 us
    dot_general x3, matrix products, per_device(): jnp.einsum('ebf,efd->bd', unit_bf16, w_down, preferred_element_type=jnp.f...  26 us
  transfers between devices with their start and end apart: 5, of which 5 were waited for; matrix products, arithmetic and copies ran while one was open for 6% of the time, Pallas kernels for 0%

commit v1 on v0

v1 whole, which is shorter than its diff:
```python
import functools

import jax
import jax.numpy as jnp
from jax import lax
from jax.experimental import pallas as pl
from jax.experimental.pallas import tpu as pltpu
from jax.sharding import PartitionSpec as P

EPS = 1e-5
ROPE_BASE = 1.0e6
F32 = jnp.float32
BF16 = jnp.bfloat16
VMEM_LIMIT = 60 * 1024 * 1024
NCHUNK = 1
NB = 8


def vspec():
    return pl.BlockSpec(memory_space=pltpu.VMEM)


def qkv_kernel(me_ref, x0, x1, x2, x3, gain_ref, w0, w1, w2, w3, cos_ref, sin_ref, out_ref, hs, ws):
    tile = pl.program_id(0)
    me = me_ref[0]
    place = [me, me + 1 - 2 * (me % 2), (me + 2) % 4]
    place.append((place[1] + 2) % 4)

    @pl.when(tile == 0)
    def _():
        xs = [r[...].astype(F32) for r in (x0, x1, x2, x3)]
        sq = [jnp.sum(v * v, axis=-1, keepdims=True) for v in xs]
        total = (sq[0] + sq[1]) + (sq[2] + sq[3])
        scale = lax.rsqrt(total / (4.0 * x0.shape[1]) + EPS)
        for i, ref in enumerate((x0, x1, x2, x3)):
            hs[place[i]] = (ref[...].astype(F32) * scale * gain_ref[i : i + 1, :]).astype(BF16)

    for i, ref in enumerate((w0, w1, w2, w3)):
        ws[place[i]] = ref[0]
    acc = jnp.dot(hs[0], ws[0], preferred_element_type=F32)
    for i in range(1, 4):
        acc += jnp.dot(hs[i], ws[i], preferred_element_type=F32)
    vals = acc.astype(BF16)

    @pl.when(tile < 4)
    def _():
        v = vals.astype(F32)
        lane = lax.broadcasted_iota(jnp.int32, (1, 256), 1) % 64
        low = lane < 32
        ahead = jnp.concatenate([v[:, 32:], v[:, :32]], axis=1)
        behind = jnp.concatenate([v[:, 224:], v[:, :224]], axis=1)
        other = jnp.where(low, ahead, behind)
        cos = jnp.concatenate([cos_ref[...], cos_ref[...]], axis=1)
        sin = jnp.concatenate([sin_ref[...], sin_ref[...]], axis=1)
        out_ref[0] = (v * cos + other * sin).astype(BF16)

    @pl.when(tile == 4)
    def _():
        out_ref[0] = vals


def qkv_call(me, xs, gains, ws, cos, sin):
    tokens, width = xs[0].shape
    grid_spec = pltpu.PrefetchScalarGridSpec(
        num_scalar_prefetch=1,
        grid=(5,),
        in_specs=[pl.BlockSpec((tokens, width), lambda i, m: (0, 0))] * 4
        + [pl.BlockSpec((4, width), lambda i, m: (0, 0))]
        + [pl.BlockSpec((1, width, 256), lambda i, m: (i, 0, 0))] * 4
        + [pl.BlockSpec((tokens, 128), lambda i, m: (0, 0))] * 2,
        out_specs=pl.BlockSpec((1, tokens, 256), lambda i, m: (i, 0, 0)),
        scratch_shapes=[pltpu.VMEM((4, tokens, width), BF16), pltpu.VMEM((4, width, 256), BF16)],
    )
    return pl.pallas_call(
        qkv_kernel,
        grid_spec=grid_spec,
        out_shape=jax.ShapeDtypeStruct((5, tokens, 256), BF16),
        compiler_params=pltpu.CompilerParams(vmem_limit_bytes=VMEM_LIMIT, dimension_semantics=("arbitrary",)),
        cost_estimate=pl.CostEstimate(flops=2 * tokens * width * 4 * 1280, bytes_accessed=9_000_000, transcendentals=0),
        name="qkv",
    )(me, *xs, gains, *ws, cos, sin)


def attn_kernel(len_ref, a_ref, k_ref, v_ref, o_ref, ko_ref, vo_ref):
    step = pl.program_id(0)
    nb = a_ref.shape[0]
    cols = jnp.transpose(a_ref[...].reshape(nb * 16, 256).astype(F32))
    slot = lax.broadcasted_iota(jnp.int32, (1, 256), 1)
    block = lax.broadcasted_iota(jnp.int32, (1, 256), 1) // 64
    row_t = lax.broadcasted_iota(jnp.int32, (64, 1), 0) % 16 % 3
    for i in range(nb):
        pos = len_ref[step * nb + i]
        kt = k_ref[i * 256 : (i + 1) * 256, :]
        vt = v_ref[i * 256 : (i + 1) * 256, :]
        for t in range(3):
            hit = slot == pos + t
            c0 = i * 16 + 9 + t
            kt = jnp.where(hit, cols[:, c0 : c0 + 1].astype(BF16), kt)
            vt = jnp.where(hit, cols[:, c0 + 3 : c0 + 4].astype(BF16), vt)
        ko_ref[i * 256 : (i + 1) * 256, :] = kt
        vo_ref[i * 256 : (i + 1) * 256, :] = vt
        q = a_ref[i]
        zero = jnp.zeros_like(q)
        lhs = jnp.concatenate([jnp.where(block == k, q, zero) for k in range(4)], axis=0)
        s = jnp.dot(lhs, kt, preferred_element_type=F32) * 0.125
        valid = slot <= row_t + pos
        s = jnp.where(valid, s, -1.0e30)
        peak = jnp.max(s, axis=-1, keepdims=True)
        e = jnp.where(valid, jnp.exp(s - peak), 0.0)
        total = jnp.sum(e, axis=-1, keepdims=True)
        mixed = lax.dot_general(e.astype(BF16), vt, (((1,), (1,)), ((), ())), preferred_element_type=F32)
        mixed = mixed / total
        res = mixed[0:16]
        for k in range(1, 4):
            res = jnp.where(block == k, mixed[16 * k : 16 * k + 16], res)
        o_ref[i] = res.astype(BF16)


def attn_call(lengths, acts, k_rows, v_rows):
    batch = acts.shape[0]
    grid_spec = pltpu.PrefetchScalarGridSpec(
        num_scalar_prefetch=1,
        grid=(batch // NB,),
        in_specs=[pl.BlockSpec((NB, 16, 256), lambda i, m: (i, 0, 0))] + [pl.BlockSpec((NB * 256, 256), lambda i, m: (i, 0))] * 2,
        out_specs=[pl.BlockSpec((NB, 16, 256), lambda i, m: (i, 0, 0))] + [pl.BlockSpec((NB * 256, 256), lambda i, m: (i, 0))] * 2,
    )
    return pl.pallas_call(
        attn_kernel,
        grid_spec=grid_spec,
        out_shape=[
            jax.ShapeDtypeStruct((batch, 16, 256), BF16),
            jax.ShapeDtypeStruct(k_rows.shape, BF16),
            jax.ShapeDtypeStruct(v_rows.shape, BF16),
        ],
        compiler_params=pltpu.CompilerParams(vmem_limit_bytes=VMEM_LIMIT, dimension_semantics=("arbitrary",)),
        cost_estimate=pl.CostEstimate(flops=40_000_000_000, bytes_accessed=134_000_000, transcendentals=0),
        name="attn",
    )(lengths, acts, k_rows, v_rows)


E1 = 4


def moe1_kernel(cx_ref, h_ref, ch_ref, a0, l0, a1, l1, keep_ref, send_ref, dense):
    step = pl.program_id(0)
    half = keep_ref.shape[1]
    for k in range(E1):
        top = jnp.concatenate([a0[k], l0[k]], axis=1)
        low = jnp.concatenate([a1[k], l1[k]], axis=1)
        w = jnp.concatenate([top, low], axis=0)
        dense[k] = jnp.dot(h_ref[...], w, preferred_element_type=F32).astype(BF16)
    cx = cx_ref[0]
    rt = 32

    def run(first):
        for part, ref in ((0, keep_ref), (1, send_ref)):
            row0 = ((cx + part) % 2) * half

            def body(i, carry):
                src = pl.ds(pl.multiple_of(row0 + i * rt, rt), rt)
                dst = pl.ds(pl.multiple_of(i * rt, rt), rt)
                d = [dense[k, src, :] for k in range(E1)]
                for j in range(8):
                    chj = ch_ref[j, src, :]
                    hits = [chj == (step * E1 + k).astype(F32).astype(BF16) for k in range(E1)]
                    for side in range(2):
                        lanes = slice(side * 128, side * 128 + 128)
                        acc = jnp.zeros((rt, 128), BF16) if first else ref[j, dst, lanes]
                        for k in range(E1):
                            acc = jnp.where(hits[k], d[k][:, lanes], acc)
                        ref[j, dst, lanes] = acc
                return carry

            lax.fori_loop(0, half // rt, body, 0)

    @pl.when(step == 0)
    def _():
        run(True)

    @pl.when(step > 0)
    def _():
        run(False)


def moe1_call(cx, h2, ch, a0, l0, a1, l1):
    tokens = h2.shape[0]
    experts, rows, _ = a0.shape
    out = jax.ShapeDtypeStruct((8, tokens // 2, 256), BF16)
    grid_spec = pltpu.PrefetchScalarGridSpec(
        num_scalar_prefetch=1,
        grid=(experts // E1,),
        in_specs=[pl.BlockSpec((tokens, 2 * rows), lambda i, m: (0, 0)), pl.BlockSpec((8, tokens, 128), lambda i, m: (0, 0, 0))]
        + [pl.BlockSpec((E1, rows, 128), lambda i, m: (i, 0, 0))] * 4,
        out_specs=[pl.BlockSpec((8, tokens // 2, 256), lambda i, m: (0, 0, 0))] * 2,
        scratch_shapes=[pltpu.VMEM((E1, tokens, 256), BF16)],
    )
    return pl.pallas_call(
        moe1_kernel,
        grid_spec=grid_spec,
        out_shape=[out, out],
        compiler_params=pltpu.CompilerParams(vmem_limit_bytes=VMEM_LIMIT, dimension_semantics=("arbitrary",)),
        cost_estimate=pl.CostEstimate(flops=2 * tokens * 2 * rows * 256 * experts, bytes_accessed=20_000_000, transcendentals=0),
        name="moe1",
    )(cx, h2, ch, a0, l0, a1, l1)


E2 = 4


def moe2_kernel(cx_ref, um_ref, uo_ref, ch_ref, wa, wb, own_ref, send_ref, spread, acc_ref):
    step = pl.program_id(0)
    half = um_ref.shape[1]
    width = wa.shape[2]
    cx = cx_ref[0]
    rt = 32
    for part, ref in ((0, um_ref), (1, uo_ref)):
        row0 = ((cx + part) % 2) * half

        def body(i, carry):
            dst = pl.ds(pl.multiple_of(row0 + i * rt, rt), rt)
            src = pl.ds(pl.multiple_of(i * rt, rt), rt)
            out = [jnp.zeros((rt, 128), BF16) for _ in range(E2)]
            for j in range(8):
                chj = ch_ref[j, dst, :]
                uj = ref[j, src, :]
                for k in range(E2):
                    out[k] = jnp.where(chj == (step * E2 + k).astype(F32).astype(BF16), uj, out[k])
            for k in range(E2):
                spread[dst, k * 128 : (k + 1) * 128] = out[k]
            return carry

        lax.fori_loop(0, half // rt, body, 0)
    w = jnp.concatenate([wa[...].reshape(E2 * 128, width), wb[...].reshape(E2 * 128, width)], axis=1)
    prod = jnp.dot(spread[...], w, preferred_element_type=F32)

    @pl.when(step == 0)
    def _():
        acc_ref[...] = prod

    @pl.when(step > 0)
    def _():
        acc_ref[...] += prod

    @pl.when(step == pl.num_programs(0) - 1)
    def _():
        own_ref[...] = acc_ref[:, :width]
        send_ref[...] = acc_ref[:, width:].astype(BF16)


def moe2_call(cx, um, uo, ch, wa, wb):
    tokens = ch.shape[1]
    experts, rows, width = wa.shape
    grid_spec = pltpu.PrefetchScalarGridSpec(
        num_scalar_prefetch=1,
        grid=(experts // E2,),
        in_specs=[pl.BlockSpec((8, tokens // 2, 128), lambda i, m: (0, 0, 0))] * 2
        + [pl.BlockSpec((8, tokens, 128), lambda i, m: (0, 0, 0))]
        + [pl.BlockSpec((E2, rows, width), lambda i, m: (i, 0, 0))] * 2,
        out_specs=[pl.BlockSpec((tokens, width), lambda i, m: (0, 0))] * 2,
        scratch_shapes=[pltpu.VMEM((tokens, E2 * 128), BF16), pltpu.VMEM((tokens, 2 * width), F32)],
    )
    return pl.pallas_call(
        moe2_kernel,
        grid_spec=grid_spec,
        out_shape=[jax.ShapeDtypeStruct((tokens, width), F32), jax.ShapeDtypeStruct((tokens, width), BF16)],
        compiler_params=pltpu.CompilerParams(vmem_limit_bytes=VMEM_LIMIT, dimension_semantics=("arbitrary",)),
        cost_estimate=pl.CostEstimate(flops=2 * tokens * rows * 2 * width * experts, bytes_accessed=10_000_000, transcendentals=0),
        name="moe2",
    )(cx, um, uo, ch, wa, wb)


def solution(mesh):
    cache_spec = P('dp', None, 'y', None)
    in_specs = (P(None, 'dp'), P('dp'), P(None, 'dp', None), P(None, 'x'), cache_spec, cache_spec, P('x'), P('x', 'y'), P('x', 'y'), P('x', 'y'), P('y', 'x'), P('x'), P('x', None), P(None, 'x', 'y'), P(None, 'x', 'y'), P(None, 'y', 'x'))
    out_specs = (P(None, 'dp', 'x'), cache_spec, cache_spec)

    def core_swap(v):
        return lax.ppermute(v, 'x', [(0, 1), (1, 0), (2, 3), (3, 2)])

    def chip_swap(v):
        return lax.ppermute(v, 'x', [(0, 2), (2, 0), (1, 3), (3, 1)])

    def y_swap(v):
        return lax.ppermute(v, 'y', [(0, 1), (1, 0)])

    def per_device(tokens, lengths, choices, emb_table, k_cache, v_cache, g_attn, w_q, w_k, w_v, w_o, g_ffn, w_router, w_act, w_lin, w_down):
        steps, batch = tokens.shape
        width = emb_table.shape[1]
        kv, hd = k_cache.shape[2], k_cache.shape[3]
        slots = k_cache.shape[1]
        group = w_q.shape[1] // (kv * hd)
        experts = w_act.shape[0]
        width_full = width * 4
        me = lax.axis_index('x').astype(jnp.int32)
        my = lax.axis_index('y').astype(jnp.int32)
        core = me % 2
        cx = me // 2
        n_tok = steps * batch

        wq = w_q.reshape(width, kv, group, hd).transpose(2, 0, 1, 3).reshape(group, width, kv * hd)
        w0 = jnp.concatenate([wq, w_k[None], w_v[None]], axis=0)
        w2 = chip_swap(w0)
        w1 = core_swap(w0)
        w3 = core_swap(w2)
        gains = jnp.stack([g_attn, g_ffn]).astype(F32)
        gains_c = core_swap(gains)
        gains_x = chip_swap(jnp.concatenate([gains, gains_c], axis=0))
        gain4 = jnp.stack([gains[0], gains_c[0], gains_x[0], gains_x[2]])

        x_in = jnp.take(emb_table, tokens.reshape(n_tok), axis=0, mode='clip')
        x_mate = core_swap(x_in)
        half_tok = n_tok // 2
        part = chip_swap(lax.dynamic_slice_in_dim(x_in, my * half_tok, half_tok, 0))
        part_o = y_swap(part)
        x_far = jnp.where(my == 0, jnp.concatenate([part, part_o], 0), jnp.concatenate([part_o, part], 0))
        x_far_mate = core_swap(x_far)

        def blocks(w, axis):
            mine = lax.dynamic_slice_in_dim(w, core * 128, 128, axis)
            theirs = lax.dynamic_slice_in_dim(w, (1 - core) * 128, 128, axis)
            return mine, core_swap(theirs)

        act0, act1 = blocks(w_act, 2)
        lin0, lin1 = blocks(w_lin, 2)
        down0, down1 = blocks(w_down, 1)
        router_mate = core_swap(w_router)

        positions = lengths[None, :] + jnp.arange(steps, dtype=jnp.int32)[:, None]
        inv_freq = ROPE_BASE ** (-(jnp.arange(hd // 2, dtype=F32) * 2.0 / hd))
        angles = positions.reshape(n_tok).astype(F32)[:, None] * inv_freq[None, :]
        cos, sin = jnp.cos(angles), jnp.sin(angles)
        cos2 = jnp.concatenate([cos, cos, cos, cos], axis=1)
        sin2 = jnp.concatenate([-sin, sin, -sin, sin], axis=1)

        qkv = qkv_call(me[None], (x_in, x_mate, x_far, x_far_mate), gain4, (w0, w1, w2, w3), cos2, sin2)
        acts = qkv.reshape(5, steps, batch, 256).transpose(2, 0, 1, 3).reshape(batch, 15, 256)
        acts = jnp.pad(acts, ((0, 0), (0, 1), (0, 0)))
        k_rows = k_cache.transpose(0, 2, 3, 1).reshape(batch * kv * hd, slots)
        v_rows = v_cache.transpose(0, 2, 3, 1).reshape(batch * kv * hd, slots)
        o, k_new, v_new = attn_call(lengths, acts, k_rows, v_rows)

        def back(rows):
            return rows.reshape(batch, kv, hd, slots).transpose(0, 3, 1, 2)

        wo = w_o.reshape(kv, group, hd, width).transpose(1, 0, 2, 3).reshape(group * kv * hd, width)
        x3 = x_in.reshape(steps, batch, width)
        o4 = o[:, : steps * group].reshape(batch, group, steps, 256)

        nbc = batch // NCHUNK
        outs = []
        for ci in range(NCHUNK):
            bs = slice(ci * nbc, (ci + 1) * nbc)
            nt = steps * nbc
            x_res = x3[:, bs].reshape(nt, width)
            oc = o4[bs].transpose(2, 0, 1, 3).reshape(nt, group * 256)
            proj = jnp.dot(oc, wo, preferred_element_type=F32).astype(BF16)
            proj_y = y_swap(proj)
            x1 = (x_res.astype(F32) + (proj.astype(F32) + proj_y.astype(F32))).astype(BF16)
            x1_mate = core_swap(x1)
            x1f, x1mf = x1.astype(F32), x1_mate.astype(F32)
            sq = jnp.sum(x1f * x1f, axis=-1) + jnp.sum(x1mf * x1mf, axis=-1)
            sq = sq + chip_swap(sq)
            scale = lax.rsqrt(sq / width_full + EPS)[:, None]
            h2 = jnp.concatenate([x1f * scale * gains[1], x1mf * scale * gains_c[1]], axis=1).astype(BF16)
            router = jnp.concatenate([w_router, router_mate], axis=0)
            logits = jnp.dot(h2, router, preferred_element_type=F32)
            chc = choices[:, bs].reshape(nt, 8)
            ch_rows = jnp.broadcast_to(chc.T.astype(BF16)[:, :, None], (8, nt, 128))
            keep, send = moe1_call(cx[None], h2, ch_rows, act0, lin0, act1, lin1)
            got = chip_swap(send)
            logits = logits + chip_swap(logits)
            picked = jnp.sum(jnp.where(chc[:, :, None] == jnp.arange(experts)[None, None, :], logits[:, None, :], 0.0), axis=-1)
            gate = jax.nn.softmax(picked, axis=-1)
            gate_mine = lax.dynamic_slice_in_dim(gate, cx * (nt // 2), nt // 2, 0).T
            hid = keep.astype(F32) + got.astype(F32)
            u = (gate_mine[:, :, None] * jax.nn.silu(hid[..., :128]) * hid[..., 128:]).astype(BF16)
            u_far = chip_swap(u)
            own, snd = moe2_call(cx[None], u, u_far, ch_rows, down0, down1)
            chip_sum = (own + core_swap(snd).astype(F32)).astype(BF16)
            moe = chip_sum.astype(F32) + y_swap(chip_sum).astype(F32)
            outs.append((x1.astype(F32) + moe).astype(BF16).reshape(steps, nbc, width))
        hidden = outs[0] if NCHUNK == 1 else jnp.concatenate(outs, axis=1)
        return hidden, back(k_new), back(v_new)

    return jax.shard_map(per_device, mesh=mesh, in_specs=in_specs, out_specs=out_specs, check_vma=False)
```

time: 999 us -> 335 us (0.34)
  waiting for transfers between devices: 577 us -> 98.7 us
  matrix products: 182 us -> 1.23 us
  Pallas kernels: 0 us -> 167 us
  other arithmetic: 124 us -> 11.5 us
  local copies, waits for them, and re-layouts: 77 us -> 38.3 us
  starting transfers between devices: 0.21 us -> 16.4 us
  blocking collectives: 15.1 us -> 0 us
  between operations: 14.9 us -> 1.06 us
    psum x5 -> x0, waiting for transfers between devices: 577 us -> none  [the longest x1 470 us: per_device(): hidden_sum = lax.psum(hidden_part, 'x')]
    pallas_call x0 -> x4, Pallas kernels: none -> 167 us  [the longest x1 97.9 us: attn_call(): pl.pallas_call(attn_kernel, grid_spec=grid_spec, out_shape=[jax.ShapeDtyp...]
    dot_general x27 -> x2, matrix products: 122 us -> 1.23 us  [the longest x1 0.78 us: per_device(): proj = jnp.dot(oc, wo, preferred_element_type=F32).astype(BF16)]
    ppermute x0 -> x21, waiting for transfers between devices: none -> 98.7 us  [the longest x7 63 us: chip_swap(): return lax.ppermute(v, 'x', [(0, 2), (2, 0), (1, 3), (3, 1)])]
    sub x3 -> x0, matrix products: 60.3 us -> none  [attention(): weight = jnp.where(valid_mask, jnp.exp(scores - peak_val), 0.0)]
    select_n x4 -> x1, other arithmetic: 60.2 us -> 0.2 us  [per_device(): jnp.where(my == 0, jnp.concatenate([part, part_o], 0), jnp.concatenate([p...]
    gather x18 -> x1, local copies, waits for them, and re-layouts: 58 us -> 5.01 us  [per_device(): x_in = jnp.take(emb_table, tokens.reshape(n_tok), axis=0, mode='clip')]
    another operation x11 -> x2, other arithmetic: 31.2 us -> 0.96 us  [the longest x1 0.6 us: per_device(): gain4 = jnp.stack([gains[0], gains_c[0], gains_x[0], gains_x[2]])]
  transfers between devices with their start and end apart: 5 -> 21, of which waited for: 5 -> 10; matrix products, arithmetic and copies ran while one was open for 6% -> 13% of each run, Pallas kernels for 0% -> 43%
where the time goes in v1:
time: 335 us; the launch traced here: 334 us
  Pallas kernels  167 us (50%)
  waiting for transfers between devices  98.7 us (29%)
  local copies, waits for them, and re-layouts  38.3 us (11%)
  starting transfers between devices  16.4 us (5%)
  other arithmetic  11.5 us (3%)
    pallas_call x1, Pallas kernels, attn_call(): pl.pallas_call(attn_kernel, grid_spec=grid_spec, out_shape=[jax.ShapeDtyp...  97.9 us
    ppermute x7, waiting for transfers between devices, chip_swap(): return lax.ppermute(v, 'x', [(0, 2), (2, 0), (1, 3), (3, 1)])  63 us
    pallas_call x1, Pallas kernels, moe1_call(): pl.pallas_call(moe1_kernel, grid_spec=grid_spec, out_shape=[out, out], co...  33.3 us
    ppermute x3, waiting for transfers between devices, y_swap(): return lax.ppermute(v, 'y', [(0, 1), (1, 0)])  32.4 us
    pallas_call x1, Pallas kernels, moe2_call(): pl.pallas_call(moe2_kernel, grid_spec=grid_spec, out_shape=[jax.ShapeDtyp...  24.8 us
    dynamic_slice x3, local copies, waits for them, and re-layouts, blocks(): theirs = lax.dynamic_slice_in_dim(w, (1 - core) * 128, 128, axis)  20 us
    pallas_call x1, Pallas kernels, qkv_call(): pl.pallas_call(qkv_kernel, grid_spec=grid_spec, out_shape=jax.ShapeDtypeS...  11.3 us
    ppermute x7, starting transfers between devices, chip_swap(): return lax.ppermute(v, 'x', [(0, 2), (2, 0), (1, 3), (3, 1)])  9.96 us
  transfers between devices with their start and end apart: 21, of which 10 were waited for; matrix products, arithmetic and copies ran while one was open for 13% of the time, Pallas kernels for 43%

profile of v1, /device:TPU:0, one launch (start us, length us, event | category | flops | bytes accessed | tf_op | source)
XLA Modules:
  0.0 334.4 jit_solution(15974387922383800039)
XLA Ops:
  0.7 1.4 copy.47
  2.6 3.4 %collective-permute-start.7 = (bf16[5,384,256]{2,1,0:T(8,128)(2,1)S(1)}, bf16[5,384,256]{2,1,0:T(8,128)(2,1)}, u32[]{:S(2)}, u32[]{:S(2)}) collective-permute-start(bf16[5,384,256]{2,1,0:T(8,128)(2,1)S(1)} %pad_maximum_fusion.1.w0), channel_id=1, source_target_pairs={{0,2},{2,0},{1,3},{3,1},{4,6},{6,4},{5,7},{7,5}} | collective-permute-start | bytes 2949128 | tf_op jit(solution)/shard_map/ppermute | solution.py:281
  6.0 5.0 %gather_fusion = bf16[768,384]{1,0:T(8,128)(2,1)S(1)} fusion(bf16[49155,384]{1,0:T(8,128)(2,1)} %param.19, s32[1024]{0:T(1024)S(1)} %pad_clamp_fusion), kind=kCustom, calls=%fused_computation | custom fusion | bytes 1182720 | tf_op jit(solution)/shard_map/jit(_take)/gather | solution.py:310
  11.0 0.5 collective-permute-start
  11.9 1.4 fusion.8
  13.4 7.5 %constant_dynamic-slice_fusion.3 = (bf16[40,384,128]{2,1,0:T(8,128)(2,1)}, bf16[40,384,128]{2,1,0:T(8,128)(2,1)}) fusion(bf16[40,384,256]{2,1,0:T(8,128)(2,1)} %param.29, s32[]{:T(128)S(6)} %select_n.47, s32[]{:T(128)S(6)} %select_n.46), kind=kLoop, calls=%fused_computation.45 | loop fusion | bytes 15728648 | tf_op jit(solution)/shard_map/dynamic_slice | solution.py:320
  20.9 4.5 %constant_dynamic-slice_fusion.2 = (bf16[40,384,128]{2,1,0:T(8,128)(2,1)}, bf16[40,384,128]{2,1,0:T(8,128)(2,1)}) fusion(bf16[40,384,256]{2,1,0:T(8,128)(2,1)S(1)} %bitcast.45, s32[]{:T(128)S(6)} %select_n.47, s32[]{:T(128)S(6)} %select_n.46), kind=kLoop, calls=%fused_computation.44 | loop fusion | bytes 15728648 | tf_op jit(solution)/shard_map/dynamic_slice | solution.py:320
  25.4 8.6 %collective-permute-done.1 = bf16[384,384]{1,0:T(8,128)(2,1)S(1)} collective-permute-done((bf16[384,384]{1,0:T(8,128)(2,1)S(1)}, bf16[384,384]{1,0:T(8,128)(2,1)S(1)}, u32[]{:S(2)}, u32[]{:S(2)}) %collective-permute-start.1) | collective-permute-done | bytes 294944 | tf_op jit(solution)/shard_map/ppermute | solution.py:281
  34.0 1.8 collective-permute-start.2
  35.8 1.6 pad_maximum_fusion.2
  37.4 4.8 %collective-permute-done.2 = bf16[384,384]{1,0:T(8,128)(2,1)S(1)} collective-permute-done((bf16[384,384]{1,0:T(8,128)(2,1)S(1)}, bf16[384,384]{1,0:T(8,128)(2,1)S(1)}, u32[]{:S(2)}, u32[]{:S(2)}) %collective-permute-start.2) | collective-permute-done | bytes 294944 | tf_op jit(solution)/shard_map/ppermute | solution.py:284
  42.5 1.5 collective-permute-start.5
  44.0 2.1 collective-permute-done.5
  46.1 0.6 pad_maximum_fusion.5.gain_ref
  46.7 0.5 collective-permute-start.15
  47.2 0.8 copy-done.14
  48.0 11.3 %qkv.1 = bf16[5,768,256]{2,1,0:T(8,128)(2,1)} custom-call(s32[1]{0:T(128)} %bitcast.me_ref, bf16[768,384]{1,0:T(8,128)(2,1)} %copy-done, bf16[768,384]{1,0:T(8,128)(2,1)} %collective-permute-done.x1, bf16[768,384]{1,0:T(8,128)(2,1)} %copy-done.5, bf16[768,384]{1,0:T(8,128)(2,1)} %copy-done.14, f32[4,384]{1,0:T(4,128)} %pad_maximum_fusion.5.gain_ref, ...), custom_call_target="tpu_custom_call" | custom-call | flops 3019898880 | bytes 9000000 | tf_op jit(solution)/shard_map/qkv/pallas_call | solution.py:74
  59.3 2.7 copy.51
  62.0 1.6 pad.4.a_ref
  63.6 97.9 %attn.1 = (bf16[256,16,256]{2,1,0:T(8,128)(2,1)}, bf16[65536,256]{1,0:T(8,128)(2,1)}, bf16[65536,256]{1,0:T(8,128)(2,1)}) custom-call(s32[256]{0:T(256)} %len_ref.1, bf16[256,16,256]{2,1,0:T(8,128)(2,1)} %pad.4.a_ref, bf16[65536,256]{1,0:T(8,128)(2,1)} %bitcast.60, bf16[65536,256]{1,0:T(8,128)(2,1)} %bitcast.61), custom_call_target="tpu_custom_call" | custom-call | flops 40000000000 | bytes 134000000 | tf_op jit(solution)/shard_map/attn/pallas_call | solution.py:127
  161.5 2.0 copy.52
  163.5 1.0 copy.53
  164.8 0.8 convolution_convert_fusion
  165.6 1.5 collective-permute-start.9
  167.1 13.8 %collective-permute-done.9 = bf16[768,384]{1,0:T(8,128)(2,1)S(1)} collective-permute-done((bf16[768,384]{1,0:T(8,128)(2,1)S(1)}, bf16[768,384]{1,0:T(8,128)(2,1)S(1)}, u32[]{:S(2)}, u32[]{:S(2)}) %collective-permute-start.9) | collective-permute-done | bytes 589856 | tf_op jit(solution)/shard_map/ppermute | solution.py:284
  181.3 8.0 %constant_dynamic-slice_fusion = (bf16[40,128,384]{2,1,0:T(8,128)(2,1)}, bf16[40,128,384]{2,1,0:T(8,128)(2,1)}) fusion(bf16[40,256,384]{2,1,0:T(8,128)(2,1)} %param.31, s32[]{:T(128)S(6)} %select_n.47, s32[]{:T(128)S(6)} %select_n.46), kind=kLoop, calls=%fused_computation.42 | loop fusion | bytes 15728648 | tf_op jit(solution)/shard_map/dynamic_slice | solution.py:320
  189.3 0.5 collective-permute-start.18
  189.9 1.5 collective-permute-start.11
  191.5 2.1 collective-permute-done.11
  193.9 1.1 pad_maximum_fusion.h_ref
  195.1 1.9 broadcast_in_dim.52.ch_ref
  197.0 33.3 %moe1.1 = (bf16[8,384,256]{2,1,0:T(8,128)(2,1)}, bf16[8,384,256]{2,1,0:T(8,128)(2,1)}) custom-call(s32[1]{0:T(128)} %bitcast.18.cx_ref, bf16[768,768]{1,0:T(8,128)(2,1)} %pad_maximum_fusion.h_ref, bf16[8,768,128]{2,1,0:T(8,128)(2,1)} %broadcast_in_dim.52.ch_ref, bf16[40,384,128]{2,1,0:T(8,128)(2,1)} %get-tuple-element.26.a0, ...), custom_call_target="tpu_custom_call" | custom-call | flops 12079595520 | bytes 20000000 | tf_op jit(solution)/shard_map/moe1/pallas_call | solution.py:197
  230.3 1.5 collective-permute-start.16
  231.8 1.2 collective-permute-done.12
  233.0 0.5 fusion.9
  233.4 0.6 collective-permute-start.13
  234.0 34.1 %collective-permute-done.13 = f32[768,40]{0,1:T(8,128)S(1)} collective-permute-done((f32[768,40]{0,1:T(8,128)S(1)}, f32[768,40]{0,1:T(8,128)S(1)}, u32[]{:S(2)}, u32[]{:S(2)}) %collective-permute-start.13) | collective-permute-done | bytes 122912 | tf_op jit(solution)/shard_map/ppermute | solution.py:281
  268.4 2.2 convert_add_fusion
  270.6 0.6 fusion.um_ref
  271.3 1.5 collective-permute-start.17
  272.8 16.1 %collective-permute-done.17.uo_ref = bf16[8,384,128]{2,1,0:T(8,128)(2,1)S(1)} collective-permute-done((bf16[8,384,128]{2,1,0:T(8,128)(2,1)S(1)}, bf16[8,384,128]{2,1,0:T(8,128)(2,1)S(1)}, u32[]{:S(2)}, u32[]{:S(2)}) %collective-permute-start.17) | collective-permute-done | bytes 786464 | tf_op jit(solution)/shard_map/ppermute | solution.py:281
  288.9 0.9 copy-done.13
  289.8 24.8 %moe2.1 = (f32[768,384]{1,0:T(8,128)}, bf16[768,384]{1,0:T(8,128)(2,1)}) custom-call(s32[1]{0:T(128)} %bitcast.18.cx_ref, bf16[8,384,128]{2,1,0:T(8,128)(2,1)} %copy-done.3, bf16[8,384,128]{2,1,0:T(8,128)(2,1)} %copy-done.13, bf16[8,768,128]{2,1,0:T(8,128)(2,1)} %broadcast_in_dim.52.ch_ref, bf16[40,128,384]{2,1,0:T(8,128)(2,1)} %get-tuple-element.22.wa, ...), custom_call_target="tpu_custom_call" | custom-call | flops 6039797760 | bytes 10000000 | tf_op jit(solution)/shard_map/moe2/pallas_call | solution.py:262
  314.6 2.0 collective-permute-done.19
  316.6 1.4 add_convert_fusion
  318.0 1.5 collective-permute-start.20
  319.5 13.9 %collective-permute-done.20 = bf16[768,384]{1,0:T(8,128)(2,1)S(1)} collective-permute-done((bf16[768,384]{1,0:T(8,128)(2,1)S(1)}, bf16[768,384]{1,0:T(8,128)(2,1)S(1)}, u32[]{:S(2)}, u32[]{:S(2)}) %collective-permute-start.20) | collective-permute-done | bytes 589856 | tf_op jit(solution)/shard_map/ppermute | solution.py:284
  333.4 1.0 fusion.7
  (86 shorter events, 2.6 us)
Async XLA Ops:
  0.6 1.8 copy-start.7
  0.6 1.8 copy-start.6
  2.1 3.8 %copy-start.9 = (s32[3,256]{1,0:T(4,128)S(1)}, s32[3,256]{1,0:T(4,128)}, u32[]{:S(2)}) copy-start(s32[3,256]{1,0:T(4,128)} %param.16) | copy-start | bytes 9220
  2.5 8.5 %copy-start.2 = (bf16[5,384,256]{2,1,0:T(8,128)(2,1)}, bf16[5,384,256]{2,1,0:T(8,128)(2,1)S(1)}, u32[]{:S(2)}) copy-start(bf16[5,384,256]{2,1,0:T(8,128)(2,1)S(1)} %pad_maximum_fusion.1.w0) | copy-start | bytes 2949124
  2.6 34.8 %collective-permute-start.7 = (bf16[5,384,256]{2,1,0:T(8,128)(2,1)S(1)}, bf16[5,384,256]{2,1,0:T(8,128)(2,1)}, u32[]{:S(2)}, u32[]{:S(2)}) collective-permute-start(bf16[5,384,256]{2,1,0:T(8,128)(2,1)S(1)} %pad_maximum_fusion.1.w0), channel_id=1, source_target_pairs={{0,2},{2,0},{1,3},{3,1},{4,6},{6,4},{5,7},{7,5}} | collective-permute-start | bytes 2949128 | tf_op jit(solution)/shard_map/ppermute | solution.py:281
  5.9 41.3 %collective-permute-start.6 = (bf16[5,384,256]{2,1,0:T(8,128)(2,1)S(1)}, bf16[5,384,256]{2,1,0:T(8,128)(2,1)}, u32[]{:S(2)}, u32[]{:S(2)}) collective-permute-start(bf16[5,384,256]{2,1,0:T(8,128)(2,1)S(1)} %pad_maximum_fusion.1.w0), channel_id=1, source_target_pairs={{0,1},{1,0},{2,3},{3,2},{4,5},{5,4},{6,7},{7,6}} | collective-permute-start | bytes 2949128 | tf_op jit(solution)/shard_map/ppermute | solution.py:278
  6.0 5.7 %copy-start.11 = (bf16[384]{0:T(512)(128)(2,1)S(1)}, bf16[384]{0:T(512)(128)(2,1)}, u32[]{:S(2)}) copy-start(bf16[384]{0:T(512)(128)(2,1)} %param.22) | copy-start | bytes 2308
  6.0 5.7 %copy-start.12 = (bf16[384]{0:T(512)(128)(2,1)S(1)}, bf16[384]{0:T(512)(128)(2,1)}, u32[]{:S(2)}) copy-start(bf16[384]{0:T(512)(128)(2,1)} %param.27) | copy-start | bytes 2308
  6.0 5.8 %copy-start.10 = (s32[256]{0:T(256)S(1)}, s32[256]{0:T(256)}, u32[]{:S(2)}) copy-start(s32[256]{0:T(256)} %len_ref.1) | copy-start | bytes 3076
  6.0 5.8 %copy-start.4 = (bf16[768,384]{1,0:T(8,128)(2,1)S(1)}, bf16[768,384]{1,0:T(8,128)(2,1)}, u32[]{:S(2)}) copy-start(bf16[768,384]{1,0:T(8,128)(2,1)} %param.26) | copy-start | bytes 1769476
  11.0 9.8 %copy-start = (bf16[768,384]{1,0:T(8,128)(2,1)}, bf16[768,384]{1,0:T(8,128)(2,1)S(1)}, u32[]{:S(2)}) copy-start(bf16[768,384]{1,0:T(8,128)(2,1)S(1)} %gather_fusion) | copy-start | bytes 1769476
  11.0 35.7 %collective-permute-start = (bf16[768,384]{1,0:T(8,128)(2,1)S(1)}, bf16[768,384]{1,0:T(8,128)(2,1)}, u32[]{:S(2)}, u32[]{:S(2)}) collective-permute-start(bf16[768,384]{1,0:T(8,128)(2,1)S(1)} %gather_fusion), channel_id=1, source_target_pairs={{0,1},{1,0},{2,3},{3,2},{4,5},{5,4},{6,7},{7,6}} | collective-permute-start | bytes 1769480 | tf_op jit(solution)/shard_map/ppermute | solution.py:278
  11.6 22.4 %collective-permute-start.1 = (bf16[384,384]{1,0:T(8,128)(2,1)S(1)}, bf16[384,384]{1,0:T(8,128)(2,1)S(1)}, u32[]{:S(2)}, u32[]{:S(2)}) collective-permute-start(bf16[384,384]{1,0:T(8,128)(2,1)S(1)} %constant_dynamic-slice_fusion.6), channel_id=1, source_target_pairs={{0,2},{2,0},{1,3},{3,1},{4,6},{6,4},{5,7},{7,5}} | collective-permute-start | bytes 884744 | tf_op jit(solution)/shard_map/ppermute | solution.py:281
  11.7 30.7 %collective-permute-start.4 = (f32[2,384]{1,0:T(2,128)S(1)}, f32[2,384]{1,0:T(2,128)S(1)}, u32[]{:S(2)}, u32[]{:S(2)}) collective-permute-start(f32[2,384]{1,0:T(2,128)S(1)} %maximum_convert_fusion), channel_id=1, source_target_pairs={{0,1},{1,0},{2,3},{3,2},{4,5},{5,4},{6,7},{7,6}} | collective-permute-start | bytes 9224 | tf_op jit(solution)/shard_map/ppermute | solution.py:278
  11.9 9.0 %slice-start = ((s8[7864320]{0:T(1024)(128)(4,1)}), s8[4194304]{0:T(1024)(128)(4,1)S(1)}, s32[]{:S(2)}) async-start(s8[7864320]{0:T(1024)(128)(4,1)} %bitcast.44), calls=%async_computation | async-start | bytes 8388608
  13.4 7.5 %slice-start.1 = ((s8[7864320]{0:T(1024)(128)(4,1)}), s8[3670016]{0:T(1024)(128)(4,1)S(1)}, s32[]{:S(2)}) async-start(s8[7864320]{0:T(1024)(128)(4,1)} %bitcast.44), calls=%async_computation.1 | async-start | bytes 7340032
  34.0 8.2 %collective-permute-start.2 = (bf16[384,384]{1,0:T(8,128)(2,1)S(1)}, bf16[384,384]{1,0:T(8,128)(2,1)S(1)}, u32[]{:S(2)}, u32[]{:S(2)}) collective-permute-start(bf16[384,384]{1,0:T(8,128)(2,1)S(1)} %collective-permute-done.1), channel_id=1, source_target_pairs={{0,4},{4,0},{1,5},{5,1},{2,6},{6,2},{3,7},{7,3}} | collective-permute-start | bytes 884744 | tf_op jit(solution)/shard_map/ppermute | solution.py:284
  37.3 10.7 %collective-permute-start.8 = (bf16[5,384,256]{2,1,0:T(8,128)(2,1)}, bf16[5,384,256]{2,1,0:T(8,128)(2,1)}, u32[]{:S(2)}, u32[]{:S(2)}) collective-permute-start(bf16[5,384,256]{2,1,0:T(8,128)(2,1)} %collective-permute-done.7.w2), channel_id=1, source_target_pairs={{0,1},{1,0},{2,3},{3,2},{4,5},{5,4},{6,7},{7,6}} | collective-permute-start | bytes 2949128 | tf_op jit(solution)/shard_map/ppermute | solution.py:278
  42.4 5.7 %copy-start.5 = (bf16[768,384]{1,0:T(8,128)(2,1)}, bf16[768,384]{1,0:T(8,128)(2,1)S(1)}, u32[]{:S(2)}) copy-start(bf16[768,384]{1,0:T(8,128)(2,1)S(1)} %maximum_select_fusion.x2) | copy-start | bytes 1769476
  42.4 4.8 %collective-permute-start.3 = (bf16[768,384]{1,0:T(8,128)(2,1)S(1)}, bf16[768,384]{1,0:T(8,128)(2,1)S(1)}, u32[]{:S(2)}, u32[]{:S(2)}) collective-permute-start(bf16[768,384]{1,0:T(8,128)(2,1)S(1)} %maximum_select_fusion.x2), channel_id=1, source_target_pairs={{0,1},{1,0},{2,3},{3,2},{4,5},{5,4},{6,7},{7,6}} | collective-permute-start | bytes 1769480 | tf_op jit(solution)/shard_map/ppermute | solution.py:278
  42.5 3.7 %collective-permute-start.5 = (f32[4,384]{1,0:T(4,128)S(1)}, f32[4,384]{1,0:T(4,128)S(1)}, u32[]{:S(2)}, u32[]{:S(2)}) collective-permute-start(f32[4,384]{1,0:T(4,128)S(1)} %pad_maximum_fusion.4), channel_id=1, source_target_pairs={{0,2},{2,0},{1,3},{3,1},{4,6},{6,4},{5,7},{7,5}} | collective-permute-start | bytes 18440 | tf_op jit(solution)/shard_map/ppermute | solution.py:281
  46.1 149.0 %collective-permute-start.14 = (bf16[40,384,128]{2,1,0:T(8,128)(2,1)}, bf16[40,384,128]{2,1,0:T(8,128)(2,1)}, u32[]{:S(2)}, u32[]{:S(2)}) collective-permute-start(bf16[40,384,128]{2,1,0:T(8,128)(2,1)} %get-tuple-element.25), channel_id=1, source_target_pairs={{0,1},{1,0},{2,3},{3,2},{4,5},{5,4},{6,7},{7,6}} | collective-permute-start | bytes 11796488 | tf_op jit(solution)/shard_map/ppermute | solution.py:278
  46.7 148.4 %collective-permute-start.15 = (bf16[40,384,128]{2,1,0:T(8,128)(2,1)}, bf16[40,384,128]{2,1,0:T(8,128)(2,1)}, u32[]{:S(2)}, u32[]{:S(2)}) collective-permute-start(bf16[40,384,128]{2,1,0:T(8,128)(2,1)} %get-tuple-element.23), channel_id=1, source_target_pairs={{0,1},{1,0},{2,3},{3,2},{4,5},{5,4},{6,7},{7,6}} | collective-permute-start | bytes 11796488 | tf_op jit(solution)/shard_map/ppermute | solution.py:278
  47.2 0.8 copy-start.14
  164.8 16.1 %copy-start.1 = (bf16[768,384]{1,0:T(8,128)(2,1)S(1)}, bf16[768,384]{1,0:T(8,128)(2,1)}, u32[]{:S(2)}) copy-start(bf16[768,384]{1,0:T(8,128)(2,1)} %copy-done) | copy-start | bytes 1769476
  165.6 15.3 %collective-permute-start.9 = (bf16[768,384]{1,0:T(8,128)(2,1)S(1)}, bf16[768,384]{1,0:T(8,128)(2,1)S(1)}, u32[]{:S(2)}, u32[]{:S(2)}) collective-permute-start(bf16[768,384]{1,0:T(8,128)(2,1)S(1)} %convolution_convert_fusion), channel_id=1, source_target_pairs={{0,4},{4,0},{1,5},{5,1},{2,6},{6,2},{3,7},{7,3}} | collective-permute-start | bytes 1769480 | tf_op jit(solution)/shard_map/ppermute | solution.py:284
  181.2 10.2 %copy-start.8 = (s32[3,256,8]{1,2,0:T(8,128)S(1)}, s32[3,256,8]{1,2,0:T(8,128)}, u32[]{:S(2)}) copy-start(s32[3,256,8]{1,2,0:T(8,128)} %param.18) | copy-start | bytes 73732
  181.2 8.5 %collective-permute-start.10 = (bf16[768,384]{1,0:T(8,128)(2,1)S(1)}, bf16[768,384]{1,0:T(8,128)(2,1)S(1)}, u32[]{:S(2)}, u32[]{:S(2)}) collective-permute-start(bf16[768,384]{1,0:T(8,128)(2,1)S(1)} %get-tuple-element.20), channel_id=1, source_target_pairs={{0,1},{1,0},{2,3},{3,2},{4,5},{5,4},{6,7},{7,6}} | collective-permute-start | bytes 1769480 | tf_op jit(solution)/shard_map/ppermute | solution.py:278
  189.3 83.5 %collective-permute-start.18 = (bf16[40,128,384]{2,1,0:T(8,128)(2,1)}, bf16[40,128,384]{2,1,0:T(8,128)(2,1)}, u32[]{:S(2)}, u32[]{:S(2)}) collective-permute-start(bf16[40,128,384]{2,1,0:T(8,128)(2,1)} %get-tuple-element.21), channel_id=1, source_target_pairs={{0,1},{1,0},{2,3},{3,2},{4,5},{5,4},{6,7},{7,6}} | collective-permute-start | bytes 11796488 | tf_op jit(solution)/shard_map/ppermute | solution.py:278
  189.9 3.6 %collective-permute-start.11 = (f32[768]{0:T(1024)S(1)}, f32[768]{0:T(1024)S(1)}, u32[]{:S(2)}, u32[]{:S(2)}) collective-permute-start(f32[768]{0:T(1024)S(1)} %add.85), channel_id=1, source_target_pairs={{0,2},{2,0},{1,3},{3,1},{4,6},{6,4},{5,7},{7,5}} | collective-permute-start | bytes 9224 | tf_op jit(solution)/shard_map/ppermute | solution.py:281
  197.0 34.8 %copy-start.15 = (bf16[384,40]{0,1:T(8,128)(2,1)S(1)}, bf16[384,40]{0,1:T(8,128)(2,1)}, u32[]{:S(2)}) copy-start(bf16[384,40]{0,1:T(8,128)(2,1)} %param.28) | copy-start | bytes 92164
  230.3 38.1 %collective-permute-start.16 = (bf16[8,384,256]{2,1,0:T(8,128)(2,1)}, bf16[8,384,256]{2,1,0:T(8,128)(2,1)}, u32[]{:S(2)}, u32[]{:S(2)}) collective-permute-start(bf16[8,384,256]{2,1,0:T(8,128)(2,1)} %get-tuple-element.12), channel_id=1, source_target_pairs={{0,2},{2,0},{1,3},{3,1},{4,6},{6,4},{5,7},{7,5}} | collective-permute-start | bytes 4718600 | tf_op jit(solution)/shard_map/ppermute | solution.py:281
  231.8 1.2 collective-permute-start.12
  233.4 34.7 %collective-permute-start.13 = (f32[768,40]{0,1:T(8,128)S(1)}, f32[768,40]{0,1:T(8,128)S(1)}, u32[]{:S(2)}, u32[]{:S(2)}) collective-permute-start(f32[768,40]{0,1:T(8,128)S(1)} %fusion.9), channel_id=1, source_target_pairs={{0,2},{2,0},{1,3},{3,1},{4,6},{6,4},{5,7},{7,5}} | collective-permute-start | bytes 368648 | tf_op jit(solution)/shard_map/ppermute | solution.py:281
  271.3 17.6 %copy-start.3 = (bf16[8,384,128]{2,1,0:T(8,128)(2,1)}, bf16[8,384,128]{2,1,0:T(8,128)(2,1)S(1)}, u32[]{:S(2)}) copy-start(bf16[8,384,128]{2,1,0:T(8,128)(2,1)S(1)} %fusion.um_ref) | copy-start | bytes 2359300
  271.3 17.6 %collective-permute-start.17 = (bf16[8,384,128]{2,1,0:T(8,128)(2,1)S(1)}, bf16[8,384,128]{2,1,0:T(8,128)(2,1)S(1)}, u32[]{:S(2)}, u32[]{:S(2)}) collective-permute-start(bf16[8,384,128]{2,1,0:T(8,128)(2,1)S(1)} %fusion.um_ref), channel_id=1, source_target_pairs={{0,2},{2,0},{1,3},{3,1},{4,6},{6,4},{5,7},{7,5}} | collective-permute-start | bytes 2359304 | tf_op jit(solution)/shard_map/ppermute | solution.py:281
  288.9 0.9 copy-start.13
  314.6 2.0 collective-permute-start.19
  318.0 15.4 %collective-permute-start.20 = (bf16[768,384]{1,0:T(8,128)(2,1)S(1)}, bf16[768,384]{1,0:T(8,128)(2,1)S(1)}, u32[]{:S(2)}, u32[]{:S(2)}) collective-permute-start(bf16[768,384]{1,0:T(8,128)(2,1)S(1)} %add_convert_fusion), channel_id=1, source_target_pairs={{0,4},{4,0},{1,5},{5,1},{2,6},{6,2},{3,7},{7,3}} | collective-permute-start | bytes 1769480 | tf_op jit(solution)/shard_map/ppermute | solution.py:284

commit v2 on v0

v2 whole, which is shorter than its diff:
```python
import functools

import jax
import jax.numpy as jnp
from jax import lax
from jax.experimental import pallas as pl
from jax.experimental.pallas import tpu as pltpu
from jax.sharding import PartitionSpec as P


EPS = 1e-5
ROPE_BASE = 1.0e6
F32 = jnp.float32
BF16 = jnp.bfloat16
VMEM_LIMIT = 60 * 1024 * 1024
NB = 8


def cost(flops, moved):
    return pl.CostEstimate(flops=flops, bytes_accessed=moved, transcendentals=0)


def fixed(*shape):
    return pl.BlockSpec(shape, lambda *_: (0,) * len(shape))


def lead(*shape):
    return pl.BlockSpec(shape, lambda i, *_: (i,) + (0,) * (len(shape) - 1))


def norm_into(me, refs, tokens, hs):
    place = [me, me + 1 - 2 * (me % 2), (me + 2) % 4]
    place.append((place[1] + 2) % 4)
    rt = 128
    gains = [r[tokens : tokens + 1, :].astype(F32) for r in refs]

    def body(i, carry):
        rows = pl.ds(pl.multiple_of(i * rt, rt), rt)
        sq = []
        for r in refs:
            v = r[rows, :].astype(F32)
            sq.append(jnp.sum(v * v, axis=-1, keepdims=True))
        total = (sq[0] + sq[1]) + (sq[2] + sq[3])
        scale = lax.rsqrt(total / (4.0 * refs[0].shape[1]) + EPS)
        for n, r in enumerate(refs):
            hs[place[n], rows, :] = (r[rows, :].astype(F32) * scale * gains[n]).astype(BF16)
        return carry

    lax.fori_loop(0, tokens // rt, body, 0)


def project(me, hs, refs, ws, cos_ref, sin_ref, out_ref, turn):
    place = [me, me + 1 - 2 * (me % 2), (me + 2) % 4]
    place.append((place[1] + 2) % 4)
    for n, ref in enumerate(refs):
        ws[place[n]] = ref[0]
    low = lax.broadcasted_iota(jnp.int32, (1, 256), 1) % 64 < 32
    mt = 256
    for m in range(hs.shape[1] // mt):
        rows = slice(m * mt, (m + 1) * mt)
        acc = jnp.dot(hs[0, rows, :], ws[0], preferred_element_type=F32)
        for i in range(1, 4):
            acc += jnp.dot(hs[i, rows, :], ws[i], preferred_element_type=F32)
        v = acc.astype(BF16).astype(F32)
        other = jnp.where(low, pltpu.roll(v, 224, 1), pltpu.roll(v, 32, 1))
        cos, sin = cos_ref[rows, :], sin_ref[rows, :]
        if turn is not None:
            cos, sin = jnp.where(turn, cos, 1.0), jnp.where(turn, sin, 0.0)
        cos = jnp.concatenate([cos] * 2, axis=1)
        sin = jnp.concatenate([sin] * 2, axis=1)
        out_ref[0, rows, :] = (v * cos + other * sin).astype(BF16)


def qkv_a_kernel(me_ref, x0, x1, x2, x3, w0, w1, w2, w3, cos_ref, sin_ref, hs, out_ref, ws):
    @pl.when(pl.program_id(0) == 0)
    def _():
        norm_into(me_ref[0], (x0, x1, x2, x3), cos_ref.shape[0], hs)

    project(me_ref[0], hs, (w0, w1, w2, w3), ws, cos_ref, sin_ref, out_ref, None)


def qkv_b_kernel(me_ref, hs, w0, w1, w2, w3, cos_ref, sin_ref, before, out_ref, ws):
    project(me_ref[0], hs, (w0, w1, w2, w3), ws, cos_ref, sin_ref, out_ref, pl.program_id(0) < 2)


def qkv_calls(me, xs, was, wbs, cos, sin):
    tokens = cos.shape[0]
    rows, width = xs[0].shape
    na, nb = was[0].shape[0], wbs[0].shape[0]
    full = jax.ShapeDtypeStruct((na + nb, tokens, 256), BF16)
    w_spec = [lead(1, width, 256)] * 4
    t_spec = [fixed(tokens, 128)] * 2
    h_spec = fixed(4, tokens, width)
    params = pltpu.CompilerParams(vmem_limit_bytes=VMEM_LIMIT, dimension_semantics=("arbitrary",))
    h, first = pl.pallas_call(
        qkv_a_kernel,
        grid_spec=pltpu.PrefetchScalarGridSpec(
            num_scalar_prefetch=1,
            grid=(na,),
            in_specs=[fixed(rows, width)] * 4 + w_spec + t_spec,
            out_specs=[h_spec, lead(1, tokens, 256)],
            scratch_shapes=[pltpu.VMEM((4, width, 256), BF16)],
        ),
        out_shape=[jax.ShapeDtypeStruct((4, tokens, width), BF16), full],
        compiler_params=params,
        cost_estimate=cost(2 * tokens * width * 4 * 512, 6_000_000),
        name="qkv_a",
    )(me, *xs, *was, cos, sin)
    return pl.pallas_call(
        qkv_b_kernel,
        grid_spec=pltpu.PrefetchScalarGridSpec(
            num_scalar_prefetch=1,
            grid=(nb,),
            in_specs=[h_spec] + w_spec + t_spec + [pl.BlockSpec(memory_space=pl.ANY)],
            out_specs=pl.BlockSpec((1, tokens, 256), lambda i, m: (na + i, 0, 0)),
            scratch_shapes=[pltpu.VMEM((4, width, 256), BF16)],
        ),
        out_shape=full,
        input_output_aliases={8: 0},
        compiler_params=params,
        cost_estimate=cost(2 * tokens * width * 4 * 768, 6_000_000),
        name="qkv_b",
    )(me, h, *wbs, cos, sin, first)


def attn_kernel(off_ref, len_ref, a_ref, k_ref, v_ref, o_ref, lhs_ref, snew_ref, enew_ref):
    base = (off_ref[0] + pl.program_id(0)) * NB
    slot = lax.broadcasted_iota(jnp.int32, (1, 256), 1)
    block = slot // 64
    row = lax.broadcasted_iota(jnp.int32, (64, 128), 0) % 16 % 3
    col = lax.broadcasted_iota(jnp.int32, (64, 128), 1)
    every = a_ref[...].reshape(NB * 16, 256)
    scaled = every * jnp.bfloat16(0.125)
    for i in range(NB):
        q = scaled[i * 16 : i * 16 + 16]
        zero = jnp.zeros_like(q)
        lhs_ref[i * 64 : i * 64 + 64, :] = jnp.concatenate([jnp.where(block == k, q, zero) for k in range(4)], axis=0)
    snew_ref[...] = lax.dot_general(lhs_ref[...], every, (((1,), (1,)), ((), ())), preferred_element_type=F32)
    totals, mixes = [], []
    for i in range(NB):
        pos = len_ref[base + i]
        rows = slice(i * 64, i * 64 + 64)
        s_old = jnp.dot(lhs_ref[rows, :], k_ref[i * 256 : (i + 1) * 256, :], preferred_element_type=F32)
        fresh = (col >= i * 16 + 9) & (col <= row + (i * 16 + 9))
        s_old = jnp.where(slot < pos, s_old, -1.0e30)
        s_new = jnp.where(fresh, snew_ref[rows, :], -1.0e30)
        peak = jnp.max(jnp.maximum(jnp.maximum(s_old[:, :128], s_old[:, 128:]), s_new), axis=-1, keepdims=True)
        e_old = jnp.exp(s_old - peak)
        e_new = jnp.exp(s_new - peak)
        enew_ref[rows, :] = e_new.astype(BF16)
        total = jnp.sum(e_old[:, :128] + e_old[:, 128:] + e_new, axis=-1, keepdims=True)
        mixed = lax.dot_general(e_old.astype(BF16), v_ref[i * 256 : (i + 1) * 256, :], (((1,), (1,)), ((), ())), preferred_element_type=F32)
        res = mixed[0:16]
        tot = jnp.broadcast_to(total[0:16], (16, 256))
        for k in range(1, 4):
            part = slice(16 * k, 16 * k + 16)
            res = jnp.where(block == k, mixed[part], res)
            tot = jnp.where(block == k, total[part], tot)
        mixes.append(res)
        totals.append(tot)
    fresh_v = jnp.concatenate([every[3:], every[:3]], axis=0)
    extra = jnp.dot(enew_ref[...], fresh_v, preferred_element_type=F32)
    for i in range(NB):
        res = extra[i * 64 : i * 64 + 16]
        for k in range(1, 4):
            res = jnp.where(block == k, extra[i * 64 + 16 * k : i * 64 + 16 * k + 16], res)
        o_ref[i] = ((mixes[i] + res) / totals[i]).astype(BF16)


def attn_call(offset, lengths, acts, k_rows, v_rows, count):
    grid_spec = pltpu.PrefetchScalarGridSpec(
        num_scalar_prefetch=2,
        grid=(count // NB,),
        in_specs=[pl.BlockSpec((NB, 16, 256), lambda i, f, m: (f[0] + i, 0, 0))] + [pl.BlockSpec((NB * 256, 256), lambda i, f, m: (f[0] + i, 0))] * 2,
        out_specs=lead(NB, 16, 256),
        scratch_shapes=[pltpu.VMEM((NB * 64, 256), BF16), pltpu.VMEM((NB * 64, 128), F32), pltpu.VMEM((NB * 64, 128), BF16)],
    )
    return pl.pallas_call(
        attn_kernel,
        grid_spec=grid_spec,
        out_shape=jax.ShapeDtypeStruct((count, 16, 256), BF16),
        compiler_params=pltpu.CompilerParams(vmem_limit_bytes=VMEM_LIMIT, dimension_semantics=("arbitrary",)),
        cost_estimate=cost(count * 120_000_000, count * 262144),
        name="attn",
    )(offset, lengths, acts, k_rows, v_rows)


WB = 16
PIECES = (64, 96, 32, 64)


def write_kernel(start, aliased, len_ref, a_ref, k_ref, v_ref, *rest):
    ko_ref, vo_ref = rest[2:] if aliased else rest
    base = start + pl.program_id(0) * WB
    cols = jnp.transpose(a_ref[...].reshape(WB * 16, 256).astype(F32))
    slot = lax.broadcasted_iota(jnp.int32, (1, 256), 1)
    for i in range(WB):
        pos = len_ref[base + i]
        rows = slice(i * 256, (i + 1) * 256)
        hit = (slot >= pos) & (slot <= pos + 2)
        part = cols[:, (i // 8) * 128 : (i // 8) * 128 + 128]
        for first, src, dst in ((9, k_ref, ko_ref), (12, v_ref, vo_ref)):
            moved = pltpu.roll(part, (pos - (i % 8) * 16 - first + 256) % 128, 1).astype(BF16)
            for side in range(2):
                lanes = slice(side * 128, side * 128 + 128)
                dst[rows, lanes] = jnp.where(hit[:, lanes], moved, src[rows, lanes])


def write_call(start, count, lengths, acts, k_rows, v_rows, before):
    s0 = start // WB
    block = pl.BlockSpec((WB * 256, 256), lambda i, m: (s0 + i, 0))
    aliased = before is not None
    grid_spec = pltpu.PrefetchScalarGridSpec(
        num_scalar_prefetch=1,
        grid=(count // WB,),
        in_specs=[pl.BlockSpec((WB, 16, 256), lambda i, m: (s0 + i, 0, 0)), block, block]
        + ([pl.BlockSpec(memory_space=pl.ANY)] * 2 if aliased else []),
        out_specs=[block, block],
    )
    return pl.pallas_call(
        functools.partial(write_kernel, start, aliased),
        grid_spec=grid_spec,
        out_shape=[jax.ShapeDtypeStruct(k_rows.shape, BF16)] * 2,
        input_output_aliases={4: 0, 5: 1} if aliased else {},
        compiler_params=pltpu.CompilerParams(vmem_limit_bytes=VMEM_LIMIT, dimension_semantics=("arbitrary",)),
        cost_estimate=cost(count * 180_000_000, count * 524288),
        name="write",
    )(lengths, acts, k_rows, v_rows, *(before if aliased else ()))


E1 = 8


def moe1_kernel(half_ref, h_ref, ch_ref, a0, l0, a1, l1, out_ref, dense):
    step = pl.program_id(0)
    half = out_ref.shape[1]
    rt = 16

    @pl.when(step == 0)
    def _():
        out_ref[...] = jnp.zeros_like(out_ref)

    for g in range(E1 // 4):
        for k in range(4):
            e = g * 4 + k
            top = jnp.concatenate([a0[e], l0[e]], axis=1)
            low = jnp.concatenate([a1[e], l1[e]], axis=1)
            w = jnp.concatenate([top, low], axis=0)
            dense[g, k] = jnp.dot(h_ref[...], w, preferred_element_type=F32).astype(BF16)
        ids = [(step * E1 + g * 4 + k).astype(F32).astype(BF16) for k in range(4)]
        for i in range(half // rt):
            rows = slice(i * rt, (i + 1) * rt)
            d = [dense[g, k, rows, :] for k in range(4)]
            for j in range(8):
                chj = ch_ref[j, rows, :]
                hits = [chj == ids[k] for k in range(4)]
                for side in range(2):
                    lanes = slice(side * 128, side * 128 + 128)
                    acc = out_ref[j, rows, lanes]
                    for k in range(4):
                        acc = jnp.where(hits[k], d[k][:, lanes], acc)
                    out_ref[j, rows, lanes] = acc


def moe1_call(pick, h2, ch, w_act, w_lin, a1, l1):
    half = h2.shape[0] // 2
    experts, rows, _ = a1.shape
    mine = pl.BlockSpec((E1, rows, 128), lambda i, m: (i, 0, m[1]))
    theirs = lead(E1, rows, 128)
    grid_spec = pltpu.PrefetchScalarGridSpec(
        num_scalar_prefetch=1,
        grid=(experts // E1,),
        in_specs=[pl.BlockSpec((half, 2 * rows), lambda i, m: (m[0], 0)), pl.BlockSpec((8, half, 128), lambda i, m: (0, m[0], 0)), mine, mine, theirs, theirs],
        out_specs=fixed(8, half, 256),
        scratch_shapes=[pltpu.VMEM((E1 // 4, 4, half, 256), BF16)],
    )
    return pl.pallas_call(
        moe1_kernel,
        grid_spec=grid_spec,
        out_shape=jax.ShapeDtypeStruct((8, half, 256), BF16),
        compiler_params=pltpu.CompilerParams(vmem_limit_bytes=VMEM_LIMIT, dimension_semantics=("arbitrary",)),
        cost_estimate=cost(2 * half * 2 * rows * 256 * experts, 20_000_000),
        name="moe1",
    )(pick, h2, ch, w_act, w_lin, a1, l1)


E2 = 8


def moe2_kernel(half_ref, u_ref, ch_ref, wa, wb, own_ref, send_ref, spread, acc_ref):
    step = pl.program_id(0)
    half = u_ref.shape[1]
    width = wa.shape[2]
    rt = 16

    @pl.when(step == 0)
    def _():
        acc_ref[...] = jnp.zeros_like(acc_ref)

    prod = None
    for g in range(E2 // 4):
        ids = [(step * E2 + g * 4 + k).astype(F32).astype(BF16) for k in range(4)]
        for i in range(half // rt):
            rows = slice(i * rt, (i + 1) * rt)
            out = [jnp.zeros((rt, 128), BF16) for _ in range(4)]
            for j in range(8):
                chj = ch_ref[j, rows, :]
                uj = u_ref[j, rows, :]
                for k in range(4):
                    out[k] = jnp.where(chj == ids[k], uj, out[k])
            for k in range(4):
                spread[g, rows, k * 128 : (k + 1) * 128] = out[k]
        es = slice(g * 4, g * 4 + 4)
        w = jnp.concatenate([wa[es].reshape(512, width), wb[es].reshape(512, width)], axis=1)
        part = jnp.dot(spread[g], w, preferred_element_type=F32)
        prod = part if prod is None else prod + part
    acc_ref[...] += prod

    @pl.when(step == pl.num_programs(0) - 1)
    def _():
        own_ref[...] = acc_ref[:, :width]
        send_ref[...] = acc_ref[:, width:].astype(BF16)


def moe2_call(pick, u, ch, w_down, wb):
    half = u.shape[1]
    experts, rows, width = wb.shape
    grid_spec = pltpu.PrefetchScalarGridSpec(
        num_scalar_prefetch=1,
        grid=(experts // E2,),
        in_specs=[
            fixed(8, half, 128),
            pl.BlockSpec((8, half, 128), lambda i, m: (0, m[0], 0)),
            pl.BlockSpec((E2, rows, width), lambda i, m: (i, m[1], 0)),
            lead(E2, rows, width),
        ],
        out_specs=[fixed(half, width)] * 2,
        scratch_shapes=[pltpu.VMEM((E2 // 4, half, 512), BF16), pltpu.VMEM((half, 2 * width), F32)],
    )
    return pl.pallas_call(
        moe2_kernel,
        grid_spec=grid_spec,
        out_shape=[jax.ShapeDtypeStruct((half, width), F32), jax.ShapeDtypeStruct((half, width), BF16)],
        compiler_params=pltpu.CompilerParams(vmem_limit_bytes=VMEM_LIMIT, dimension_semantics=("arbitrary",)),
        cost_estimate=cost(2 * half * rows * 2 * width * experts, 10_000_000),
        name="moe2",
    )(pick, u, ch, w_down, wb)


def solution(mesh):
    cache_spec = P('dp', None, 'y', None)
    in_specs = (P(None, 'dp'), P('dp'), P(None, 'dp', None), P(None, 'x'), cache_spec, cache_spec, P('x'), P('x', 'y'), P('x', 'y'), P('x', 'y'), P('y', 'x'), P('x'), P('x', None), P(None, 'x', 'y'), P(None, 'x', 'y'), P(None, 'y', 'x'))
    out_specs = (P(None, 'dp', 'x'), cache_spec, cache_spec)

    def core_swap(v):
        return lax.ppermute(v, 'x', [(0, 1), (1, 0), (2, 3), (3, 2)])

    def chip_swap(v):
        return lax.ppermute(v, 'x', [(0, 2), (2, 0), (1, 3), (3, 1)])

    def y_swap(v):
        return lax.ppermute(v, 'y', [(0, 1), (1, 0)])

    def layer(tokens, lengths, choices, emb_table, k_cache, v_cache, g_attn, w_q, w_k, w_v, w_o, g_ffn, w_router, w_act, w_lin, w_down):
        steps, batch = tokens.shape
        width = emb_table.shape[1]
        kv, hd = k_cache.shape[2], k_cache.shape[3]
        slots = k_cache.shape[1]
        group = w_q.shape[1] // (kv * hd)
        experts = w_act.shape[0]
        width_full = width * 4
        me = lax.axis_index('x').astype(jnp.int32)
        my = lax.axis_index('y').astype(jnp.int32)
        core = me % 2
        cx = me // 2
        n_tok = steps * batch

        barrier = lax.optimization_barrier
        wq = w_q.reshape(width, kv, group, hd).transpose(2, 0, 1, 3).reshape(group, width, kv * hd)
        w_a = wq[:2]
        w_b = jnp.concatenate([wq[2:], w_k[None], w_v[None]], axis=0)
        half_tok = n_tok // 2
        x_in = jnp.take(emb_table, tokens.reshape(n_tok), axis=0, mode='clip')
        g_rows = jnp.concatenate([g_attn[None], g_ffn[None], jnp.zeros((14, width), BF16)], axis=0)
        x_ext = jnp.concatenate([x_in, g_rows])
        part = jnp.concatenate([lax.dynamic_slice_in_dim(x_in, my * half_tok, half_tok, 0), g_rows], axis=0)
        part, x_ext = barrier((part, x_ext))
        part = chip_swap(part)
        x_mate = core_swap(x_ext)
        wa2 = chip_swap(w_a)
        wb2 = chip_swap(w_b)

        def theirs(w, axis):
            return lax.dynamic_slice_in_dim(w, (1 - core) * 128, 128, axis)

        act_s = theirs(w_act, 2)
        lin_s, down_s = theirs(w_lin, 2), theirs(w_down, 1)
        part, act_s = barrier((part, act_s))
        part_o = y_swap(part[:half_tok])
        part_o, lin_s, down_s = barrier((part_o, lin_s, down_s))
        lo = jnp.where(my == 0, part[:half_tok], part_o)
        hi = jnp.where(my == 0, part_o, part[:half_tok])
        x_far = jnp.concatenate([lo, hi, part[half_tok:]])
        x_far_mate = core_swap(x_far)
        wa1, wb1, wa3 = core_swap(w_a), core_swap(w_b), core_swap(wa2)

        router = jnp.concatenate([w_router, core_swap(w_router)], axis=0)

        positions = lengths[None, :] + jnp.arange(steps, dtype=jnp.int32)[:, None]
        inv_freq = ROPE_BASE ** (-(jnp.arange(hd // 2, dtype=F32) * 2.0 / hd))
        angles = positions.reshape(n_tok).astype(F32)[:, None] * inv_freq[None, :]
        cos, sin = jnp.cos(angles), jnp.sin(angles)
        cos2, sin2 = jnp.tile(cos, (1, 4)), jnp.tile(jnp.concatenate([-sin, sin], axis=1), (1, 2))
        choice_rows = choices.reshape(n_tok, 8)
        ch_rows = jnp.broadcast_to(choice_rows.T.astype(BF16)[:, :, None], (8, n_tok, 128))
        wo = w_o.reshape(kv, group, hd, width).transpose(1, 0, 2, 3).reshape(group * kv * hd, width)

        pick_m, pick_f = jnp.stack([cx, core]), jnp.stack([1 - cx, core])
        offset = (core * (batch // 2) // NB)[None]
        wb2, ch_rows, wo, pick_m, pick_f, offset = barrier((wb2, ch_rows, wo, pick_m, pick_f, offset))
        wb3 = core_swap(wb2)
        act1, lin1, down1 = core_swap(act_s), core_swap(lin_s), core_swap(down_s)
        qkv = qkv_calls(me[None], (x_ext, x_mate, x_far, x_far_mate), (w_a, wa1, wa2, wa3), (w_b, wb1, wb2, wb3), cos2, sin2)
        acts = qkv.reshape(5, steps, batch, 256).transpose(2, 0, 1, 3).reshape(batch, 15, 256)
        acts = jnp.pad(acts, ((0, 0), (0, 1), (0, 0)))
        k_rows = k_cache.transpose(0, 2, 3, 1).reshape(batch * kv * hd, slots)
        v_rows = v_cache.transpose(0, 2, 3, 1).reshape(batch * kv * hd, slots)
        starts = [sum(PIECES[:i]) for i in range(len(PIECES))]

        def write(i, acts, before):
            return tuple(write_call(starts[i], PIECES[i], lengths, acts, k_rows, v_rows, before))

        def back(rows):
            return rows.reshape(batch, kv, hd, slots).transpose(0, 3, 1, 2)

        o = attn_call(offset, lengths, acts, k_rows, v_rows, batch // 2)[:, : steps * group]
        o_mate = core_swap(o)
        o = jnp.where(core == 0, jnp.concatenate([o, o_mate]), jnp.concatenate([o_mate, o]))
        oc = o.reshape(batch, group, steps, 256).transpose(2, 0, 1, 3).reshape(n_tok, group * 256)
        proj = jnp.dot(oc, wo, preferred_element_type=F32).astype(BF16)

        proj, acts = barrier((proj, acts))
        proj_y = y_swap(proj)
        caches = write(0, acts, None)
        proj_y, caches = barrier((proj_y, caches))

        x1 = (x_in.astype(F32) + (proj.astype(F32) + proj_y.astype(F32))).astype(BF16)
        x1_mate = core_swap(x1)
        x1f, x1mf = x1.astype(F32), x1_mate.astype(F32)
        sq = jnp.sum(x1f * x1f, axis=-1) + jnp.sum(x1mf * x1mf, axis=-1)
        sq = sq + chip_swap(sq)
        scale = lax.rsqrt(sq / width_full + EPS)[:, None]
        g_own, g_mate = g_ffn.astype(F32), x_mate[n_tok + 1].astype(F32)
        h2 = jnp.concatenate([x1f * scale * g_own, x1mf * scale * g_mate], axis=1).astype(BF16)
        logits = jnp.dot(h2, router, preferred_element_type=F32)

        send = moe1_call(pick_f, h2, ch_rows, w_act, w_lin, act1, lin1)
        send, h2, acts = barrier((send, h2, acts))
        got = chip_swap(send)
        keep = moe1_call(pick_m, h2, ch_rows, w_act, w_lin, act1, lin1)
        caches = write(1, acts, caches)
        logits = logits + chip_swap(logits)
        picked = jnp.sum(jnp.where(choice_rows[:, :, None] == jnp.arange(experts)[None, None, :], logits[:, None, :], 0.0), axis=-1)
        gate = jax.nn.softmax(picked, axis=-1)
        gate_mine = lax.dynamic_slice_in_dim(gate, cx * half_tok, half_tok, 0).T
        got, caches, gate_mine = barrier((got, caches, gate_mine))
        hid = keep.astype(F32) + got.astype(F32)
        u = (gate_mine[:, :, None] * jax.nn.silu(hid[..., :128]) * hid[..., 128:]).astype(BF16)

        u, acts = barrier((u, acts))
        u_far = chip_swap(u)
        own_m, snd_m = moe2_call(pick_m, u, ch_rows, w_down, down1)
        caches = write(2, acts, caches)
        u_far, caches, acts, snd_m = barrier((u_far, caches, acts, snd_m))
        sum_m = (own_m + core_swap(snd_m).astype(F32)).astype(BF16)
        sum_m_y = y_swap(sum_m)
        own_f, snd_f = moe2_call(pick_f, u_far, ch_rows, w_down, down1)
        snd_f, acts = barrier((snd_f, acts))
        sum_f = (own_f + core_swap(snd_f).astype(F32)).astype(BF16)
        sum_f_y = y_swap(sum_f)
        caches = write(3, acts, caches)
        sum_f_y, caches = barrier((sum_f_y, caches))
        moe_m = sum_m.astype(F32) + sum_m_y.astype(F32)
        moe_f = sum_f.astype(F32) + sum_f_y.astype(F32)
        moe = jnp.where(cx == 0, jnp.concatenate([moe_m, moe_f]), jnp.concatenate([moe_f, moe_m]))
        hidden = (x1.astype(F32) + moe).astype(BF16).reshape(steps, batch, width)
        k_new, v_new = caches
        return hidden, back(k_new), back(v_new)

    return jax.shard_map(layer, mesh=mesh, in_specs=in_specs, out_specs=out_specs, check_vma=False)
```

time: 999 us -> 235 us (0.24)
  waiting for transfers between devices: 577 us -> 20.9 us
  matrix products: 182 us -> 1.23 us
  Pallas kernels: 0 us -> 147 us
  other arithmetic: 124 us -> 10.2 us
  local copies, waits for them, and re-layouts: 77 us -> 35.2 us
  starting transfers between devices: 0.21 us -> 17.8 us
  blocking collectives: 15.1 us -> 0 us
  between operations: 14.9 us -> 1.16 us
    psum x5 -> x0, waiting for transfers between devices: 577 us -> none  [the longest x1 470 us: per_device(): hidden_sum = lax.psum(hidden_part, 'x')]
    pallas_call x0 -> x11, Pallas kernels: none -> 147 us  [the longest x4 53.2 us: write_call(): pl.pallas_call(functools.partial(write_kernel, start, aliased), grid_spec...]
    dot_general x27 -> x2, matrix products: 122 us -> 1.23 us  [the longest x1 0.77 us: layer(): proj = jnp.dot(oc, wo, preferred_element_type=F32).astype(BF16)]
    sub x3 -> x0, matrix products: 60.3 us -> none  [attention(): weight = jnp.where(valid_mask, jnp.exp(scores - peak_val), 0.0)]
    select_n x4 -> x1, other arithmetic: 60.2 us -> 1.02 us  [layer(): lo = jnp.where(my == 0, part[:half_tok], part_o)]
    gather x18 -> x1, local copies, waits for them, and re-layouts: 58 us -> 5.01 us  [layer(): x_in = jnp.take(emb_table, tokens.reshape(n_tok), axis=0, mode='clip')]
    another operation x11 -> x2, other arithmetic: 31.2 us -> 0.95 us  [the longest x1 0.6 us: layer(): pick_m, pick_f = (jnp.stack([cx, core]), jnp.stack([1 - cx, core]))]
    dot_general x1 -> x0, other arithmetic: 22.7 us -> none  [attention(): jnp.einsum('bkgs,bskh->bkgh', weight.astype(jnp.bfloat16), val_cache, pre...]
  transfers between devices with their start and end apart: 5 -> 25, of which waited for: 5 -> 7; matrix products, arithmetic and copies ran while one was open for 6% -> 15% of each run, Pallas kernels for 0% -> 44%
where the time goes in v2:
time: 235 us; the launch traced here: 234 us
  Pallas kernels  147 us (63%)
  local copies, waits for them, and re-layouts  35.2 us (15%)
  waiting for transfers between devices  20.9 us (9%)
  starting transfers between devices  17.8 us (8%)
  other arithmetic  10.2 us (4%)
    pallas_call x4, Pallas kernels, write_call(): pl.pallas_call(functools.partial(write_kernel, start, aliased), grid_spec...  53.2 us
    pallas_call x2, Pallas kernels, moe1_call(): pl.pallas_call(moe1_kernel, grid_spec=grid_spec, out_shape=jax.ShapeDtype...  31.8 us
    pallas_call x1, Pallas kernels, attn_call(): pl.pallas_call(attn_kernel, grid_spec=grid_spec, out_shape=jax.ShapeDtype...  26.8 us
    pallas_call x2, Pallas kernels, moe2_call(): pl.pallas_call(moe2_kernel, grid_spec=grid_spec, out_shape=[jax.ShapeDtyp...  21.8 us
    ppermute x7, waiting for transfers between devices, chip_swap(): return lax.ppermute(v, 'x', [(0, 2), (2, 0), (1, 3), (3, 1)])  14.9 us
    dynamic_slice x3, local copies, waits for them, and re-layouts, theirs(): return lax.dynamic_slice_in_dim(w, (1 - core) * 128, 128, axis)  13.6 us
    ppermute x7, starting transfers between devices, chip_swap(): return lax.ppermute(v, 'x', [(0, 2), (2, 0), (1, 3), (3, 1)])  10.5 us
    pallas_call x1, Pallas kernels, qkv_calls(): pl.pallas_call(qkv_a_kernel, grid_spec=pltpu.PrefetchScalarGridSpec(num_s...  6.91 us
  transfers between devices with their start and end apart: 25, of which 7 were waited for; matrix products, arithmetic and copies ran while one was open for 15% of the time, Pallas kernels for 44%

profile of v2, /device:TPU:0, one launch (start us, length us, event | category | flops | bytes accessed | tf_op | source)
XLA Modules:
  0.0 233.8 jit_solution(8645615254021931821)
XLA Ops:
  0.6 1.4 copy.80
  2.4 3.3 %collective-permute-start.6 = (bf16[2,384,256]{2,1,0:T(8,128)(2,1)S(1)}, bf16[2,384,256]{2,1,0:T(8,128)(2,1)}, u32[]{:S(2)}, u32[]{:S(2)}) collective-permute-start(bf16[2,384,256]{2,1,0:T(8,128)(2,1)S(1)} %copy.86.w0), channel_id=1, source_target_pairs={{0,2},{2,0},{1,3},{3,1},{4,6},{6,4},{5,7},{7,5}} | collective-permute-start | bytes 1179656 | tf_op jit(solution)/shard_map/ppermute | solution.py:359
  6.6 5.0 %gather_fusion = bf16[768,384]{1,0:T(8,128)(2,1)S(1)} fusion(bf16[49155,384]{1,0:T(8,128)(2,1)} %param.19, s32[1024]{0:T(1024)S(1)} %pad_clamp_fusion), kind=kCustom, calls=%fused_computation | custom fusion | bytes 1182720 | tf_op jit(solution)/shard_map/jit(_take)/gather | solution.py:383
  11.8 2.0 collective-permute-start.2
  13.8 4.5 %constant_dynamic-slice_fusion.2 = bf16[40,384,128]{2,1,0:T(8,128)(2,1)} fusion(bf16[40,384,256]{2,1,0:T(8,128)(2,1)} %a0.3, s32[]{:T(128)S(6)} %select_n.64), kind=kLoop, calls=%fused_computation.53 | loop fusion | bytes 7864324 | tf_op jit(solution)/shard_map/dynamic_slice | solution.py:394
  18.3 4.5 %constant_dynamic-slice_fusion.1 = bf16[40,384,128]{2,1,0:T(8,128)(2,1)} fusion(bf16[40,384,256]{2,1,0:T(8,128)(2,1)} %l0.3, s32[]{:T(128)S(6)} %select_n.64), kind=kLoop, calls=%fused_computation.52 | loop fusion | bytes 7864324 | tf_op jit(solution)/shard_map/dynamic_slice | solution.py:394
  22.8 11.3 %collective-permute-done.2 = bf16[400,384]{1,0:T(8,128)(2,1)S(1)} collective-permute-done((bf16[400,384]{1,0:T(8,128)(2,1)S(1)}, bf16[400,384]{1,0:T(8,128)(2,1)S(1)}, u32[]{:S(2)}, u32[]{:S(2)}) %collective-permute-start.2) | collective-permute-done | bytes 307232 | tf_op jit(solution)/shard_map/ppermute | solution.py:359
  34.1 1.8 collective-permute-start.3
  35.9 4.7 %constant_dynamic-slice_fusion = bf16[40,128,384]{2,1,0:T(8,128)(2,1)} fusion(bf16[40,256,384]{2,1,0:T(8,128)(2,1)} %wa.3, s32[]{:T(128)S(6)} %select_n.64), kind=kLoop, calls=%fused_computation.51 | loop fusion | bytes 7864324 | tf_op jit(solution)/shard_map/dynamic_slice | solution.py:394
  41.1 0.9 copy.82
  42.1 1.9 broadcast_in_dim.58.ch_ref
  44.4 1.0 broadcast_select_fusion.1
  46.6 0.9 copy.88.sin_ref
  47.6 0.9 copy.87.cos_ref
  48.5 0.9 copy-done.7
  49.4 6.9 %qkv_a.1 = (bf16[4,768,384]{2,1,0:T(8,128)(2,1)}, bf16[5,768,256]{2,1,0:T(8,128)(2,1)}) custom-call(s32[1]{0:T(128)} %bitcast.14.me_ref, bf16[784,384]{1,0:T(8,128)(2,1)} %copy-done.3, bf16[784,384]{1,0:T(8,128)(2,1)} %copy-done.7, bf16[784,384]{1,0:T(8,128)(2,1)} %copy-done.2, bf16[784,384]{1,0:T(8,128)(2,1)} %collective-permute-done.4.x3, ...), custom_call_target="tpu_custom_call" | custom-call | flops 1207959552 | bytes 6000000 | tf_op jit(solution)/shard_map/qkv_a/pallas_call | solution.py:95
  56.3 6.8 %qkv_b.1 = bf16[5,768,256]{2,1,0:T(8,128)(2,1)} custom-call(s32[1]{0:T(128)} %bitcast.14.me_ref, bf16[4,768,384]{2,1,0:T(8,128)(2,1)} %get-tuple-element.59.hs, bf16[3,384,256]{2,1,0:T(8,128)(2,1)} %copy-done.4, bf16[3,384,256]{2,1,0:T(8,128)(2,1)} %collective-permute-done.8.w1, ...), custom_call_target="tpu_custom_call", output_to_operand_aliasing={{}: (8, {})} | custom-call | flops 1811939328 | bytes 6000000 | tf_op jit(solution)/shard_map/qkv_b/pallas_call | solution.py:109
  63.1 2.7 %copy.91 = bf16[256,15,256]{2,1,0:T(8,128)(2,1)S(1)} copy(bf16[256,15,256]{2,0,1:T(8,128)(2,1)} %bitcast.63) | data formatting | bytes 3932160 | tf_op jit(solution)/shard_map/reshape | solution.py:424
  65.8 1.6 pad.4.a_ref
  67.4 26.8 %attn.1 = bf16[128,16,256]{2,1,0:T(8,128)(2,1)} custom-call(s32[1]{0:T(128)} %bitcast.13.off_ref, s32[256]{0:T(256)} %len_ref.9, bf16[256,16,256]{2,1,0:T(8,128)(2,1)} %pad.4.a_ref, bf16[65536,256]{1,0:T(8,128)(2,1)} %bitcast.51, bf16[65536,256]{1,0:T(8,128)(2,1)} %bitcast.56), custom_call_target="tpu_custom_call" | custom-call | flops 15360000000 | bytes 33554432 | tf_op jit(solution)/shard_map/attn/pallas_call | solution.py:178
  94.2 1.4 copy.92
  96.2 1.5 collective-permute-done.10
  97.9 1.0 copy.94
  99.2 0.8 copy-done.9
  100.0 0.8 convolution_convert_fusion
  101.1 13.4 %write.4 = (bf16[65536,256]{1,0:T(8,128)(2,1)}, bf16[65536,256]{1,0:T(8,128)(2,1)}) custom-call(s32[256]{0:T(256)} %len_ref.9, bf16[256,16,256]{2,1,0:T(8,128)(2,1)} %pad.4.a_ref, bf16[65536,256]{1,0:T(8,128)(2,1)} %bitcast.52, bf16[65536,256]{1,0:T(8,128)(2,1)} %bitcast.57), custom_call_target="tpu_custom_call" | custom-call | flops 11520000000 | bytes 33554432 | tf_op jit(solution)/shard_map/write/pallas_call | solution.py:220
  114.5 1.7 collective-permute-done.11
  117.1 1.5 collective-permute-done.12
  118.8 1.5 collective-permute-start.13
  120.3 0.7 fusion.15
  121.0 1.4 collective-permute-done.13
  123.2 1.5 collective-permute-start.18
  124.8 1.1 pad_maximum_fusion.h_ref
  125.9 2.3 collective-permute-done.18
  128.5 15.9 %moe1.2 = bf16[8,384,256]{2,1,0:T(8,128)(2,1)} custom-call(s32[2]{0:T(128)} %get-tuple-element.69.half_ref, bf16[768,768]{1,0:T(8,128)(2,1)} %pad_maximum_fusion.h_ref, bf16[8,768,128]{2,1,0:T(8,128)(2,1)} %broadcast_in_dim.58.ch_ref, bf16[40,384,256]{2,1,0:T(8,128)(2,1)} %a0.3, bf16[40,384,256]{2,1,0:T(8,128)(2,1)} %l0.3, ...), custom_call_target="tpu_custom_call" | custom-call | flops 6039797760 | bytes 20000000 | tf_op jit(solution)/shard_map/moe1/pallas_call | solution.py:277
  144.3 1.5 collective-permute-start.16
  145.8 15.9 %moe1.3 = bf16[8,384,256]{2,1,0:T(8,128)(2,1)} custom-call(s32[2]{0:T(128)} %get-tuple-element.68.half_ref, bf16[768,768]{1,0:T(8,128)(2,1)} %pad_maximum_fusion.h_ref, bf16[8,768,128]{2,1,0:T(8,128)(2,1)} %broadcast_in_dim.58.ch_ref, bf16[40,384,256]{2,1,0:T(8,128)(2,1)} %a0.3, bf16[40,384,256]{2,1,0:T(8,128)(2,1)} %l0.3, ...), custom_call_target="tpu_custom_call" | custom-call | flops 6039797760 | bytes 20000000 | tf_op jit(solution)/shard_map/moe1/pallas_call | solution.py:277
  161.8 19.5 %write.5 = (bf16[65536,256]{1,0:T(8,128)(2,1)}, bf16[65536,256]{1,0:T(8,128)(2,1)}) custom-call(s32[256]{0:T(256)} %len_ref.9, bf16[256,16,256]{2,1,0:T(8,128)(2,1)} %pad.4.a_ref, bf16[65536,256]{1,0:T(8,128)(2,1)} %bitcast.53, bf16[65536,256]{1,0:T(8,128)(2,1)} %bitcast.58, ...), custom_call_target="tpu_custom_call", output_to_operand_aliasing={{0}: (4, {}), {1}: (5, {})} | custom-call | flops 17280000000 | bytes 50331648 | tf_op jit(solution)/shard_map/write/pallas_call | solution.py:220
  181.2 1.7 convert_add_fusion
  184.5 10.7 %moe2.2 = (f32[384,384]{1,0:T(8,128)}, bf16[384,384]{1,0:T(8,128)(2,1)}) custom-call(s32[2]{0:T(128)} %get-tuple-element.68.half_ref, bf16[8,384,128]{2,1,0:T(8,128)(2,1)} %copy-done.1, bf16[8,768,128]{2,1,0:T(8,128)(2,1)} %broadcast_in_dim.58.ch_ref, bf16[40,256,384]{2,1,0:T(8,128)(2,1)} %wa.3, bf16[40,128,384]{2,1,0:T(8,128)(2,1)} %collective-permute-done.19.wb), custom_call_target="tpu_custom_call" | custom-call | flops 3019898880 | bytes 10000000 | tf_op jit(solution)/shard_map/moe2/pallas_call | solution.py:340
  195.2 7.1 %write.6 = (bf16[65536,256]{1,0:T(8,128)(2,1)}, bf16[65536,256]{1,0:T(8,128)(2,1)}) custom-call(s32[256]{0:T(256)} %len_ref.9, bf16[256,16,256]{2,1,0:T(8,128)(2,1)} %pad.4.a_ref, bf16[65536,256]{1,0:T(8,128)(2,1)} %bitcast.54, bf16[65536,256]{1,0:T(8,128)(2,1)} %bitcast.59, ...), custom_call_target="tpu_custom_call", output_to_operand_aliasing={{0}: (4, {}), {1}: (5, {})} | custom-call | flops 5760000000 | bytes 16777216 | tf_op jit(solution)/shard_map/write/pallas_call | solution.py:220
  202.3 0.9 copy-done.6
  203.2 11.1 %moe2.3 = (f32[384,384]{1,0:T(8,128)}, bf16[384,384]{1,0:T(8,128)(2,1)}) custom-call(s32[2]{0:T(128)} %get-tuple-element.69.half_ref, bf16[8,384,128]{2,1,0:T(8,128)(2,1)} %copy-done.6, bf16[8,768,128]{2,1,0:T(8,128)(2,1)} %broadcast_in_dim.58.ch_ref, bf16[40,256,384]{2,1,0:T(8,128)(2,1)} %wa.3, bf16[40,128,384]{2,1,0:T(8,128)(2,1)} %collective-permute-done.19.wb), custom_call_target="tpu_custom_call" | custom-call | flops 3019898880 | bytes 10000000 | tf_op jit(solution)/shard_map/moe2/pallas_call | solution.py:340
  214.8 1.3 collective-permute-done.23
  216.1 1.1 add_convert_fusion.1
  217.8 1.5 collective-permute-start.22
  219.4 13.2 %write.7 = (bf16[65536,256]{1,0:T(8,128)(2,1)}, bf16[65536,256]{1,0:T(8,128)(2,1)}) custom-call(s32[256]{0:T(256)} %len_ref.9, bf16[256,16,256]{2,1,0:T(8,128)(2,1)} %pad.4.a_ref, bf16[65536,256]{1,0:T(8,128)(2,1)} %bitcast.55, bf16[65536,256]{1,0:T(8,128)(2,1)} %bitcast.60, ...), custom_call_target="tpu_custom_call", output_to_operand_aliasing={{0}: (4, {}), {1}: (5, {})} | custom-call | flops 11520000000 | bytes 33554432 | tf_op jit(solution)/shard_map/write/pallas_call | solution.py:220
  232.7 1.0 fusion.7
  (118 shorter events, 9.9 us)
Async XLA Ops:
  2.0 3.9 %copy-start.11 = (bf16[384,256]{1,0:T(8,128)(2,1)S(1)}, bf16[384,256]{1,0:T(8,128)(2,1)}, u32[]{:S(2)}) copy-start(bf16[384,256]{1,0:T(8,128)(2,1)} %param.25) | copy-start | bytes 589828
  2.0 3.9 %copy-start.12 = (bf16[384,256]{1,0:T(8,128)(2,1)S(1)}, bf16[384,256]{1,0:T(8,128)(2,1)}, u32[]{:S(2)}) copy-start(bf16[384,256]{1,0:T(8,128)(2,1)} %param.24) | copy-start | bytes 589828
  2.1 4.4 %copy-start.17 = (bf16[384]{0:T(512)(128)(2,1)S(1)}, bf16[384]{0:T(512)(128)(2,1)}, u32[]{:S(2)}) copy-start(bf16[384]{0:T(512)(128)(2,1)} %param.22) | copy-start | bytes 2308
  2.1 4.4 %copy-start.15 = (bf16[384]{0:T(512)(128)(2,1)S(1)}, bf16[384]{0:T(512)(128)(2,1)}, u32[]{:S(2)}) copy-start(bf16[384]{0:T(512)(128)(2,1)} %param.27) | copy-start | bytes 2308
  2.1 4.4 %copy-start.16 = (s32[3,256]{1,0:T(4,128)S(1)}, s32[3,256]{1,0:T(4,128)}, u32[]{:S(2)}) copy-start(s32[3,256]{1,0:T(4,128)} %param.16) | copy-start | bytes 9220
  2.3 9.3 %copy-start.5 = (bf16[2,384,256]{2,1,0:T(8,128)(2,1)}, bf16[2,384,256]{2,1,0:T(8,128)(2,1)S(1)}, u32[]{:S(2)}) copy-start(bf16[2,384,256]{2,1,0:T(8,128)(2,1)S(1)} %copy.86.w0) | copy-start | bytes 1179652
  2.4 43.2 %collective-permute-start.6 = (bf16[2,384,256]{2,1,0:T(8,128)(2,1)S(1)}, bf16[2,384,256]{2,1,0:T(8,128)(2,1)}, u32[]{:S(2)}, u32[]{:S(2)}) collective-permute-start(bf16[2,384,256]{2,1,0:T(8,128)(2,1)S(1)} %copy.86.w0), channel_id=1, source_target_pairs={{0,2},{2,0},{1,3},{3,1},{4,6},{6,4},{5,7},{7,5}} | collective-permute-start | bytes 1179656 | tf_op jit(solution)/shard_map/ppermute | solution.py:359
  5.7 39.9 %collective-permute-start.5 = (bf16[2,384,256]{2,1,0:T(8,128)(2,1)S(1)}, bf16[2,384,256]{2,1,0:T(8,128)(2,1)}, u32[]{:S(2)}, u32[]{:S(2)}) collective-permute-start(bf16[2,384,256]{2,1,0:T(8,128)(2,1)S(1)} %copy.86.w0), channel_id=1, source_target_pairs={{0,1},{1,0},{2,3},{3,2},{4,5},{5,4},{6,7},{7,6}} | collective-permute-start | bytes 1179656 | tf_op jit(solution)/shard_map/ppermute | solution.py:356
  6.0 5.7 %copy-start.4 = (bf16[3,384,256]{2,1,0:T(8,128)(2,1)}, bf16[3,384,256]{2,1,0:T(8,128)(2,1)S(1)}, u32[]{:S(2)}) copy-start(bf16[3,384,256]{2,1,0:T(8,128)(2,1)S(1)} %pad_maximum_fusion.3.w0) | copy-start | bytes 1769476
  6.0 50.3 %collective-permute-start.8 = (bf16[3,384,256]{2,1,0:T(8,128)(2,1)S(1)}, bf16[3,384,256]{2,1,0:T(8,128)(2,1)}, u32[]{:S(2)}, u32[]{:S(2)}) collective-permute-start(bf16[3,384,256]{2,1,0:T(8,128)(2,1)S(1)} %pad_maximum_fusion.3.w0), channel_id=1, source_target_pairs={{0,1},{1,0},{2,3},{3,2},{4,5},{5,4},{6,7},{7,6}} | collective-permute-start | bytes 1769480 | tf_op jit(solution)/shard_map/ppermute | solution.py:356
  6.5 35.5 %collective-permute-start = (bf16[3,384,256]{2,1,0:T(8,128)(2,1)S(1)}, bf16[3,384,256]{2,1,0:T(8,128)(2,1)}, u32[]{:S(2)}, u32[]{:S(2)}) collective-permute-start(bf16[3,384,256]{2,1,0:T(8,128)(2,1)S(1)} %pad_maximum_fusion.3.w0), channel_id=1, source_target_pairs={{0,2},{2,0},{1,3},{3,1},{4,6},{6,4},{5,7},{7,5}} | collective-permute-start | bytes 1769480 | tf_op jit(solution)/shard_map/ppermute | solution.py:359
  11.8 30.2 %copy-start.3 = (bf16[784,384]{1,0:T(8,128)(2,1)}, bf16[784,384]{1,0:T(8,128)(2,1)S(1)}, u32[]{:S(2)}) copy-start(bf16[784,384]{1,0:T(8,128)(2,1)S(1)} %pad_maximum_fusion.1.x0) | copy-start | bytes 1806340
  11.8 22.2 %collective-permute-start.2 = (bf16[400,384]{1,0:T(8,128)(2,1)S(1)}, bf16[400,384]{1,0:T(8,128)(2,1)S(1)}, u32[]{:S(2)}, u32[]{:S(2)}) collective-permute-start(bf16[400,384]{1,0:T(8,128)(2,1)S(1)} %pad_maximum_fusion.4), channel_id=1, source_target_pairs={{0,2},{2,0},{1,3},{3,1},{4,6},{6,4},{5,7},{7,5}} | collective-permute-start | bytes 921608 | tf_op jit(solution)/shard_map/ppermute | solution.py:359
  18.3 4.5 %copy-start.13 = (s32[3,256,8]{1,2,0:T(8,128)S(1)}, s32[3,256,8]{1,2,0:T(8,128)}, u32[]{:S(2)}) copy-start(s32[3,256,8]{1,2,0:T(8,128)} %param.18) | copy-start | bytes 73732
  34.1 7.1 %copy-start.8 = (bf16[768,384]{1,0:T(8,128)(2,1)S(1)}, bf16[768,384]{1,0:T(8,128)(2,1)}, u32[]{:S(2)}) copy-start(bf16[768,384]{1,0:T(8,128)(2,1)} %param.26) | copy-start | bytes 1769476
  34.1 9.9 %collective-permute-start.3 = (bf16[384,384]{1,0:T(8,128)(2,1)S(1)}, bf16[384,384]{1,0:T(8,128)(2,1)}, u32[]{:S(2)}, u32[]{:S(2)}) collective-permute-start(bf16[384,384]{1,0:T(8,128)(2,1)S(1)} %slice.34), channel_id=1, source_target_pairs={{0,4},{4,0},{1,5},{5,1},{2,6},{6,2},{3,7},{7,3}} | collective-permute-start | bytes 884744 | tf_op jit(solution)/shard_map/ppermute | solution.py:362
  42.0 6.5 %collective-permute-start.1 = (bf16[784,384]{1,0:T(8,128)(2,1)S(1)}, bf16[784,384]{1,0:T(8,128)(2,1)S(1)}, u32[]{:S(2)}, u32[]{:S(2)}) collective-permute-start(bf16[784,384]{1,0:T(8,128)(2,1)S(1)} %pad_maximum_fusion.1.x0), channel_id=1, source_target_pairs={{0,1},{1,0},{2,3},{3,2},{4,5},{5,4},{6,7},{7,6}} | collective-permute-start | bytes 1806344 | tf_op jit(solution)/shard_map/ppermute | solution.py:356
  43.9 1.7 copy-start.14
  43.9 12.4 %collective-permute-start.9 = (bf16[3,384,256]{2,1,0:T(8,128)(2,1)}, bf16[3,384,256]{2,1,0:T(8,128)(2,1)}, u32[]{:S(2)}, u32[]{:S(2)}) collective-permute-start(bf16[3,384,256]{2,1,0:T(8,128)(2,1)} %collective-permute-done.w2), channel_id=1, source_target_pairs={{0,1},{1,0},{2,3},{3,2},{4,5},{5,4},{6,7},{7,6}} | collective-permute-start | bytes 1769480 | tf_op jit(solution)/shard_map/ppermute | solution.py:356
  45.5 3.0 %copy-start.2 = (bf16[784,384]{1,0:T(8,128)(2,1)}, bf16[784,384]{1,0:T(8,128)(2,1)S(1)}, u32[]{:S(2)}) copy-start(bf16[784,384]{1,0:T(8,128)(2,1)S(1)} %pad_maximum_fusion.2.x2) | copy-start | bytes 1806340
  45.5 3.0 %collective-permute-start.4 = (bf16[784,384]{1,0:T(8,128)(2,1)S(1)}, bf16[784,384]{1,0:T(8,128)(2,1)}, u32[]{:S(2)}, u32[]{:S(2)}) collective-permute-start(bf16[784,384]{1,0:T(8,128)(2,1)S(1)} %pad_maximum_fusion.2.x2), channel_id=1, source_target_pairs={{0,1},{1,0},{2,3},{3,2},{4,5},{5,4},{6,7},{7,6}} | collective-permute-start | bytes 1806344 | tf_op jit(solution)/shard_map/ppermute | solution.py:356
  45.6 2.9 %collective-permute-start.7 = (bf16[2,384,256]{2,1,0:T(8,128)(2,1)}, bf16[2,384,256]{2,1,0:T(8,128)(2,1)}, u32[]{:S(2)}, u32[]{:S(2)}) collective-permute-start(bf16[2,384,256]{2,1,0:T(8,128)(2,1)} %collective-permute-done.6.w2), channel_id=1, source_target_pairs={{0,1},{1,0},{2,3},{3,2},{4,5},{5,4},{6,7},{7,6}} | collective-permute-start | bytes 1179656 | tf_op jit(solution)/shard_map/ppermute | solution.py:356
  48.5 0.9 copy-start.7
  95.6 2.0 collective-permute-start.10
  95.7 32.8 %collective-permute-start.14 = (bf16[40,384,128]{2,1,0:T(8,128)(2,1)}, bf16[40,384,128]{2,1,0:T(8,128)(2,1)}, u32[]{:S(2)}, u32[]{:S(2)}) collective-permute-start(bf16[40,384,128]{2,1,0:T(8,128)(2,1)} %constant_dynamic-slice_fusion.2), channel_id=1, source_target_pairs={{0,1},{1,0},{2,3},{3,2},{4,5},{5,4},{6,7},{7,6}} | collective-permute-start | bytes 11796488 | tf_op jit(solution)/shard_map/ppermute | solution.py:356
  96.1 32.3 %collective-permute-start.15 = (bf16[40,384,128]{2,1,0:T(8,128)(2,1)}, bf16[40,384,128]{2,1,0:T(8,128)(2,1)}, u32[]{:S(2)}, u32[]{:S(2)}) collective-permute-start(bf16[40,384,128]{2,1,0:T(8,128)(2,1)} %constant_dynamic-slice_fusion.1), channel_id=1, source_target_pairs={{0,1},{1,0},{2,3},{3,2},{4,5},{5,4},{6,7},{7,6}} | collective-permute-start | bytes 11796488 | tf_op jit(solution)/shard_map/ppermute | solution.py:356
  99.0 1.1 copy-start.9
  100.8 15.4 %collective-permute-start.11 = (bf16[768,384]{1,0:T(8,128)(2,1)S(1)}, bf16[768,384]{1,0:T(8,128)(2,1)S(1)}, u32[]{:S(2)}, u32[]{:S(2)}) collective-permute-start(bf16[768,384]{1,0:T(8,128)(2,1)S(1)} %convolution_convert_fusion), channel_id=1, source_target_pairs={{0,4},{4,0},{1,5},{5,1},{2,6},{6,2},{3,7},{7,3}} | collective-permute-start | bytes 1769480 | tf_op jit(solution)/shard_map/ppermute | solution.py:362
  114.5 2.1 copy-start.19
  116.6 2.0 collective-permute-start.12
  116.6 6.2 %collective-permute-start.17 = (bf16[384,40]{0,1:T(8,128)(2,1)S(1)}, bf16[384,40]{0,1:T(8,128)(2,1)S(1)}, u32[]{:S(2)}, u32[]{:S(2)}) collective-permute-start(bf16[384,40]{0,1:T(8,128)(2,1)S(1)} %copy-done.19), channel_id=1, source_target_pairs={{0,1},{1,0},{2,3},{3,2},{4,5},{5,4},{6,7},{7,6}} | collective-permute-start | bytes 92168 | tf_op jit(solution)/shard_map/ppermute | solution.py:356
  118.8 3.6 %collective-permute-start.13 = (f32[768]{0:T(1024)S(1)}, f32[768]{0:T(1024)S(1)}, u32[]{:S(2)}, u32[]{:S(2)}) collective-permute-start(f32[768]{0:T(1024)S(1)} %add.89), channel_id=1, source_target_pairs={{0,2},{2,0},{1,3},{3,1},{4,6},{6,4},{5,7},{7,5}} | collective-permute-start | bytes 9224 | tf_op jit(solution)/shard_map/ppermute | solution.py:359
  121.0 63.1 %collective-permute-start.19 = (bf16[40,128,384]{2,1,0:T(8,128)(2,1)}, bf16[40,128,384]{2,1,0:T(8,128)(2,1)}, u32[]{:S(2)}, u32[]{:S(2)}) collective-permute-start(bf16[40,128,384]{2,1,0:T(8,128)(2,1)} %constant_dynamic-slice_fusion), channel_id=1, source_target_pairs={{0,1},{1,0},{2,3},{3,2},{4,5},{5,4},{6,7},{7,6}} | collective-permute-start | bytes 11796488 | tf_op jit(solution)/shard_map/ppermute | solution.py:356
  123.2 4.9 %collective-permute-start.18 = (f32[768,40]{0,1:T(8,128)S(1)}, f32[768,40]{0,1:T(8,128)S(1)}, u32[]{:S(2)}, u32[]{:S(2)}) collective-permute-start(f32[768,40]{0,1:T(8,128)S(1)} %fusion.9), channel_id=1, source_target_pairs={{0,2},{2,0},{1,3},{3,1},{4,6},{6,4},{5,7},{7,5}} | collective-permute-start | bytes 368648 | tf_op jit(solution)/shard_map/ppermute | solution.py:359
  144.3 36.9 %collective-permute-start.16 = (bf16[8,384,256]{2,1,0:T(8,128)(2,1)}, bf16[8,384,256]{2,1,0:T(8,128)(2,1)}, u32[]{:S(2)}, u32[]{:S(2)}) collective-permute-start(bf16[8,384,256]{2,1,0:T(8,128)(2,1)} %moe1.2), channel_id=1, source_target_pairs={{0,2},{2,0},{1,3},{3,1},{4,6},{6,4},{5,7},{7,5}} | collective-permute-start | bytes 4718600 | tf_op jit(solution)/shard_map/ppermute | solution.py:359
  161.8 19.5 %copy-start = (bf16[8,384,256]{2,1,0:T(8,128)(2,1)S(1)}, bf16[8,384,256]{2,1,0:T(8,128)(2,1)}, u32[]{:S(2)}) copy-start(bf16[8,384,256]{2,1,0:T(8,128)(2,1)} %moe1.3) | copy-start | bytes 4718596
  183.6 0.9 copy-start.1
  183.6 18.7 %collective-permute-start.20 = (bf16[8,384,128]{2,1,0:T(8,128)(2,1)S(1)}, bf16[8,384,128]{2,1,0:T(8,128)(2,1)S(1)}, u32[]{:S(2)}, u32[]{:S(2)}) collective-permute-start(bf16[8,384,128]{2,1,0:T(8,128)(2,1)S(1)} %fusion.u_ref), channel_id=1, source_target_pairs={{0,2},{2,0},{1,3},{3,1},{4,6},{6,4},{5,7},{7,5}} | collective-permute-start | bytes 2359304 | tf_op jit(solution)/shard_map/ppermute | solution.py:359
  202.3 0.9 copy-start.6
  203.2 11.1 %copy-start.18 = (bf16[384,384]{1,0:T(8,128)(2,1)S(1)}, bf16[384,384]{1,0:T(8,128)(2,1)}, u32[]{:S(2)}) copy-start(bf16[384,384]{1,0:T(8,128)(2,1)} %get-tuple-element.91) | copy-start | bytes 884740
  214.3 3.5 %copy-start.10 = (f32[384,384]{1,0:T(8,128)S(1)}, f32[384,384]{1,0:T(8,128)}, u32[]{:S(2)}) copy-start(f32[384,384]{1,0:T(8,128)} %get-tuple-element.84) | copy-start | bytes 1769476
  214.3 1.8 collective-permute-start.23
  214.3 3.4 %collective-permute-start.21 = (bf16[384,384]{1,0:T(8,128)(2,1)S(1)}, bf16[384,384]{1,0:T(8,128)(2,1)S(1)}, u32[]{:S(2)}, u32[]{:S(2)}) collective-permute-start(bf16[384,384]{1,0:T(8,128)(2,1)S(1)} %copy-done.18), channel_id=1, source_target_pairs={{0,1},{1,0},{2,3},{3,2},{4,5},{5,4},{6,7},{7,6}} | collective-permute-start | bytes 884744 | tf_op jit(solution)/shard_map/ppermute | solution.py:356
  217.2 15.4 %collective-permute-start.24 = (bf16[384,384]{1,0:T(8,128)(2,1)S(1)}, bf16[384,384]{1,0:T(8,128)(2,1)S(1)}, u32[]{:S(2)}, u32[]{:S(2)}) collective-permute-start(bf16[384,384]{1,0:T(8,128)(2,1)S(1)} %add_convert_fusion.1), channel_id=1, source_target_pairs={{0,4},{4,0},{1,5},{5,1},{2,6},{6,2},{3,7},{7,3}} | collective-permute-start | bytes 884744 | tf_op jit(solution)/shard_map/ppermute | solution.py:362
  217.8 14.8 %collective-permute-start.22 = (bf16[384,384]{1,0:T(8,128)(2,1)S(1)}, bf16[384,384]{1,0:T(8,128)(2,1)S(1)}, u32[]{:S(2)}, u32[]{:S(2)}) collective-permute-start(bf16[384,384]{1,0:T(8,128)(2,1)S(1)} %add_convert_fusion.2), channel_id=1, source_target_pairs={{0,4},{4,0},{1,5},{5,1},{2,6},{6,2},{3,7},{7,3}} | collective-permute-start | bytes 884744 | tf_op jit(solution)/shard_map/ppermute | solution.py:362

commit v3 on v2

--- a/solution.py
+++ b/solution.py
@@ -13,6 +13,8 @@
 F32 = jnp.float32
 BF16 = jnp.bfloat16
 VMEM_LIMIT = 60 * 1024 * 1024
+LANE = 128
+WIDE = 256
 NB = 8
 
 
@@ -31,7 +33,8 @@
 def norm_into(me, refs, tokens, hs):
     place = [me, me + 1 - 2 * (me % 2), (me + 2) % 4]
     place.append((place[1] + 2) % 4)
-    rt = 128
+    rt = LANE
+    width = refs[0].shape[1]
     gains = [r[tokens : tokens + 1, :].astype(F32) for r in refs]
 
     def body(i, carry):
@@ -43,7 +46,7 @@
         total = (sq[0] + sq[1]) + (sq[2] + sq[3])
         scale = lax.rsqrt(total / (4.0 * refs[0].shape[1]) + EPS)
         for n, r in enumerate(refs):
-            hs[place[n], rows, :] = (r[rows, :].astype(F32) * scale * gains[n]).astype(BF16)
+            hs[rows, pl.ds(pl.multiple_of(place[n] * width, LANE), width)] = (r[rows, :].astype(F32) * scale * gains[n]).astype(BF16)
         return carry
 
     lax.fori_loop(0, tokens // rt, body, 0)
@@ -53,14 +56,12 @@
     place = [me, me + 1 - 2 * (me % 2), (me + 2) % 4]
     place.append((place[1] + 2) % 4)
     for n, ref in enumerate(refs):
-        ws[place[n]] = ref[0]
-    low = lax.broadcasted_iota(jnp.int32, (1, 256), 1) % 64 < 32
-    mt = 256
-    for m in range(hs.shape[1] // mt):
+        ws[pl.ds(pl.multiple_of(place[n] * ref.shape[1], LANE), ref.shape[1]), :] = ref[0]
+    low = lax.broadcasted_iota(jnp.int32, (1, WIDE), 1) % 64 < 32
+    mt = hs.shape[0]
+    for m in range(hs.shape[0] // mt):
         rows = slice(m * mt, (m + 1) * mt)
-        acc = jnp.dot(hs[0, rows, :], ws[0], preferred_element_type=F32)
-        for i in range(1, 4):
-            acc += jnp.dot(hs[i, rows, :], ws[i], preferred_element_type=F32)
+        acc = jnp.dot(hs[rows, :], ws[...], preferred_element_type=F32)
         v = acc.astype(BF16).astype(F32)
         other = jnp.where(low, pltpu.roll(v, 224, 1), pltpu.roll(v, 32, 1))
         cos, sin = cos_ref[rows, :], sin_ref[rows, :]
@@ -87,10 +88,10 @@
     tokens = cos.shape[0]
     rows, width = xs[0].shape
     na, nb = was[0].shape[0], wbs[0].shape[0]
-    full = jax.ShapeDtypeStruct((na + nb, tokens, 256), BF16)
-    w_spec = [lead(1, width, 256)] * 4
-    t_spec = [fixed(tokens, 128)] * 2
-    h_spec = fixed(4, tokens, width)
+    full = jax.ShapeDtypeStruct((na + nb, tokens, WIDE), BF16)
+    w_spec = [lead(1, width, WIDE)] * 4
+    t_spec = [fixed(tokens, LANE)] * 2
+    h_spec = fixed(tokens, 4 * width)
     params = pltpu.CompilerParams(vmem_limit_bytes=VMEM_LIMIT, dimension_semantics=("arbitrary",))
     h, first = pl.pallas_call(
         qkv_a_kernel,
@@ -98,10 +99,10 @@
             num_scalar_prefetch=1,
             grid=(na,),
             in_specs=[fixed(rows, width)] * 4 + w_spec + t_spec,
-            out_specs=[h_spec, lead(1, tokens, 256)],
-            scratch_shapes=[pltpu.VMEM((4, width, 256), BF16)],
+            out_specs=[h_spec, lead(1, tokens, WIDE)],
+            scratch_shapes=[pltpu.VMEM((4 * width, WIDE), BF16)],
         ),
-        out_shape=[jax.ShapeDtypeStruct((4, tokens, width), BF16), full],
+        out_shape=[jax.ShapeDtypeStruct((tokens, 4 * width), BF16), full],
         compiler_params=params,
         cost_estimate=cost(2 * tokens * width * 4 * 512, 6_000_000),
         name="qkv_a",
@@ -112,8 +113,8 @@
             num_scalar_prefetch=1,
             grid=(nb,),
             in_specs=[h_spec] + w_spec + t_spec + [pl.BlockSpec(memory_space=pl.ANY)],
-            out_specs=pl.BlockSpec((1, tokens, 256), lambda i, m: (na + i, 0, 0)),
-            scratch_shapes=[pltpu.VMEM((4, width, 256), BF16)],
+            out_specs=pl.BlockSpec((1, tokens, WIDE), lambda i, m: (na + i, 0, 0)),
+            scratch_shapes=[pltpu.VMEM((4 * width, WIDE), BF16)],
         ),
         out_shape=full,
         input_output_aliases={8: 0},
@@ -123,13 +124,25 @@
     )(me, h, *wbs, cos, sin, first)
 
 
-def attn_kernel(off_ref, len_ref, a_ref, k_ref, v_ref, o_ref, lhs_ref, snew_ref, enew_ref):
+def by_sequence(a_ref, rows_ref, turned_ref):
+    kinds, count, _ = a_ref.shape
+    for side in range(2):
+        lanes = slice(side * LANE, side * LANE + LANE)
+        for r in range(kinds):
+            rows_ref[side, r * count : (r + 1) * count, :] = a_ref[r, :, lanes].astype(F32)
+        rows_ref[side, kinds * count :, :] = jnp.zeros((count, LANE), F32)
+        for i in range(count):
+            turned_ref[i * 16 : i * 16 + 16, lanes] = rows_ref[side, pl.ds(i, 16, stride=count), :].astype(turned_ref.dtype)
+
+
+def attn_kernel(off_ref, len_ref, a_ref, k_ref, k2_ref, v_ref, v2_ref, o_ref, lhs_ref, snew_ref, enew_ref, rows_ref, turned_ref):
     base = (off_ref[0] + pl.program_id(0)) * NB
-    slot = lax.broadcasted_iota(jnp.int32, (1, 256), 1)
+    slot = lax.broadcasted_iota(jnp.int32, (1, WIDE), 1)
     block = slot // 64
-    row = lax.broadcasted_iota(jnp.int32, (64, 128), 0) % 16 % 3
-    col = lax.broadcasted_iota(jnp.int32, (64, 128), 1)
-    every = a_ref[...].reshape(NB * 16, 256)
+    row = lax.broadcasted_iota(jnp.int32, (64, LANE), 0) % 16 % 3
+    col = lax.broadcasted_iota(jnp.int32, (64, LANE), 1)
+    by_sequence(a_ref, rows_ref, turned_ref)
+    every = turned_ref[...]
     scaled = every * jnp.bfloat16(0.125)
     for i in range(NB):
         q = scaled[i * 16 : i * 16 + 16]
@@ -140,18 +153,18 @@
     for i in range(NB):
         pos = len_ref[base + i]
         rows = slice(i * 64, i * 64 + 64)
-        s_old = jnp.dot(lhs_ref[rows, :], k_ref[i * 256 : (i + 1) * 256, :], preferred_element_type=F32)
+        s_old = jnp.dot(lhs_ref[rows, :], (k_ref, k2_ref)[i // 4][i % 4 * WIDE : (i % 4 + 1) * WIDE, :], preferred_element_type=F32)
         fresh = (col >= i * 16 + 9) & (col <= row + (i * 16 + 9))
         s_old = jnp.where(slot < pos, s_old, -1.0e30)
         s_new = jnp.where(fresh, snew_ref[rows, :], -1.0e30)
-        peak = jnp.max(jnp.maximum(jnp.maximum(s_old[:, :128], s_old[:, 128:]), s_new), axis=-1, keepdims=True)
+        peak = jnp.max(jnp.maximum(jnp.maximum(s_old[:, :LANE], s_old[:, LANE:]), s_new), axis=-1, keepdims=True)
         e_old = jnp.exp(s_old - peak)
         e_new = jnp.exp(s_new - peak)
         enew_ref[rows, :] = e_new.astype(BF16)
-        total = jnp.sum(e_old[:, :128] + e_old[:, 128:] + e_new, axis=-1, keepdims=True)
-        mixed = lax.dot_general(e_old.astype(BF16), v_ref[i * 256 : (i + 1) * 256, :], (((1,), (1,)), ((), ())), preferred_element_type=F32)
+        total = jnp.sum(e_old[:, :LANE] + e_old[:, LANE:] + e_new, axis=-1, keepdims=True)
+        mixed = lax.dot_general(e_old.astype(BF16), (v_ref, v2_ref)[i // 4][i % 4 * WIDE : (i % 4 + 1) * WIDE, :], (((1,), (1,)), ((), ())), preferred_element_type=F32)
         res = mixed[0:16]
-        tot = jnp.broadcast_to(total[0:16], (16, 256))
+        tot = jnp.broadcast_to(total[0:16], (16, WIDE))
         for k in range(1, 4):
             part = slice(16 * k, 16 * k + 16)
             res = jnp.where(block == k, mixed[part], res)
@@ -168,54 +181,58 @@
 
 
 def attn_call(offset, lengths, acts, k_rows, v_rows, count):
+    even = pl.BlockSpec((NB * LANE, WIDE), lambda i, f, m: (2 * (f[0] + i), 0))
+    odd = pl.BlockSpec((NB * LANE, WIDE), lambda i, f, m: (2 * (f[0] + i) + 1, 0))
     grid_spec = pltpu.PrefetchScalarGridSpec(
         num_scalar_prefetch=2,
         grid=(count // NB,),
-        in_specs=[pl.BlockSpec((NB, 16, 256), lambda i, f, m: (f[0] + i, 0, 0))] + [pl.BlockSpec((NB * 256, 256), lambda i, f, m: (f[0] + i, 0))] * 2,
-        out_specs=lead(NB, 16, 256),
-        scratch_shapes=[pltpu.VMEM((NB * 64, 256), BF16), pltpu.VMEM((NB * 64, 128), F32), pltpu.VMEM((NB * 64, 128), BF16)],
+        in_specs=[pl.BlockSpec((15, NB, WIDE), lambda i, f, m: (0, f[0] + i, 0)), even, odd, even, odd],
+        out_specs=lead(NB, 16, WIDE),
+        scratch_shapes=[pltpu.VMEM((NB * 64, WIDE), BF16), pltpu.VMEM((NB * 64, LANE), F32), pltpu.VMEM((NB * 64, LANE), BF16), pltpu.VMEM((2, NB * 16, LANE), F32), pltpu.VMEM((NB * 16, WIDE), BF16)],
     )
     return pl.pallas_call(
         attn_kernel,
         grid_spec=grid_spec,
-        out_shape=jax.ShapeDtypeStruct((count, 16, 256), BF16),
+        out_shape=jax.ShapeDtypeStruct((count, 16, WIDE), BF16),
         compiler_params=pltpu.CompilerParams(vmem_limit_bytes=VMEM_LIMIT, dimension_semantics=("arbitrary",)),
         cost_estimate=cost(count * 120_000_000, count * 262144),
         name="attn",
-    )(offset, lengths, acts, k_rows, v_rows)
+    )(offset, lengths, acts, k_rows, k_rows, v_rows, v_rows)
 
 
 WB = 16
-PIECES = (64, 96, 32, 64)
+PIECES = (48, 64, 80, 32, 32)
 
 
 def write_kernel(start, aliased, len_ref, a_ref, k_ref, v_ref, *rest):
-    ko_ref, vo_ref = rest[2:] if aliased else rest
+    ko_ref, vo_ref, rows_ref, turned_ref = rest[2:] if aliased else rest
+    by_sequence(a_ref, rows_ref, turned_ref)
     base = start + pl.program_id(0) * WB
-    cols = jnp.transpose(a_ref[...].reshape(WB * 16, 256).astype(F32))
-    slot = lax.broadcasted_iota(jnp.int32, (1, 256), 1)
+    cols = jnp.transpose(turned_ref[...])
+    slot = lax.broadcasted_iota(jnp.int32, (1, WIDE), 1)
     for i in range(WB):
         pos = len_ref[base + i]
-        rows = slice(i * 256, (i + 1) * 256)
+        rows = slice(i * WIDE, (i + 1) * WIDE)
         hit = (slot >= pos) & (slot <= pos + 2)
-        part = cols[:, (i // 8) * 128 : (i // 8) * 128 + 128]
+        part = cols[:, (i // 8) * LANE : (i // 8) * LANE + LANE]
         for first, src, dst in ((9, k_ref, ko_ref), (12, v_ref, vo_ref)):
-            moved = pltpu.roll(part, (pos - (i % 8) * 16 - first + 256) % 128, 1).astype(BF16)
+            moved = pltpu.roll(part, (pos - (i % 8) * 16 - first + WIDE) % LANE, 1).astype(BF16)
             for side in range(2):
-                lanes = slice(side * 128, side * 128 + 128)
+                lanes = slice(side * LANE, side * LANE + LANE)
                 dst[rows, lanes] = jnp.where(hit[:, lanes], moved, src[rows, lanes])
 
 
 def write_call(start, count, lengths, acts, k_rows, v_rows, before):
     s0 = start // WB
-    block = pl.BlockSpec((WB * 256, 256), lambda i, m: (s0 + i, 0))
+    block = pl.BlockSpec((WB * WIDE, WIDE), lambda i, m: (s0 + i, 0))
     aliased = before is not None
     grid_spec = pltpu.PrefetchScalarGridSpec(
         num_scalar_prefetch=1,
         grid=(count // WB,),
-        in_specs=[pl.BlockSpec((WB, 16, 256), lambda i, m: (s0 + i, 0, 0)), block, block]
+        in_specs=[pl.BlockSpec((15, WB, WIDE), lambda i, m: (0, s0 + i, 0)), block, block]
         + ([pl.BlockSpec(memory_space=pl.ANY)] * 2 if aliased else []),
         out_specs=[block, block],
+        scratch_shapes=[pltpu.VMEM((2, WB * 16, LANE), F32), pltpu.VMEM((WB * 16, WIDE), F32)],
     )
     return pl.pallas_call(
         functools.partial(write_kernel, start, aliased),
@@ -255,7 +272,7 @@
                 chj = ch_ref[j, rows, :]
                 hits = [chj == ids[k] for k in range(4)]
                 for side in range(2):
-                    lanes = slice(side * 128, side * 128 + 128)
+                    lanes = slice(side * LANE, side * LANE + LANE)
                     acc = out_ref[j, rows, lanes]
                     for k in range(4):
                         acc = jnp.where(hits[k], d[k][:, lanes], acc)
@@ -265,21 +282,21 @@
 def moe1_call(pick, h2, ch, w_act, w_lin, a1, l1):
     half = h2.shape[0] // 2
     experts, rows, _ = a1.shape
-    mine = pl.BlockSpec((E1, rows, 128), lambda i, m: (i, 0, m[1]))
-    theirs = lead(E1, rows, 128)
+    mine = pl.BlockSpec((E1, rows, LANE), lambda i, m: (i, 0, m[1]))
+    theirs = lead(E1, rows, LANE)
     grid_spec = pltpu.PrefetchScalarGridSpec(
         num_scalar_prefetch=1,
         grid=(experts // E1,),
-        in_specs=[pl.BlockSpec((half, 2 * rows), lambda i, m: (m[0], 0)), pl.BlockSpec((8, half, 128), lambda i, m: (0, m[0], 0)), mine, mine, theirs, theirs],
-        out_specs=fixed(8, half, 256),
-        scratch_shapes=[pltpu.VMEM((E1 // 4, 4, half, 256), BF16)],
+        in_specs=[pl.BlockSpec((half, 2 * rows), lambda i, m: (m[0], 0)), pl.BlockSpec((8, half, LANE), lambda i, m: (0, m[0], 0)), mine, mine, theirs, theirs],
+        out_specs=fixed(8, half, WIDE),
+        scratch_shapes=[pltpu.VMEM((E1 // 4, 4, half, WIDE), BF16)],
     )
     return pl.pallas_call(
         moe1_kernel,
         grid_spec=grid_spec,
-        out_shape=jax.ShapeDtypeStruct((8, half, 256), BF16),
+        out_shape=jax.ShapeDtypeStruct((8, half, WIDE), BF16),
         compiler_params=pltpu.CompilerParams(vmem_limit_bytes=VMEM_LIMIT, dimension_semantics=("arbitrary",)),
-        cost_estimate=cost(2 * half * 2 * rows * 256 * experts, 20_000_000),
+        cost_estimate=cost(2 * half * 2 * rows * WIDE * experts, 20_000_000),
         name="moe1",
     )(pick, h2, ch, w_act, w_lin, a1, l1)
 
@@ -302,14 +319,14 @@
         ids = [(step * E2 + g * 4 + k).astype(F32).astype(BF16) for k in range(4)]
         for i in range(half // rt):
             rows = slice(i * rt, (i + 1) * rt)
-            out = [jnp.zeros((rt, 128), BF16) for _ in range(4)]
+            out = [jnp.zeros((rt, LANE), BF16) for _ in range(4)]
             for j in range(8):
                 chj = ch_ref[j, rows, :]
                 uj = u_ref[j, rows, :]
                 for k in range(4):
                     out[k] = jnp.where(chj == ids[k], uj, out[k])
             for k in range(4):
-                spread[g, rows, k * 128 : (k + 1) * 128] = out[k]
+                spread[g, rows, k * LANE : (k + 1) * LANE] = out[k]
         es = slice(g * 4, g * 4 + 4)
         w = jnp.concatenate([wa[es].reshape(512, width), wb[es].reshape(512, width)], axis=1)
         part = jnp.dot(spread[g], w, preferred_element_type=F32)
@@ -329,8 +346,8 @@
         num_scalar_prefetch=1,
         grid=(experts // E2,),
         in_specs=[
-            fixed(8, half, 128),
-            pl.BlockSpec((8, half, 128), lambda i, m: (0, m[0], 0)),
+            fixed(8, half, LANE),
+            pl.BlockSpec((8, half, LANE), lambda i, m: (0, m[0], 0)),
             pl.BlockSpec((E2, rows, width), lambda i, m: (i, m[1], 0)),
             lead(E2, rows, width),
         ],
@@ -391,7 +408,7 @@
         wb2 = chip_swap(w_b)
 
         def theirs(w, axis):
-            return lax.dynamic_slice_in_dim(w, (1 - core) * 128, 128, axis)
+            return lax.dynamic_slice_in_dim(w, (1 - core) * LANE, LANE, axis)
 
         act_s = theirs(w_act, 2)
         lin_s, down_s = theirs(w_lin, 2), theirs(w_down, 1)
@@ -412,17 +429,16 @@
         cos, sin = jnp.cos(angles), jnp.sin(angles)
         cos2, sin2 = jnp.tile(cos, (1, 4)), jnp.tile(jnp.concatenate([-sin, sin], axis=1), (1, 2))
         choice_rows = choices.reshape(n_tok, 8)
-        ch_rows = jnp.broadcast_to(choice_rows.T.astype(BF16)[:, :, None], (8, n_tok, 128))
+        ch_rows = jnp.broadcast_to(choice_rows.T.astype(BF16)[:, :, None], (8, n_tok, LANE))
         wo = w_o.reshape(kv, group, hd, width).transpose(1, 0, 2, 3).reshape(group * kv * hd, width)
 
         pick_m, pick_f = jnp.stack([cx, core]), jnp.stack([1 - cx, core])
-        offset = (core * (batch // 2) // NB)[None]
+        offset = (me * (batch // 4) // NB)[None]
         wb2, ch_rows, wo, pick_m, pick_f, offset = barrier((wb2, ch_rows, wo, pick_m, pick_f, offset))
         wb3 = core_swap(wb2)
         act1, lin1, down1 = core_swap(act_s), core_swap(lin_s), core_swap(down_s)
         qkv = qkv_calls(me[None], (x_ext, x_mate, x_far, x_far_mate), (w_a, wa1, wa2, wa3), (w_b, wb1, wb2, wb3), cos2, sin2)
-        acts = qkv.reshape(5, steps, batch, 256).transpose(2, 0, 1, 3).reshape(batch, 15, 256)
-        acts = jnp.pad(acts, ((0, 0), (0, 1), (0, 0)))
+        acts = qkv.reshape(5 * steps, batch, WIDE)
         k_rows = k_cache.transpose(0, 2, 3, 1).reshape(batch * kv * hd, slots)
         v_rows = v_cache.transpose(0, 2, 3, 1).reshape(batch * kv * hd, slots)
         starts = [sum(PIECES[:i]) for i in range(len(PIECES))]
@@ -433,15 +449,23 @@
         def back(rows):
             return rows.reshape(batch, kv, hd, slots).transpose(0, 3, 1, 2)
 
-        o = attn_call(offset, lengths, acts, k_rows, v_rows, batch // 2)[:, : steps * group]
-        o_mate = core_swap(o)
-        o = jnp.where(core == 0, jnp.concatenate([o, o_mate]), jnp.concatenate([o_mate, o]))
-        oc = o.reshape(batch, group, steps, 256).transpose(2, 0, 1, 3).reshape(n_tok, group * 256)
+        o = attn_call(offset, lengths, acts, k_rows, v_rows, batch // 4)[:, : steps * group]
+        o, acts = barrier((o, acts))
+        o_far = chip_swap(o)
+        caches = write(0, acts, None)
+        o_far, caches = barrier((o_far, caches))
+
+        def in_order(v, mate):
+            return jnp.where(core == 0, jnp.concatenate([v, mate]), jnp.concatenate([mate, v]))
+
+        near, far = in_order(o, core_swap(o)), in_order(o_far, core_swap(o_far))
+        o = jnp.where(cx == 0, jnp.concatenate([near, far]), jnp.concatenate([far, near]))
+        oc = o.reshape(batch, group, steps, WIDE).transpose(2, 0, 1, 3).reshape(n_tok, group * WIDE)
         proj = jnp.dot(oc, wo, preferred_element_type=F32).astype(BF16)
 
         proj, acts = barrier((proj, acts))
         proj_y = y_swap(proj)
-        caches = write(0, acts, None)
+        caches = write(1, acts, caches)
         proj_y, caches = barrier((proj_y, caches))
 
         x1 = (x_in.astype(F32) + (proj.astype(F32) + proj_y.astype(F32))).astype(BF16)
@@ -458,27 +482,27 @@
         send, h2, acts = barrier((send, h2, acts))
         got = chip_swap(send)
         keep = moe1_call(pick_m, h2, ch_rows, w_act, w_lin, act1, lin1)
-        caches = write(1, acts, caches)
+        caches = write(2, acts, caches)
         logits = logits + chip_swap(logits)
         picked = jnp.sum(jnp.where(choice_rows[:, :, None] == jnp.arange(experts)[None, None, :], logits[:, None, :], 0.0), axis=-1)
         gate = jax.nn.softmax(picked, axis=-1)
         gate_mine = lax.dynamic_slice_in_dim(gate, cx * half_tok, half_tok, 0).T
         got, caches, gate_mine = barrier((got, caches, gate_mine))
         hid = keep.astype(F32) + got.astype(F32)
-        u = (gate_mine[:, :, None] * jax.nn.silu(hid[..., :128]) * hid[..., 128:]).astype(BF16)
+        u = (gate_mine[:, :, None] * jax.nn.silu(hid[..., :LANE]) * hid[..., LANE:]).astype(BF16)
 
         u, acts = barrier((u, acts))
         u_far = chip_swap(u)
         own_m, snd_m = moe2_call(pick_m, u, ch_rows, w_down, down1)
-        caches = write(2, acts, caches)
-        u_far, caches, acts, snd_m = barrier((u_far, caches, acts, snd_m))
+        caches = write(3, acts, caches)
         sum_m = (own_m + core_swap(snd_m).astype(F32)).astype(BF16)
+        u_far, caches, acts, sum_m = barrier((u_far, caches, acts, sum_m))
         sum_m_y = y_swap(sum_m)
         own_f, snd_f = moe2_call(pick_f, u_far, ch_rows, w_down, down1)
         snd_f, acts = barrier((snd_f, acts))
         sum_f = (own_f + core_swap(snd_f).astype(F32)).astype(BF16)
         sum_f_y = y_swap(sum_f)
-        caches = write(3, acts, caches)
+        caches = write(4, acts, caches)
         sum_f_y, caches = barrier((sum_f_y, caches))
         moe_m = sum_m.astype(F32) + sum_m_y.astype(F32)
         moe_f = sum_f.astype(F32) + sum_f_y.astype(F32)

time: 235 us -> 227 us (0.966)
  Pallas kernels: 147 us -> 140 us
  local copies, waits for them, and re-layouts: 35.2 us -> 29.9 us
  waiting for transfers between devices: 20.9 us -> 25.3 us
    pallas_call x1, Pallas kernels: 26.8 us -> 14.8 us  [attn_call(): pl.pallas_call(attn_kernel, grid_spec=grid_spec, out_shape=jax.ShapeDtype...]
    pallas_call x4 -> x5, Pallas kernels: 53.2 us -> 58.2 us  [write_call(): pl.pallas_call(functools.partial(write_kernel, start, aliased), grid_spec...]
    ppermute x4, waiting for transfers between devices: 1.71 us -> 6.51 us  [y_swap(): return lax.ppermute(v, 'y', [(0, 1), (1, 0)])]
    reshape x1 -> x0, local copies, waits for them, and re-layouts: 2.66 us -> none  [layer(): qkv.reshape(5, steps, batch, 256).transpose(2, 0, 1, 3)]
    ppermute x7 -> x8, starting transfers between devices: 10.5 us -> 12 us  [chip_swap(): return lax.ppermute(v, 'x', [(0, 2), (2, 0), (1, 3), (3, 1)])]
    ppermute x7 -> x8, waiting for transfers between devices: 14.9 us -> 15.5 us  [chip_swap(): return lax.ppermute(v, 'x', [(0, 2), (2, 0), (1, 3), (3, 1)])]
  transfers between devices with their start and end apart: 25 -> 27, of which waited for: 7 -> 9; matrix products, arithmetic and copies ran while one was open for 15% -> 16% of each run, Pallas kernels for 44% -> 47%
where the time goes in v3:
time: 227 us; the launch traced here: 226 us
  Pallas kernels  140 us (62%)
  local copies, waits for them, and re-layouts  29.9 us (13%)
  waiting for transfers between devices  25.3 us (11%)
  starting transfers between devices  18.2 us (8%)
  other arithmetic  10.9 us (5%)
    pallas_call x5, Pallas kernels, write_call(): pl.pallas_call(functools.partial(write_kernel, start, aliased), grid_spec...  58.2 us
    pallas_call x2, Pallas kernels, moe1_call(): pl.pallas_call(moe1_kernel, grid_spec=grid_spec, out_shape=jax.ShapeDtype...  31.8 us
    pallas_call x2, Pallas kernels, moe2_call(): pl.pallas_call(moe2_kernel, grid_spec=grid_spec, out_shape=[jax.ShapeDtyp...  21.7 us
    ppermute x8, waiting for transfers between devices, chip_swap(): return lax.ppermute(v, 'x', [(0, 2), (2, 0), (1, 3), (3, 1)])  15.5 us
    pallas_call x1, Pallas kernels, attn_call(): pl.pallas_call(attn_kernel, grid_spec=grid_spec, out_shape=jax.ShapeDtype...  14.8 us
    dynamic_slice x3, local copies, waits for them, and re-layouts, theirs(): return lax.dynamic_slice_in_dim(w, (1 - core) * LANE, LANE, axis)  13.6 us
    ppermute x8, starting transfers between devices, chip_swap(): return lax.ppermute(v, 'x', [(0, 2), (2, 0), (1, 3), (3, 1)])  12 us
    pallas_call x1, Pallas kernels, qkv_calls(): pl.pallas_call(qkv_a_kernel, grid_spec=pltpu.PrefetchScalarGridSpec(num_s...  6.59 us
  transfers between devices with their start and end apart: 27, of which 9 were waited for; matrix products, arithmetic and copies ran while one was open for 16% of the time, Pallas kernels for 47%

profile of v3, /device:TPU:0, one launch (start us, length us, event | category | flops | bytes accessed | tf_op | source)
XLA Modules:
  0.0 226.2 jit_solution(7353152891387707768)
XLA Ops:
  0.6 1.4 copy.66
  2.4 3.3 %collective-permute-start.6 = (bf16[2,384,256]{2,1,0:T(8,128)(2,1)S(1)}, bf16[2,384,256]{2,1,0:T(8,128)(2,1)}, u32[]{:S(2)}, u32[]{:S(2)}) collective-permute-start(bf16[2,384,256]{2,1,0:T(8,128)(2,1)S(1)} %copy.72.w0), channel_id=1, source_target_pairs={{0,2},{2,0},{1,3},{3,1},{4,6},{6,4},{5,7},{7,5}} | collective-permute-start | bytes 1179656 | tf_op jit(solution)/shard_map/ppermute | solution.py:376
  6.6 5.0 %gather_fusion = bf16[768,384]{1,0:T(8,128)(2,1)S(1)} fusion(bf16[49155,384]{1,0:T(8,128)(2,1)} %param.19, s32[1024]{0:T(1024)S(1)} %pad_clamp_fusion), kind=kCustom, calls=%fused_computation | custom fusion | bytes 1182720 | tf_op jit(solution)/shard_map/jit(_take)/gather | solution.py:400
  11.8 2.0 collective-permute-start.2
  13.8 4.5 %constant_dynamic-slice_fusion.2 = bf16[40,384,128]{2,1,0:T(8,128)(2,1)} fusion(bf16[40,384,256]{2,1,0:T(8,128)(2,1)} %a0.3, s32[]{:T(128)S(6)} %select_n.79), kind=kLoop, calls=%fused_computation.55 | loop fusion | bytes 7864324 | tf_op jit(solution)/shard_map/dynamic_slice | solution.py:411
  18.3 4.5 %constant_dynamic-slice_fusion.1 = bf16[40,384,128]{2,1,0:T(8,128)(2,1)} fusion(bf16[40,384,256]{2,1,0:T(8,128)(2,1)} %l0.3, s32[]{:T(128)S(6)} %select_n.79), kind=kLoop, calls=%fused_computation.54 | loop fusion | bytes 7864324 | tf_op jit(solution)/shard_map/dynamic_slice | solution.py:411
  22.8 11.3 %collective-permute-done.2 = bf16[400,384]{1,0:T(8,128)(2,1)S(1)} collective-permute-done((bf16[400,384]{1,0:T(8,128)(2,1)S(1)}, bf16[400,384]{1,0:T(8,128)(2,1)S(1)}, u32[]{:S(2)}, u32[]{:S(2)}) %collective-permute-start.2) | collective-permute-done | bytes 307232 | tf_op jit(solution)/shard_map/ppermute | solution.py:376
  34.1 1.8 collective-permute-start.3
  35.9 4.7 %constant_dynamic-slice_fusion = bf16[40,128,384]{2,1,0:T(8,128)(2,1)} fusion(bf16[40,256,384]{2,1,0:T(8,128)(2,1)} %wa.3, s32[]{:T(128)S(6)} %select_n.79), kind=kLoop, calls=%fused_computation.53 | loop fusion | bytes 7864324 | tf_op jit(solution)/shard_map/dynamic_slice | solution.py:411
  40.5 0.7 pad_add_fusion
  41.2 0.9 copy.68
  42.2 1.9 broadcast_in_dim.58.ch_ref
  44.5 1.0 broadcast_select_fusion.1
  46.7 0.9 copy.74.sin_ref
  47.7 0.9 copy.73.cos_ref
  48.6 0.8 copy-done.8
  49.5 6.6 %qkv_a.1 = (bf16[768,1536]{1,0:T(8,128)(2,1)}, bf16[5,768,256]{2,1,0:T(8,128)(2,1)}) custom-call(s32[1]{0:T(128)} %bitcast.14.me_ref, bf16[784,384]{1,0:T(8,128)(2,1)} %copy-done.3, bf16[784,384]{1,0:T(8,128)(2,1)} %copy-done.8, bf16[784,384]{1,0:T(8,128)(2,1)} %copy-done.2, bf16[784,384]{1,0:T(8,128)(2,1)} %collective-permute-done.4.x3, ...), custom_call_target="tpu_custom_call" | custom-call | flops 1207959552 | bytes 6000000 | tf_op jit(solution)/shard_map/qkv_a/pallas_call | solution.py:96
  56.1 6.5 %qkv_b.1 = bf16[5,768,256]{2,1,0:T(8,128)(2,1)} custom-call(s32[1]{0:T(128)} %bitcast.14.me_ref, bf16[768,1536]{1,0:T(8,128)(2,1)} %get-tuple-element.66.hs, bf16[3,384,256]{2,1,0:T(8,128)(2,1)} %copy-done.4, bf16[3,384,256]{2,1,0:T(8,128)(2,1)} %collective-permute-done.8.w1, ...), custom_call_target="tpu_custom_call", output_to_operand_aliasing={{}: (8, {})} | custom-call | flops 1811939328 | bytes 6000000 | tf_op jit(solution)/shard_map/qkv_b/pallas_call | solution.py:110
  62.7 14.8 %attn.1 = bf16[64,16,256]{2,1,0:T(8,128)(2,1)} custom-call(s32[1]{0:T(128)} %bitcast.13.off_ref, s32[256]{0:T(256)} %len_ref.11, bf16[15,256,256]{2,1,0:T(8,128)(2,1)} %bitcast.65, bf16[65536,256]{1,0:T(8,128)(2,1)} %bitcast.49, bf16[65536,256]{1,0:T(8,128)(2,1)} %bitcast.50, bf16[65536,256]{1,0:T(8,128)(2,1)} %bitcast.56, bf16[65536,256]{1,0:T(8,128)(2,1)} %bitcast.57), custom_call_target="tpu_custom_call" | custom-call | flops 7680000000 | bytes 16777216 | tf_op jit(solution)/shard_map/attn/pallas_call | solution.py:193
  77.4 1.5 collective-permute-start.11
  78.9 12.0 %write.5 = (bf16[65536,256]{1,0:T(8,128)(2,1)}, bf16[65536,256]{1,0:T(8,128)(2,1)}) custom-call(s32[256]{0:T(256)} %len_ref.11, bf16[15,256,256]{2,1,0:T(8,128)(2,1)} %bitcast.66, bf16[65536,256]{1,0:T(8,128)(2,1)} %bitcast.51, bf16[65536,256]{1,0:T(8,128)(2,1)} %bitcast.58), custom_call_target="tpu_custom_call" | custom-call | flops 8640000000 | bytes 25165824 | tf_op jit(solution)/shard_map/write/pallas_call | solution.py:237
  92.6 0.8 collective-permute-done.12
  94.1 1.0 copy.81
  95.5 0.8 copy-done.10
  96.2 0.8 convolution_convert_fusion
  97.4 13.5 %write.6 = (bf16[65536,256]{1,0:T(8,128)(2,1)}, bf16[65536,256]{1,0:T(8,128)(2,1)}) custom-call(s32[256]{0:T(256)} %len_ref.11, bf16[15,256,256]{2,1,0:T(8,128)(2,1)} %bitcast.67, bf16[65536,256]{1,0:T(8,128)(2,1)} %bitcast.52, bf16[65536,256]{1,0:T(8,128)(2,1)} %bitcast.59, ...), custom_call_target="tpu_custom_call", output_to_operand_aliasing={{0}: (4, {}), {1}: (5, {})} | custom-call | flops 11520000000 | bytes 33554432 | tf_op jit(solution)/shard_map/write/pallas_call | solution.py:237
  110.8 1.6 collective-permute-done.13
  113.3 1.5 collective-permute-done.14
  115.0 1.5 collective-permute-start.15
  116.5 0.7 fusion.15
  117.2 1.4 collective-permute-done.15
  119.4 1.5 collective-permute-start.20
  121.0 1.1 pad_maximum_fusion.h_ref
  122.1 2.3 %collective-permute-done.20 = f32[768,40]{0,1:T(8,128)S(1)} collective-permute-done((f32[768,40]{0,1:T(8,128)S(1)}, f32[768,40]{0,1:T(8,128)S(1)}, u32[]{:S(2)}, u32[]{:S(2)}) %collective-permute-start.20) | collective-permute-done | bytes 122912 | tf_op jit(solution)/shard_map/ppermute | solution.py:376
  124.7 15.9 %moe1.2 = bf16[8,384,256]{2,1,0:T(8,128)(2,1)} custom-call(s32[2]{0:T(128)} %get-tuple-element.82.half_ref, bf16[768,768]{1,0:T(8,128)(2,1)} %pad_maximum_fusion.h_ref, bf16[8,768,128]{2,1,0:T(8,128)(2,1)} %broadcast_in_dim.58.ch_ref, bf16[40,384,256]{2,1,0:T(8,128)(2,1)} %a0.3, bf16[40,384,256]{2,1,0:T(8,128)(2,1)} %l0.3, ...), custom_call_target="tpu_custom_call" | custom-call | flops 6039797760 | bytes 20000000 | tf_op jit(solution)/shard_map/moe1/pallas_call | solution.py:294
  140.5 1.5 collective-permute-start.18
  142.0 15.9 %moe1.3 = bf16[8,384,256]{2,1,0:T(8,128)(2,1)} custom-call(s32[2]{0:T(128)} %get-tuple-element.93.half_ref, bf16[768,768]{1,0:T(8,128)(2,1)} %pad_maximum_fusion.h_ref, bf16[8,768,128]{2,1,0:T(8,128)(2,1)} %broadcast_in_dim.58.ch_ref, bf16[40,384,256]{2,1,0:T(8,128)(2,1)} %a0.3, bf16[40,384,256]{2,1,0:T(8,128)(2,1)} %l0.3, ...), custom_call_target="tpu_custom_call" | custom-call | flops 6039797760 | bytes 20000000 | tf_op jit(solution)/shard_map/moe1/pallas_call | solution.py:294
  157.9 18.2 %write.7 = (bf16[65536,256]{1,0:T(8,128)(2,1)}, bf16[65536,256]{1,0:T(8,128)(2,1)}) custom-call(s32[256]{0:T(256)} %len_ref.11, bf16[15,256,256]{2,1,0:T(8,128)(2,1)} %bitcast.68, bf16[65536,256]{1,0:T(8,128)(2,1)} %bitcast.53, bf16[65536,256]{1,0:T(8,128)(2,1)} %bitcast.60, ...), custom_call_target="tpu_custom_call", output_to_operand_aliasing={{0}: (4, {}), {1}: (5, {})} | custom-call | flops 14400000000 | bytes 41943040 | tf_op jit(solution)/shard_map/write/pallas_call | solution.py:237
  176.2 1.7 convert_add_fusion
  179.4 10.7 %moe2.2 = (f32[384,384]{1,0:T(8,128)}, bf16[384,384]{1,0:T(8,128)(2,1)}) custom-call(s32[2]{0:T(128)} %get-tuple-element.93.half_ref, bf16[8,384,128]{2,1,0:T(8,128)(2,1)} %copy-done.1, bf16[8,768,128]{2,1,0:T(8,128)(2,1)} %broadcast_in_dim.58.ch_ref, bf16[40,256,384]{2,1,0:T(8,128)(2,1)} %wa.3, bf16[40,128,384]{2,1,0:T(8,128)(2,1)} %collective-permute-done.22.wb), custom_call_target="tpu_custom_call" | custom-call | flops 3019898880 | bytes 10000000 | tf_op jit(solution)/shard_map/moe2/pallas_call | solution.py:357
  190.2 7.3 %write.8 = (bf16[65536,256]{1,0:T(8,128)(2,1)}, bf16[65536,256]{1,0:T(8,128)(2,1)}) custom-call(s32[256]{0:T(256)} %len_ref.11, bf16[15,256,256]{2,1,0:T(8,128)(2,1)} %bitcast.69, bf16[65536,256]{1,0:T(8,128)(2,1)} %bitcast.54, bf16[65536,256]{1,0:T(8,128)(2,1)} %bitcast.61, ...), custom_call_target="tpu_custom_call", output_to_operand_aliasing={{0}: (4, {}), {1}: (5, {})} | custom-call | flops 5760000000 | bytes 16777216 | tf_op jit(solution)/shard_map/write/pallas_call | solution.py:237
  197.6 0.9 copy-done.7
  198.5 10.9 %moe2.3 = (f32[384,384]{1,0:T(8,128)}, bf16[384,384]{1,0:T(8,128)(2,1)}) custom-call(s32[2]{0:T(128)} %get-tuple-element.82.half_ref, bf16[8,384,128]{2,1,0:T(8,128)(2,1)} %copy-done.7, bf16[8,768,128]{2,1,0:T(8,128)(2,1)} %broadcast_in_dim.58.ch_ref, bf16[40,256,384]{2,1,0:T(8,128)(2,1)} %wa.3, bf16[40,128,384]{2,1,0:T(8,128)(2,1)} %collective-permute-done.22.wb), custom_call_target="tpu_custom_call" | custom-call | flops 3019898880 | bytes 10000000 | tf_op jit(solution)/shard_map/moe2/pallas_call | solution.py:357
  210.3 0.9 collective-permute-done.25
  211.2 1.1 add_convert_fusion.1
  213.0 7.2 %write.9 = (bf16[65536,256]{1,0:T(8,128)(2,1)}, bf16[65536,256]{1,0:T(8,128)(2,1)}) custom-call(s32[256]{0:T(256)} %len_ref.11, bf16[15,256,256]{2,1,0:T(8,128)(2,1)} %bitcast.70, bf16[65536,256]{1,0:T(8,128)(2,1)} %bitcast.55, bf16[65536,256]{1,0:T(8,128)(2,1)} %bitcast.62, ...), custom_call_target="tpu_custom_call", output_to_operand_aliasing={{0}: (4, {}), {1}: (5, {})} | custom-call | flops 5760000000 | bytes 16777216 | tf_op jit(solution)/shard_map/write/pallas_call | solution.py:237
  220.2 5.0 %collective-permute-done.26 = bf16[384,384]{1,0:T(8,128)(2,1)S(1)} collective-permute-done((bf16[384,384]{1,0:T(8,128)(2,1)S(1)}, bf16[384,384]{1,0:T(8,128)(2,1)S(1)}, u32[]{:S(2)}, u32[]{:S(2)}) %collective-permute-start.26) | collective-permute-done | bytes 294944 | tf_op jit(solution)/shard_map/ppermute | solution.py:379
  225.2 1.0 fusion.7
  (126 shorter events, 11.4 us)
Async XLA Ops:
  2.1 3.8 %copy-start.12 = (bf16[384,256]{1,0:T(8,128)(2,1)S(1)}, bf16[384,256]{1,0:T(8,128)(2,1)}, u32[]{:S(2)}) copy-start(bf16[384,256]{1,0:T(8,128)(2,1)} %param.25) | copy-start | bytes 589828
  2.1 3.8 %copy-start.13 = (bf16[384,256]{1,0:T(8,128)(2,1)S(1)}, bf16[384,256]{1,0:T(8,128)(2,1)}, u32[]{:S(2)}) copy-start(bf16[384,256]{1,0:T(8,128)(2,1)} %param.24) | copy-start | bytes 589828
  2.1 4.4 %copy-start.18 = (bf16[384]{0:T(512)(128)(2,1)S(1)}, bf16[384]{0:T(512)(128)(2,1)}, u32[]{:S(2)}) copy-start(bf16[384]{0:T(512)(128)(2,1)} %param.22) | copy-start | bytes 2308
  2.1 4.4 %copy-start.16 = (bf16[384]{0:T(512)(128)(2,1)S(1)}, bf16[384]{0:T(512)(128)(2,1)}, u32[]{:S(2)}) copy-start(bf16[384]{0:T(512)(128)(2,1)} %param.27) | copy-start | bytes 2308
  2.1 4.4 %copy-start.17 = (s32[3,256]{1,0:T(4,128)S(1)}, s32[3,256]{1,0:T(4,128)}, u32[]{:S(2)}) copy-start(s32[3,256]{1,0:T(4,128)} %param.16) | copy-start | bytes 9220
  2.3 9.3 %copy-start.6 = (bf16[2,384,256]{2,1,0:T(8,128)(2,1)}, bf16[2,384,256]{2,1,0:T(8,128)(2,1)S(1)}, u32[]{:S(2)}) copy-start(bf16[2,384,256]{2,1,0:T(8,128)(2,1)S(1)} %copy.72.w0) | copy-start | bytes 1179652
  2.4 43.3 %collective-permute-start.6 = (bf16[2,384,256]{2,1,0:T(8,128)(2,1)S(1)}, bf16[2,384,256]{2,1,0:T(8,128)(2,1)}, u32[]{:S(2)}, u32[]{:S(2)}) collective-permute-start(bf16[2,384,256]{2,1,0:T(8,128)(2,1)S(1)} %copy.72.w0), channel_id=1, source_target_pairs={{0,2},{2,0},{1,3},{3,1},{4,6},{6,4},{5,7},{7,5}} | collective-permute-start | bytes 1179656 | tf_op jit(solution)/shard_map/ppermute | solution.py:376
  5.7 40.0 %collective-permute-start.5 = (bf16[2,384,256]{2,1,0:T(8,128)(2,1)S(1)}, bf16[2,384,256]{2,1,0:T(8,128)(2,1)}, u32[]{:S(2)}, u32[]{:S(2)}) collective-permute-start(bf16[2,384,256]{2,1,0:T(8,128)(2,1)S(1)} %copy.72.w0), channel_id=1, source_target_pairs={{0,1},{1,0},{2,3},{3,2},{4,5},{5,4},{6,7},{7,6}} | collective-permute-start | bytes 1179656 | tf_op jit(solution)/shard_map/ppermute | solution.py:373
  6.0 5.7 %copy-start.4 = (bf16[3,384,256]{2,1,0:T(8,128)(2,1)}, bf16[3,384,256]{2,1,0:T(8,128)(2,1)S(1)}, u32[]{:S(2)}) copy-start(bf16[3,384,256]{2,1,0:T(8,128)(2,1)S(1)} %pad_maximum_fusion.3.w0) | copy-start | bytes 1769476
  6.0 50.1 %collective-permute-start.8 = (bf16[3,384,256]{2,1,0:T(8,128)(2,1)S(1)}, bf16[3,384,256]{2,1,0:T(8,128)(2,1)}, u32[]{:S(2)}, u32[]{:S(2)}) collective-permute-start(bf16[3,384,256]{2,1,0:T(8,128)(2,1)S(1)} %pad_maximum_fusion.3.w0), channel_id=1, source_target_pairs={{0,1},{1,0},{2,3},{3,2},{4,5},{5,4},{6,7},{7,6}} | collective-permute-start | bytes 1769480 | tf_op jit(solution)/shard_map/ppermute | solution.py:373
  6.5 35.6 %collective-permute-start = (bf16[3,384,256]{2,1,0:T(8,128)(2,1)S(1)}, bf16[3,384,256]{2,1,0:T(8,128)(2,1)}, u32[]{:S(2)}, u32[]{:S(2)}) collective-permute-start(bf16[3,384,256]{2,1,0:T(8,128)(2,1)S(1)} %pad_maximum_fusion.3.w0), channel_id=1, source_target_pairs={{0,2},{2,0},{1,3},{3,1},{4,6},{6,4},{5,7},{7,5}} | collective-permute-start | bytes 1769480 | tf_op jit(solution)/shard_map/ppermute | solution.py:376
  11.8 30.3 %copy-start.3 = (bf16[784,384]{1,0:T(8,128)(2,1)}, bf16[784,384]{1,0:T(8,128)(2,1)S(1)}, u32[]{:S(2)}) copy-start(bf16[784,384]{1,0:T(8,128)(2,1)S(1)} %pad_maximum_fusion.1.x0) | copy-start | bytes 1806340
  11.8 22.2 %collective-permute-start.2 = (bf16[400,384]{1,0:T(8,128)(2,1)S(1)}, bf16[400,384]{1,0:T(8,128)(2,1)S(1)}, u32[]{:S(2)}, u32[]{:S(2)}) collective-permute-start(bf16[400,384]{1,0:T(8,128)(2,1)S(1)} %pad_maximum_fusion.4), channel_id=1, source_target_pairs={{0,2},{2,0},{1,3},{3,1},{4,6},{6,4},{5,7},{7,5}} | collective-permute-start | bytes 921608 | tf_op jit(solution)/shard_map/ppermute | solution.py:376
  18.3 4.5 %copy-start.14 = (s32[3,256,8]{1,2,0:T(8,128)S(1)}, s32[3,256,8]{1,2,0:T(8,128)}, u32[]{:S(2)}) copy-start(s32[3,256,8]{1,2,0:T(8,128)} %param.18) | copy-start | bytes 73732
  34.1 7.1 %copy-start.9 = (bf16[768,384]{1,0:T(8,128)(2,1)S(1)}, bf16[768,384]{1,0:T(8,128)(2,1)}, u32[]{:S(2)}) copy-start(bf16[768,384]{1,0:T(8,128)(2,1)} %param.26) | copy-start | bytes 1769476
  34.1 10.0 %collective-permute-start.3 = (bf16[384,384]{1,0:T(8,128)(2,1)S(1)}, bf16[384,384]{1,0:T(8,128)(2,1)}, u32[]{:S(2)}, u32[]{:S(2)}) collective-permute-start(bf16[384,384]{1,0:T(8,128)(2,1)S(1)} %slice.34), channel_id=1, source_target_pairs={{0,4},{4,0},{1,5},{5,1},{2,6},{6,2},{3,7},{7,3}} | collective-permute-start | bytes 884744 | tf_op jit(solution)/shard_map/ppermute | solution.py:379
  42.1 6.5 %collective-permute-start.1 = (bf16[784,384]{1,0:T(8,128)(2,1)S(1)}, bf16[784,384]{1,0:T(8,128)(2,1)S(1)}, u32[]{:S(2)}, u32[]{:S(2)}) collective-permute-start(bf16[784,384]{1,0:T(8,128)(2,1)S(1)} %pad_maximum_fusion.1.x0), channel_id=1, source_target_pairs={{0,1},{1,0},{2,3},{3,2},{4,5},{5,4},{6,7},{7,6}} | collective-permute-start | bytes 1806344 | tf_op jit(solution)/shard_map/ppermute | solution.py:373
  44.1 1.7 copy-start.15
  44.1 12.0 %collective-permute-start.9 = (bf16[3,384,256]{2,1,0:T(8,128)(2,1)}, bf16[3,384,256]{2,1,0:T(8,128)(2,1)}, u32[]{:S(2)}, u32[]{:S(2)}) collective-permute-start(bf16[3,384,256]{2,1,0:T(8,128)(2,1)} %collective-permute-done.w2), channel_id=1, source_target_pairs={{0,1},{1,0},{2,3},{3,2},{4,5},{5,4},{6,7},{7,6}} | collective-permute-start | bytes 1769480 | tf_op jit(solution)/shard_map/ppermute | solution.py:373
  45.6 2.1 copy-start.2
  45.7 3.0 %collective-permute-start.4 = (bf16[784,384]{1,0:T(8,128)(2,1)S(1)}, bf16[784,384]{1,0:T(8,128)(2,1)}, u32[]{:S(2)}, u32[]{:S(2)}) collective-permute-start(bf16[784,384]{1,0:T(8,128)(2,1)S(1)} %pad_maximum_fusion.2.x2), channel_id=1, source_target_pairs={{0,1},{1,0},{2,3},{3,2},{4,5},{5,4},{6,7},{7,6}} | collective-permute-start | bytes 1806344 | tf_op jit(solution)/shard_map/ppermute | solution.py:373
  45.7 2.9 %collective-permute-start.7 = (bf16[2,384,256]{2,1,0:T(8,128)(2,1)}, bf16[2,384,256]{2,1,0:T(8,128)(2,1)}, u32[]{:S(2)}, u32[]{:S(2)}) collective-permute-start(bf16[2,384,256]{2,1,0:T(8,128)(2,1)} %collective-permute-done.6.w2), channel_id=1, source_target_pairs={{0,1},{1,0},{2,3},{3,2},{4,5},{5,4},{6,7},{7,6}} | collective-permute-start | bytes 1179656 | tf_op jit(solution)/shard_map/ppermute | solution.py:373
  48.6 0.9 copy-start.8
  77.4 14.6 %copy-start.5 = (bf16[64,16,256]{2,1,0:T(8,128)(2,1)S(1)}, bf16[64,16,256]{2,1,0:T(8,128)(2,1)}, u32[]{:S(2)}) copy-start(bf16[64,16,256]{2,1,0:T(8,128)(2,1)} %attn.1) | copy-start | bytes 1572868
  77.4 14.1 %collective-permute-start.11 = (bf16[64,9,256]{2,1,0:T(8,128)(2,1)}, bf16[64,9,256]{2,1,0:T(8,128)(2,1)S(1)}, u32[]{:S(2)}, u32[]{:S(2)}) collective-permute-start(bf16[64,9,256]{2,1,0:T(8,128)(2,1)} %bitcast.74), channel_id=1, source_target_pairs={{0,2},{2,0},{1,3},{3,1},{4,6},{6,4},{5,7},{7,5}} | collective-permute-start | bytes 884744 | tf_op jit(solution)/shard_map/ppermute | solution.py:376
  78.9 13.3 %collective-permute-start.10 = (bf16[64,9,256]{2,1,0:T(8,128)(2,1)}, bf16[64,9,256]{2,1,0:T(8,128)(2,1)S(1)}, u32[]{:S(2)}, u32[]{:S(2)}) collective-permute-start(bf16[64,9,256]{2,1,0:T(8,128)(2,1)} %bitcast.75), channel_id=1, source_target_pairs={{0,1},{1,0},{2,3},{3,2},{4,5},{5,4},{6,7},{7,6}} | collective-permute-start | bytes 884744 | tf_op jit(solution)/shard_map/ppermute | solution.py:373
  91.5 1.9 collective-permute-start.12
  91.5 33.2 %collective-permute-start.16 = (bf16[40,384,128]{2,1,0:T(8,128)(2,1)}, bf16[40,384,128]{2,1,0:T(8,128)(2,1)}, u32[]{:S(2)}, u32[]{:S(2)}) collective-permute-start(bf16[40,384,128]{2,1,0:T(8,128)(2,1)} %constant_dynamic-slice_fusion.2), channel_id=1, source_target_pairs={{0,1},{1,0},{2,3},{3,2},{4,5},{5,4},{6,7},{7,6}} | collective-permute-start | bytes 11796488 | tf_op jit(solution)/shard_map/ppermute | solution.py:373
  92.0 32.7 %collective-permute-start.17 = (bf16[40,384,128]{2,1,0:T(8,128)(2,1)}, bf16[40,384,128]{2,1,0:T(8,128)(2,1)}, u32[]{:S(2)}, u32[]{:S(2)}) collective-permute-start(bf16[40,384,128]{2,1,0:T(8,128)(2,1)} %constant_dynamic-slice_fusion.1), channel_id=1, source_target_pairs={{0,1},{1,0},{2,3},{3,2},{4,5},{5,4},{6,7},{7,6}} | collective-permute-start | bytes 11796488 | tf_op jit(solution)/shard_map/ppermute | solution.py:373
  95.2 1.1 copy-start.10
  97.0 15.4 %collective-permute-start.13 = (bf16[768,384]{1,0:T(8,128)(2,1)S(1)}, bf16[768,384]{1,0:T(8,128)(2,1)S(1)}, u32[]{:S(2)}, u32[]{:S(2)}) collective-permute-start(bf16[768,384]{1,0:T(8,128)(2,1)S(1)} %convolution_convert_fusion), channel_id=1, source_target_pairs={{0,4},{4,0},{1,5},{5,1},{2,6},{6,2},{3,7},{7,3}} | collective-permute-start | bytes 1769480 | tf_op jit(solution)/shard_map/ppermute | solution.py:379
  110.8 2.0 copy-start.19
  112.8 2.0 collective-permute-start.14
  112.8 6.2 %collective-permute-start.19 = (bf16[384,40]{0,1:T(8,128)(2,1)S(1)}, bf16[384,40]{0,1:T(8,128)(2,1)S(1)}, u32[]{:S(2)}, u32[]{:S(2)}) collective-permute-start(bf16[384,40]{0,1:T(8,128)(2,1)S(1)} %copy-done.19), channel_id=1, source_target_pairs={{0,1},{1,0},{2,3},{3,2},{4,5},{5,4},{6,7},{7,6}} | collective-permute-start | bytes 92168 | tf_op jit(solution)/shard_map/ppermute | solution.py:373
  115.0 3.6 %collective-permute-start.15 = (f32[768]{0:T(1024)S(1)}, f32[768]{0:T(1024)S(1)}, u32[]{:S(2)}, u32[]{:S(2)}) collective-permute-start(f32[768]{0:T(1024)S(1)} %add.87), channel_id=1, source_target_pairs={{0,2},{2,0},{1,3},{3,1},{4,6},{6,4},{5,7},{7,5}} | collective-permute-start | bytes 9224 | tf_op jit(solution)/shard_map/ppermute | solution.py:376
  117.2 61.9 %collective-permute-start.22 = (bf16[40,128,384]{2,1,0:T(8,128)(2,1)}, bf16[40,128,384]{2,1,0:T(8,128)(2,1)}, u32[]{:S(2)}, u32[]{:S(2)}) collective-permute-start(bf16[40,128,384]{2,1,0:T(8,128)(2,1)} %constant_dynamic-slice_fusion), channel_id=1, source_target_pairs={{0,1},{1,0},{2,3},{3,2},{4,5},{5,4},{6,7},{7,6}} | collective-permute-start | bytes 11796488 | tf_op jit(solution)/shard_map/ppermute | solution.py:373
  119.4 4.9 %collective-permute-start.20 = (f32[768,40]{0,1:T(8,128)S(1)}, f32[768,40]{0,1:T(8,128)S(1)}, u32[]{:S(2)}, u32[]{:S(2)}) collective-permute-start(f32[768,40]{0,1:T(8,128)S(1)} %fusion.9), channel_id=1, source_target_pairs={{0,2},{2,0},{1,3},{3,1},{4,6},{6,4},{5,7},{7,5}} | collective-permute-start | bytes 368648 | tf_op jit(solution)/shard_map/ppermute | solution.py:376
  140.5 35.6 %collective-permute-start.18 = (bf16[8,384,256]{2,1,0:T(8,128)(2,1)}, bf16[8,384,256]{2,1,0:T(8,128)(2,1)}, u32[]{:S(2)}, u32[]{:S(2)}) collective-permute-start(bf16[8,384,256]{2,1,0:T(8,128)(2,1)} %moe1.2), channel_id=1, source_target_pairs={{0,2},{2,0},{1,3},{3,1},{4,6},{6,4},{5,7},{7,5}} | collective-permute-start | bytes 4718600 | tf_op jit(solution)/shard_map/ppermute | solution.py:376
  157.9 18.2 %copy-start = (bf16[8,384,256]{2,1,0:T(8,128)(2,1)S(1)}, bf16[8,384,256]{2,1,0:T(8,128)(2,1)}, u32[]{:S(2)}) copy-start(bf16[8,384,256]{2,1,0:T(8,128)(2,1)} %moe1.3) | copy-start | bytes 4718596
  178.5 0.9 copy-start.1
  178.6 19.0 %collective-permute-start.21 = (bf16[8,384,128]{2,1,0:T(8,128)(2,1)S(1)}, bf16[8,384,128]{2,1,0:T(8,128)(2,1)S(1)}, u32[]{:S(2)}, u32[]{:S(2)}) collective-permute-start(bf16[8,384,128]{2,1,0:T(8,128)(2,1)S(1)} %fusion.u_ref), channel_id=1, source_target_pairs={{0,2},{2,0},{1,3},{3,1},{4,6},{6,4},{5,7},{7,5}} | collective-permute-start | bytes 2359304 | tf_op jit(solution)/shard_map/ppermute | solution.py:376
  190.2 7.3 %copy-start.11 = (f32[384,384]{1,0:T(8,128)S(1)}, f32[384,384]{1,0:T(8,128)}, u32[]{:S(2)}) copy-start(f32[384,384]{1,0:T(8,128)} %get-tuple-element.103) | copy-start | bytes 1769476
  190.2 7.3 %collective-permute-start.23 = (bf16[384,384]{1,0:T(8,128)(2,1)}, bf16[384,384]{1,0:T(8,128)(2,1)S(1)}, u32[]{:S(2)}, u32[]{:S(2)}) collective-permute-start(bf16[384,384]{1,0:T(8,128)(2,1)} %get-tuple-element.104), channel_id=1, source_target_pairs={{0,1},{1,0},{2,3},{3,2},{4,5},{5,4},{6,7},{7,6}} | collective-permute-start | bytes 884744 | tf_op jit(solution)/shard_map/ppermute | solution.py:373
  197.6 0.9 copy-start.7
  209.4 1.8 collective-permute-start.25
  209.8 10.4 %collective-permute-start.24 = (bf16[384,384]{1,0:T(8,128)(2,1)S(1)}, bf16[384,384]{1,0:T(8,128)(2,1)S(1)}, u32[]{:S(2)}, u32[]{:S(2)}) collective-permute-start(bf16[384,384]{1,0:T(8,128)(2,1)S(1)} %add_convert_fusion.2), channel_id=1, source_target_pairs={{0,4},{4,0},{1,5},{5,1},{2,6},{6,2},{3,7},{7,3}} | collective-permute-start | bytes 884744 | tf_op jit(solution)/shard_map/ppermute | solution.py:379
  212.3 12.8 %collective-permute-start.26 = (bf16[384,384]{1,0:T(8,128)(2,1)S(1)}, bf16[384,384]{1,0:T(8,128)(2,1)S(1)}, u32[]{:S(2)}, u32[]{:S(2)}) collective-permute-start(bf16[384,384]{1,0:T(8,128)(2,1)S(1)} %add_convert_fusion.1), channel_id=1, source_target_pairs={{0,4},{4,0},{1,5},{5,1},{2,6},{6,2},{3,7},{7,3}} | collective-permute-start | bytes 884744 | tf_op jit(solution)/shard_map/ppermute | solution.py:379

commit v4 on v3

--- a/solution.py
+++ b/solution.py
@@ -201,7 +201,7 @@
 
 
 WB = 16
-PIECES = (48, 64, 80, 32, 32)
+PIECES = (32, 64, 96, 32, 32)
 
 
 def write_kernel(start, aliased, len_ref, a_ref, k_ref, v_ref, *rest):
@@ -406,15 +406,22 @@
         x_mate = core_swap(x_ext)
         wa2 = chip_swap(w_a)
         wb2 = chip_swap(w_b)
+        positions = lengths[None, :] + jnp.arange(steps, dtype=jnp.int32)[:, None]
+        inv_freq = ROPE_BASE ** (-(jnp.arange(hd // 2, dtype=F32) * 2.0 / hd))
+        angles = positions.reshape(n_tok).astype(F32)[:, None] * inv_freq[None, :]
+        cos, sin = jnp.cos(angles), jnp.sin(angles)
+        cos2, sin2 = jnp.concatenate([cos] * 4, axis=1), jnp.concatenate([-sin, sin] * 2, axis=1)
+        choice_rows = choices.reshape(n_tok, 8)
+        ch_rows = jnp.broadcast_to(choice_rows.T.astype(BF16)[:, :, None], (8, n_tok, LANE))
 
         def theirs(w, axis):
             return lax.dynamic_slice_in_dim(w, (1 - core) * LANE, LANE, axis)
 
         act_s = theirs(w_act, 2)
-        lin_s, down_s = theirs(w_lin, 2), theirs(w_down, 1)
+        lin_s = theirs(w_lin, 2)
         part, act_s = barrier((part, act_s))
         part_o = y_swap(part[:half_tok])
-        part_o, lin_s, down_s = barrier((part_o, lin_s, down_s))
+        part_o, lin_s, ch_rows, cos2, sin2 = barrier((part_o, lin_s, ch_rows, cos2, sin2))
         lo = jnp.where(my == 0, part[:half_tok], part_o)
         hi = jnp.where(my == 0, part_o, part[:half_tok])
         x_far = jnp.concatenate([lo, hi, part[half_tok:]])
@@ -423,20 +430,11 @@
 
         router = jnp.concatenate([w_router, core_swap(w_router)], axis=0)
 
-        positions = lengths[None, :] + jnp.arange(steps, dtype=jnp.int32)[:, None]
-        inv_freq = ROPE_BASE ** (-(jnp.arange(hd // 2, dtype=F32) * 2.0 / hd))
-        angles = positions.reshape(n_tok).astype(F32)[:, None] * inv_freq[None, :]
-        cos, sin = jnp.cos(angles), jnp.sin(angles)
-        cos2, sin2 = jnp.tile(cos, (1, 4)), jnp.tile(jnp.concatenate([-sin, sin], axis=1), (1, 2))
-        choice_rows = choices.reshape(n_tok, 8)
-        ch_rows = jnp.broadcast_to(choice_rows.T.astype(BF16)[:, :, None], (8, n_tok, LANE))
-        wo = w_o.reshape(kv, group, hd, width).transpose(1, 0, 2, 3).reshape(group * kv * hd, width)
 
         pick_m, pick_f = jnp.stack([cx, core]), jnp.stack([1 - cx, core])
         offset = (me * (batch // 4) // NB)[None]
-        wb2, ch_rows, wo, pick_m, pick_f, offset = barrier((wb2, ch_rows, wo, pick_m, pick_f, offset))
         wb3 = core_swap(wb2)
-        act1, lin1, down1 = core_swap(act_s), core_swap(lin_s), core_swap(down_s)
+        act1, lin1 = core_swap(act_s), core_swap(lin_s)
         qkv = qkv_calls(me[None], (x_ext, x_mate, x_far, x_far_mate), (w_a, wa1, wa2, wa3), (w_b, wb1, wb2, wb3), cos2, sin2)
         acts = qkv.reshape(5 * steps, batch, WIDE)
         k_rows = k_cache.transpose(0, 2, 3, 1).reshape(batch * kv * hd, slots)
@@ -450,10 +448,13 @@
             return rows.reshape(batch, kv, hd, slots).transpose(0, 3, 1, 2)
 
         o = attn_call(offset, lengths, acts, k_rows, v_rows, batch // 4)[:, : steps * group]
-        o, acts = barrier((o, acts))
+        o, acts, w_down, w_o = barrier((o, acts, w_down, w_o))
+        wo = w_o.reshape(kv, group, hd, width).transpose(1, 0, 2, 3).reshape(group * kv * hd, width)
         o_far = chip_swap(o)
+        down_s = theirs(w_down, 1)
         caches = write(0, acts, None)
-        o_far, caches = barrier((o_far, caches))
+        o_far, caches, down_s, wo, pick_m, pick_f = barrier((o_far, caches, down_s, wo, pick_m, pick_f))
+        down1 = core_swap(down_s)
 
         def in_order(v, mate):
             return jnp.where(core == 0, jnp.concatenate([v, mate]), jnp.concatenate([mate, v]))
@@ -478,12 +479,13 @@
         h2 = jnp.concatenate([x1f * scale * g_own, x1mf * scale * g_mate], axis=1).astype(BF16)
         logits = jnp.dot(h2, router, preferred_element_type=F32)
 
+        logits_far = chip_swap(logits)
         send = moe1_call(pick_f, h2, ch_rows, w_act, w_lin, act1, lin1)
         send, h2, acts = barrier((send, h2, acts))
         got = chip_swap(send)
         keep = moe1_call(pick_m, h2, ch_rows, w_act, w_lin, act1, lin1)
         caches = write(2, acts, caches)
-        logits = logits + chip_swap(logits)
+        logits = logits + logits_far
         picked = jnp.sum(jnp.where(choice_rows[:, :, None] == jnp.arange(experts)[None, None, :], logits[:, None, :], 0.0), axis=-1)
         gate = jax.nn.softmax(picked, axis=-1)
         gate_mine = lax.dynamic_slice_in_dim(gate, cx * half_tok, half_tok, 0).T

time: 227 us -> 216 us (0.952)
  waiting for transfers between devices: 25.3 us -> 15 us
  Pallas kernels: 140 us -> 136 us
  starting transfers between devices: 18.2 us -> 21.9 us
  local copies, waits for them, and re-layouts: 29.9 us -> 26.8 us
  other arithmetic: 10.9 us -> 13.5 us
    ppermute x8, waiting for transfers between devices: 15.5 us -> 6.74 us  [chip_swap(): return lax.ppermute(v, 'x', [(0, 2), (2, 0), (1, 3), (3, 1)])]
    pallas_call x5, Pallas kernels: 58.2 us -> 54.5 us  [write_call(): pl.pallas_call(functools.partial(write_kernel, start, aliased), grid_spec...]
    ppermute x4, starting transfers between devices: 3.27 us -> 6.78 us  [y_swap(): return lax.ppermute(v, 'y', [(0, 1), (1, 0)])]
    unnamed x42 -> x38, local copies, waits for them, and re-layouts: 4.55 us -> 4.16 us
  transfers between devices with their start and end apart: 27 -> 27, of which waited for: 9 -> 10; matrix products, arithmetic and copies ran while one was open for 16% -> 17% of each run, Pallas kernels for 47% -> 48%
where the time goes in v4:
time: 216 us; the launch traced here: 215 us
  Pallas kernels  136 us (63%)
  local copies, waits for them, and re-layouts  26.8 us (12%)
  starting transfers between devices  21.9 us (10%)
  waiting for transfers between devices  15 us (7%)
  other arithmetic  13.5 us (6%)
    pallas_call x5, Pallas kernels, write_call(): pl.pallas_call(functools.partial(write_kernel, start, aliased), grid_spec...  54.5 us
    pallas_call x2, Pallas kernels, moe1_call(): pl.pallas_call(moe1_kernel, grid_spec=grid_spec, out_shape=jax.ShapeDtype...  31.7 us
    pallas_call x2, Pallas kernels, moe2_call(): pl.pallas_call(moe2_kernel, grid_spec=grid_spec, out_shape=[jax.ShapeDtyp...  21.5 us
    pallas_call x1, Pallas kernels, attn_call(): pl.pallas_call(attn_kernel, grid_spec=grid_spec, out_shape=jax.ShapeDtype...  14.8 us
    dynamic_slice x3, local copies, waits for them, and re-layouts, theirs(): return lax.dynamic_slice_in_dim(w, (1 - core) * LANE, LANE, axis)  13.6 us
    ppermute x8, starting transfers between devices, chip_swap(): return lax.ppermute(v, 'x', [(0, 2), (2, 0), (1, 3), (3, 1)])  12.7 us
    ppermute x4, starting transfers between devices, y_swap(): return lax.ppermute(v, 'y', [(0, 1), (1, 0)])  6.78 us
    ppermute x8, waiting for transfers between devices, chip_swap(): return lax.ppermute(v, 'x', [(0, 2), (2, 0), (1, 3), (3, 1)])  6.74 us
  transfers between devices with their start and end apart: 27, of which 10 were waited for; matrix products, arithmetic and copies ran while one was open for 17% of the time, Pallas kernels for 48%

profile of v4, /device:TPU:0, one launch (start us, length us, event | category | flops | bytes accessed | tf_op | source)
XLA Modules:
  0.0 215.3 jit_solution(3167964859697802447)
XLA Ops:
  0.6 1.4 copy.71
  2.3 3.3 %collective-permute-start.5 = (bf16[2,384,256]{2,1,0:T(8,128)(2,1)S(1)}, bf16[2,384,256]{2,1,0:T(8,128)(2,1)}, u32[]{:S(2)}, u32[]{:S(2)}) collective-permute-start(bf16[2,384,256]{2,1,0:T(8,128)(2,1)S(1)} %copy.75.w0), channel_id=1, source_target_pairs={{0,2},{2,0},{1,3},{3,1},{4,6},{6,4},{5,7},{7,5}} | collective-permute-start | bytes 1179656 | tf_op jit(solution)/shard_map/ppermute | solution.py:376
  5.7 5.0 %gather_fusion = bf16[768,384]{1,0:T(8,128)(2,1)S(1)} fusion(bf16[49155,384]{1,0:T(8,128)(2,1)} %param.19, s32[1024]{0:T(1024)S(1)} %pad_clamp_fusion), kind=kCustom, calls=%fused_computation | custom fusion | bytes 1182720 | tf_op jit(solution)/shard_map/jit(_take)/gather | solution.py:400
  11.5 1.1 pad_maximum_fusion.3.w0
  12.6 1.7 collective-permute-start.8
  14.4 4.4 %constant_dynamic-slice_fusion.2 = bf16[40,384,128]{2,1,0:T(8,128)(2,1)} fusion(bf16[40,384,256]{2,1,0:T(8,128)(2,1)} %a0.3, s32[]{:T(128)S(6)} %select_n.79), kind=kLoop, calls=%fused_computation.56 | loop fusion | bytes 7864324 | tf_op jit(solution)/shard_map/dynamic_slice | solution.py:418
  18.8 1.5 fusion.9
  20.3 1.7 collective-permute-done.1
  22.1 2.0 collective-permute-start.2
  24.1 4.5 %constant_dynamic-slice_fusion.1 = bf16[40,384,128]{2,1,0:T(8,128)(2,1)} fusion(bf16[40,384,256]{2,1,0:T(8,128)(2,1)} %l0.3, s32[]{:T(128)S(6)} %select_n.79), kind=kLoop, calls=%fused_computation.55 | loop fusion | bytes 7864324 | tf_op jit(solution)/shard_map/dynamic_slice | solution.py:418
  28.6 1.6 pad_maximum_fusion.4
  30.1 1.9 broadcast_in_dim.61.ch_ref
  32.8 1.3 collective-permute-done.8.w2
  35.3 1.6 collective-permute-done.6.w3
  36.9 0.7 copy-done.11
  37.8 6.6 %qkv_a.1 = (bf16[768,1536]{1,0:T(8,128)(2,1)}, bf16[5,768,256]{2,1,0:T(8,128)(2,1)}) custom-call(s32[1]{0:T(128)} %bitcast.1.me_ref, bf16[784,384]{1,0:T(8,128)(2,1)} %copy-done.3, bf16[784,384]{1,0:T(8,128)(2,1)} %collective-permute-done.x1, bf16[784,384]{1,0:T(8,128)(2,1)} %copy-done.2, bf16[784,384]{1,0:T(8,128)(2,1)} %copy-done.8, ...), custom_call_target="tpu_custom_call" | custom-call | flops 1207959552 | bytes 6000000 | tf_op jit(solution)/shard_map/qkv_a/pallas_call | solution.py:96
  44.5 6.6 %qkv_b.1 = bf16[5,768,256]{2,1,0:T(8,128)(2,1)} custom-call(s32[1]{0:T(128)} %bitcast.1.me_ref, bf16[768,1536]{1,0:T(8,128)(2,1)} %get-tuple-element.69.hs, bf16[3,384,256]{2,1,0:T(8,128)(2,1)} %copy-done.4, bf16[3,384,256]{2,1,0:T(8,128)(2,1)} %collective-permute-done.7.w1, ...), custom_call_target="tpu_custom_call", output_to_operand_aliasing={{}: (8, {})} | custom-call | flops 1811939328 | bytes 6000000 | tf_op jit(solution)/shard_map/qkv_b/pallas_call | solution.py:110
  51.0 14.8 %attn.1 = bf16[64,16,256]{2,1,0:T(8,128)(2,1)} custom-call(s32[1]{0:T(128)} %bitcast.off_ref, s32[256]{0:T(256)} %len_ref.11, bf16[15,256,256]{2,1,0:T(8,128)(2,1)} %bitcast.63, bf16[65536,256]{1,0:T(8,128)(2,1)} %bitcast.47, bf16[65536,256]{1,0:T(8,128)(2,1)} %bitcast.48, bf16[65536,256]{1,0:T(8,128)(2,1)} %bitcast.54, bf16[65536,256]{1,0:T(8,128)(2,1)} %bitcast.55), custom_call_target="tpu_custom_call" | custom-call | flops 7680000000 | bytes 16777216 | tf_op jit(solution)/shard_map/attn/pallas_call | solution.py:193
  65.8 1.7 collective-permute-start.11
  67.5 7.2 %write.5 = (bf16[65536,256]{1,0:T(8,128)(2,1)}, bf16[65536,256]{1,0:T(8,128)(2,1)}) custom-call(s32[256]{0:T(256)} %len_ref.11, bf16[15,256,256]{2,1,0:T(8,128)(2,1)} %bitcast.64, bf16[65536,256]{1,0:T(8,128)(2,1)} %bitcast.49, bf16[65536,256]{1,0:T(8,128)(2,1)} %bitcast.56), custom_call_target="tpu_custom_call" | custom-call | flops 5760000000 | bytes 16777216 | tf_op jit(solution)/shard_map/write/pallas_call | solution.py:237
  74.8 4.7 %constant_dynamic-slice_fusion = bf16[40,128,384]{2,1,0:T(8,128)(2,1)} fusion(bf16[40,256,384]{2,1,0:T(8,128)(2,1)} %wa.1, s32[]{:T(128)S(6)} %select_n.79), kind=kLoop, calls=%fused_computation.54 | loop fusion | bytes 7864324 | tf_op jit(solution)/shard_map/dynamic_slice | solution.py:418
  81.1 0.7 collective-permute-done.12
  82.6 1.0 copy.82
  83.9 0.8 convolution_convert_fusion
  84.7 1.8 collective-permute-start.13
  86.5 13.3 %write.6 = (bf16[65536,256]{1,0:T(8,128)(2,1)}, bf16[65536,256]{1,0:T(8,128)(2,1)}) custom-call(s32[256]{0:T(256)} %len_ref.11, bf16[15,256,256]{2,1,0:T(8,128)(2,1)} %bitcast.65, bf16[65536,256]{1,0:T(8,128)(2,1)} %bitcast.50, bf16[65536,256]{1,0:T(8,128)(2,1)} %bitcast.57, ...), custom_call_target="tpu_custom_call", output_to_operand_aliasing={{0}: (4, {}), {1}: (5, {})} | custom-call | flops 11520000000 | bytes 33554432 | tf_op jit(solution)/shard_map/write/pallas_call | solution.py:237
  101.0 1.5 collective-permute-done.14
  102.7 1.7 collective-permute-start.15
  104.4 0.7 fusion.15
  105.2 1.2 collective-permute-done.15
  107.2 1.8 collective-permute-start.20
  108.9 1.1 pad_maximum_fusion.h_ref
  110.0 2.1 collective-permute-done.20
  112.4 15.9 %moe1.2 = bf16[8,384,256]{2,1,0:T(8,128)(2,1)} custom-call(s32[2]{0:T(128)} %get-tuple-element.86.half_ref, bf16[768,768]{1,0:T(8,128)(2,1)} %pad_maximum_fusion.h_ref, bf16[8,768,128]{2,1,0:T(8,128)(2,1)} %broadcast_in_dim.61.ch_ref, bf16[40,384,256]{2,1,0:T(8,128)(2,1)} %a0.3, bf16[40,384,256]{2,1,0:T(8,128)(2,1)} %l0.3, ...), custom_call_target="tpu_custom_call" | custom-call | flops 6039797760 | bytes 20000000 | tf_op jit(solution)/shard_map/moe1/pallas_call | solution.py:294
  128.3 1.7 collective-permute-start.18
  130.0 15.8 %moe1.3 = bf16[8,384,256]{2,1,0:T(8,128)(2,1)} custom-call(s32[2]{0:T(128)} %get-tuple-element.97.half_ref, bf16[768,768]{1,0:T(8,128)(2,1)} %pad_maximum_fusion.h_ref, bf16[8,768,128]{2,1,0:T(8,128)(2,1)} %broadcast_in_dim.61.ch_ref, bf16[40,384,256]{2,1,0:T(8,128)(2,1)} %a0.3, bf16[40,384,256]{2,1,0:T(8,128)(2,1)} %l0.3, ...), custom_call_target="tpu_custom_call" | custom-call | flops 6039797760 | bytes 20000000 | tf_op jit(solution)/shard_map/moe1/pallas_call | solution.py:294
  145.8 19.6 %write.7 = (bf16[65536,256]{1,0:T(8,128)(2,1)}, bf16[65536,256]{1,0:T(8,128)(2,1)}) custom-call(s32[256]{0:T(256)} %len_ref.11, bf16[15,256,256]{2,1,0:T(8,128)(2,1)} %bitcast.66, bf16[65536,256]{1,0:T(8,128)(2,1)} %bitcast.51, bf16[65536,256]{1,0:T(8,128)(2,1)} %bitcast.58, ...), custom_call_target="tpu_custom_call", output_to_operand_aliasing={{0}: (4, {}), {1}: (5, {})} | custom-call | flops 17280000000 | bytes 50331648 | tf_op jit(solution)/shard_map/write/pallas_call | solution.py:237
  165.4 1.7 convert_add_fusion
  168.7 10.7 %moe2.2 = (f32[384,384]{1,0:T(8,128)}, bf16[384,384]{1,0:T(8,128)(2,1)}) custom-call(s32[2]{0:T(128)} %get-tuple-element.97.half_ref, bf16[8,384,128]{2,1,0:T(8,128)(2,1)} %copy-done.1, bf16[8,768,128]{2,1,0:T(8,128)(2,1)} %broadcast_in_dim.61.ch_ref, bf16[40,256,384]{2,1,0:T(8,128)(2,1)} %wa.1, bf16[40,128,384]{2,1,0:T(8,128)(2,1)} %collective-permute-done.22.wb), custom_call_target="tpu_custom_call" | custom-call | flops 3019898880 | bytes 10000000 | tf_op jit(solution)/shard_map/moe2/pallas_call | solution.py:357
  179.4 7.3 %write.8 = (bf16[65536,256]{1,0:T(8,128)(2,1)}, bf16[65536,256]{1,0:T(8,128)(2,1)}) custom-call(s32[256]{0:T(256)} %len_ref.11, bf16[15,256,256]{2,1,0:T(8,128)(2,1)} %bitcast.67, bf16[65536,256]{1,0:T(8,128)(2,1)} %bitcast.52, bf16[65536,256]{1,0:T(8,128)(2,1)} %bitcast.59, ...), custom_call_target="tpu_custom_call", output_to_operand_aliasing={{0}: (4, {}), {1}: (5, {})} | custom-call | flops 5760000000 | bytes 16777216 | tf_op jit(solution)/shard_map/write/pallas_call | solution.py:237
  186.8 0.9 copy-done.7
  187.7 10.7 %moe2.3 = (f32[384,384]{1,0:T(8,128)}, bf16[384,384]{1,0:T(8,128)(2,1)}) custom-call(s32[2]{0:T(128)} %get-tuple-element.86.half_ref, bf16[8,384,128]{2,1,0:T(8,128)(2,1)} %copy-done.7, bf16[8,768,128]{2,1,0:T(8,128)(2,1)} %broadcast_in_dim.61.ch_ref, bf16[40,256,384]{2,1,0:T(8,128)(2,1)} %wa.1, bf16[40,128,384]{2,1,0:T(8,128)(2,1)} %collective-permute-done.22.wb), custom_call_target="tpu_custom_call" | custom-call | flops 3019898880 | bytes 10000000 | tf_op jit(solution)/shard_map/moe2/pallas_call | solution.py:357
  198.8 1.5 collective-permute-start.24
  200.4 1.1 add_convert_fusion.1
  201.5 1.4 collective-permute-start.26
  202.9 7.2 %write.9 = (bf16[65536,256]{1,0:T(8,128)(2,1)}, bf16[65536,256]{1,0:T(8,128)(2,1)}) custom-call(s32[256]{0:T(256)} %len_ref.11, bf16[15,256,256]{2,1,0:T(8,128)(2,1)} %bitcast.68, bf16[65536,256]{1,0:T(8,128)(2,1)} %bitcast.53, bf16[65536,256]{1,0:T(8,128)(2,1)} %bitcast.60, ...), custom_call_target="tpu_custom_call", output_to_operand_aliasing={{0}: (4, {}), {1}: (5, {})} | custom-call | flops 5760000000 | bytes 16777216 | tf_op jit(solution)/shard_map/write/pallas_call | solution.py:237
  210.2 4.0 %collective-permute-done.26 = bf16[384,384]{1,0:T(8,128)(2,1)S(1)} collective-permute-done((bf16[384,384]{1,0:T(8,128)(2,1)S(1)}, bf16[384,384]{1,0:T(8,128)(2,1)S(1)}, u32[]{:S(2)}, u32[]{:S(2)}) %collective-permute-start.26) | collective-permute-done | bytes 294944 | tf_op jit(solution)/shard_map/ppermute | solution.py:379
  214.3 1.0 fusion.7
  (118 shorter events, 10.4 us)
Async XLA Ops:
  2.0 3.7 %copy-start.16 = (bf16[384]{0:T(512)(128)(2,1)S(1)}, bf16[384]{0:T(512)(128)(2,1)}, u32[]{:S(2)}) copy-start(bf16[384]{0:T(512)(128)(2,1)} %param.22) | copy-start | bytes 2308
  2.0 3.7 %copy-start.14 = (bf16[384]{0:T(512)(128)(2,1)S(1)}, bf16[384]{0:T(512)(128)(2,1)}, u32[]{:S(2)}) copy-start(bf16[384]{0:T(512)(128)(2,1)} %param.27) | copy-start | bytes 2308
  2.0 3.7 %copy-start.15 = (s32[3,256]{1,0:T(4,128)S(1)}, s32[3,256]{1,0:T(4,128)}, u32[]{:S(2)}) copy-start(s32[3,256]{1,0:T(4,128)} %param.16) | copy-start | bytes 9220
  2.3 8.4 %copy-start.6 = (bf16[2,384,256]{2,1,0:T(8,128)(2,1)}, bf16[2,384,256]{2,1,0:T(8,128)(2,1)S(1)}, u32[]{:S(2)}) copy-start(bf16[2,384,256]{2,1,0:T(8,128)(2,1)S(1)} %copy.75.w0) | copy-start | bytes 1179652
  2.3 29.9 %collective-permute-start.5 = (bf16[2,384,256]{2,1,0:T(8,128)(2,1)S(1)}, bf16[2,384,256]{2,1,0:T(8,128)(2,1)}, u32[]{:S(2)}, u32[]{:S(2)}) collective-permute-start(bf16[2,384,256]{2,1,0:T(8,128)(2,1)S(1)} %copy.75.w0), channel_id=1, source_target_pairs={{0,2},{2,0},{1,3},{3,1},{4,6},{6,4},{5,7},{7,5}} | collective-permute-start | bytes 1179656 | tf_op jit(solution)/shard_map/ppermute | solution.py:376
  5.7 28.4 %collective-permute-start.4 = (bf16[2,384,256]{2,1,0:T(8,128)(2,1)S(1)}, bf16[2,384,256]{2,1,0:T(8,128)(2,1)}, u32[]{:S(2)}, u32[]{:S(2)}) collective-permute-start(bf16[2,384,256]{2,1,0:T(8,128)(2,1)S(1)} %copy.75.w0), channel_id=1, source_target_pairs={{0,1},{1,0},{2,3},{3,2},{4,5},{5,4},{6,7},{7,6}} | collective-permute-start | bytes 1179656 | tf_op jit(solution)/shard_map/ppermute | solution.py:373
  10.9 3.4 %copy-start.3 = (bf16[784,384]{1,0:T(8,128)(2,1)}, bf16[784,384]{1,0:T(8,128)(2,1)S(1)}, u32[]{:S(2)}) copy-start(bf16[784,384]{1,0:T(8,128)(2,1)S(1)} %pad_maximum_fusion.1.x0) | copy-start | bytes 1806340
  10.9 3.4 %copy-start.13 = (s32[256]{0:T(256)S(1)}, s32[256]{0:T(256)}, u32[]{:S(2)}) copy-start(s32[256]{0:T(256)} %len_ref.11) | copy-start | bytes 3076
  10.9 3.4 %copy-start.12 = (s32[3,256,8]{1,2,0:T(8,128)S(1)}, s32[3,256,8]{1,2,0:T(8,128)}, u32[]{:S(2)}) copy-start(s32[3,256,8]{1,2,0:T(8,128)} %param.18) | copy-start | bytes 73732
  11.0 11.1 %collective-permute-start.1 = (bf16[400,384]{1,0:T(8,128)(2,1)S(1)}, bf16[400,384]{1,0:T(8,128)(2,1)S(1)}, u32[]{:S(2)}, u32[]{:S(2)}) collective-permute-start(bf16[400,384]{1,0:T(8,128)(2,1)S(1)} %pad_maximum_fusion.6), channel_id=1, source_target_pairs={{0,2},{2,0},{1,3},{3,1},{4,6},{6,4},{5,7},{7,5}} | collective-permute-start | bytes 921608 | tf_op jit(solution)/shard_map/ppermute | solution.py:376
  12.6 19.7 %copy-start.4 = (bf16[3,384,256]{2,1,0:T(8,128)(2,1)}, bf16[3,384,256]{2,1,0:T(8,128)(2,1)S(1)}, u32[]{:S(2)}) copy-start(bf16[3,384,256]{2,1,0:T(8,128)(2,1)S(1)} %pad_maximum_fusion.3.w0) | copy-start | bytes 1769476
  12.6 21.5 %collective-permute-start.8 = (bf16[3,384,256]{2,1,0:T(8,128)(2,1)S(1)}, bf16[3,384,256]{2,1,0:T(8,128)(2,1)}, u32[]{:S(2)}, u32[]{:S(2)}) collective-permute-start(bf16[3,384,256]{2,1,0:T(8,128)(2,1)S(1)} %pad_maximum_fusion.3.w0), channel_id=1, source_target_pairs={{0,2},{2,0},{1,3},{3,1},{4,6},{6,4},{5,7},{7,5}} | collective-permute-start | bytes 1769480 | tf_op jit(solution)/shard_map/ppermute | solution.py:376
  14.3 20.9 %collective-permute-start = (bf16[784,384]{1,0:T(8,128)(2,1)S(1)}, bf16[784,384]{1,0:T(8,128)(2,1)}, u32[]{:S(2)}, u32[]{:S(2)}) collective-permute-start(bf16[784,384]{1,0:T(8,128)(2,1)S(1)} %pad_maximum_fusion.1.x0), channel_id=1, source_target_pairs={{0,1},{1,0},{2,3},{3,2},{4,5},{5,4},{6,7},{7,6}} | collective-permute-start | bytes 1806344 | tf_op jit(solution)/shard_map/ppermute | solution.py:373
  22.1 8.1 %collective-permute-start.2 = (bf16[384,384]{1,0:T(8,128)(2,1)S(1)}, bf16[384,384]{1,0:T(8,128)(2,1)S(1)}, u32[]{:S(2)}, u32[]{:S(2)}) collective-permute-start(bf16[384,384]{1,0:T(8,128)(2,1)S(1)} %slice.32), channel_id=1, source_target_pairs={{0,4},{4,0},{1,5},{5,1},{2,6},{6,2},{3,7},{7,3}} | collective-permute-start | bytes 884744 | tf_op jit(solution)/shard_map/ppermute | solution.py:379
  32.2 4.7 %copy-start.2 = (bf16[784,384]{1,0:T(8,128)(2,1)}, bf16[784,384]{1,0:T(8,128)(2,1)S(1)}, u32[]{:S(2)}) copy-start(bf16[784,384]{1,0:T(8,128)(2,1)S(1)} %pad_maximum_fusion.2.x2) | copy-start | bytes 1806340
  32.2 4.7 %collective-permute-start.3 = (bf16[784,384]{1,0:T(8,128)(2,1)S(1)}, bf16[784,384]{1,0:T(8,128)(2,1)S(1)}, u32[]{:S(2)}, u32[]{:S(2)}) collective-permute-start(bf16[784,384]{1,0:T(8,128)(2,1)S(1)} %pad_maximum_fusion.2.x2), channel_id=1, source_target_pairs={{0,1},{1,0},{2,3},{3,2},{4,5},{5,4},{6,7},{7,6}} | collective-permute-start | bytes 1806344 | tf_op jit(solution)/shard_map/ppermute | solution.py:373
  32.3 12.2 %collective-permute-start.7 = (bf16[3,384,256]{2,1,0:T(8,128)(2,1)S(1)}, bf16[3,384,256]{2,1,0:T(8,128)(2,1)}, u32[]{:S(2)}, u32[]{:S(2)}) collective-permute-start(bf16[3,384,256]{2,1,0:T(8,128)(2,1)S(1)} %pad_maximum_fusion.3.w0), channel_id=1, source_target_pairs={{0,1},{1,0},{2,3},{3,2},{4,5},{5,4},{6,7},{7,6}} | collective-permute-start | bytes 1769480 | tf_op jit(solution)/shard_map/ppermute | solution.py:373
  34.1 10.3 %collective-permute-start.9 = (bf16[3,384,256]{2,1,0:T(8,128)(2,1)}, bf16[3,384,256]{2,1,0:T(8,128)(2,1)}, u32[]{:S(2)}, u32[]{:S(2)}) collective-permute-start(bf16[3,384,256]{2,1,0:T(8,128)(2,1)} %collective-permute-done.8.w2), channel_id=1, source_target_pairs={{0,1},{1,0},{2,3},{3,2},{4,5},{5,4},{6,7},{7,6}} | collective-permute-start | bytes 1769480 | tf_op jit(solution)/shard_map/ppermute | solution.py:373
  34.1 2.8 %collective-permute-start.6 = (bf16[2,384,256]{2,1,0:T(8,128)(2,1)}, bf16[2,384,256]{2,1,0:T(8,128)(2,1)S(1)}, u32[]{:S(2)}, u32[]{:S(2)}) collective-permute-start(bf16[2,384,256]{2,1,0:T(8,128)(2,1)} %collective-permute-done.5.w2), channel_id=1, source_target_pairs={{0,1},{1,0},{2,3},{3,2},{4,5},{5,4},{6,7},{7,6}} | collective-permute-start | bytes 1179656 | tf_op jit(solution)/shard_map/ppermute | solution.py:373
  36.9 0.7 copy-start.11
  36.9 0.9 copy-start.8
  65.8 8.9 %copy-start.9 = (bf16[768,384]{1,0:T(8,128)(2,1)S(1)}, bf16[768,384]{1,0:T(8,128)(2,1)}, u32[]{:S(2)}) copy-start(bf16[768,384]{1,0:T(8,128)(2,1)} %param.26) | copy-start | bytes 1769476
  65.8 14.2 %collective-permute-start.11 = (bf16[64,9,256]{2,1,0:T(8,128)(2,1)}, bf16[64,9,256]{2,1,0:T(8,128)(2,1)S(1)}, u32[]{:S(2)}, u32[]{:S(2)}) collective-permute-start(bf16[64,9,256]{2,1,0:T(8,128)(2,1)} %bitcast.72), channel_id=1, source_target_pairs={{0,2},{2,0},{1,3},{3,1},{4,6},{6,4},{5,7},{7,5}} | collective-permute-start | bytes 884744 | tf_op jit(solution)/shard_map/ppermute | solution.py:376
  67.5 13.2 %collective-permute-start.10 = (bf16[64,9,256]{2,1,0:T(8,128)(2,1)}, bf16[64,9,256]{2,1,0:T(8,128)(2,1)S(1)}, u32[]{:S(2)}, u32[]{:S(2)}) collective-permute-start(bf16[64,9,256]{2,1,0:T(8,128)(2,1)} %bitcast.73), channel_id=1, source_target_pairs={{0,1},{1,0},{2,3},{3,2},{4,5},{5,4},{6,7},{7,6}} | collective-permute-start | bytes 884744 | tf_op jit(solution)/shard_map/ppermute | solution.py:373
  74.8 5.8 %copy-start.5 = (bf16[64,16,256]{2,1,0:T(8,128)(2,1)S(1)}, bf16[64,16,256]{2,1,0:T(8,128)(2,1)}, u32[]{:S(2)}) copy-start(bf16[64,16,256]{2,1,0:T(8,128)(2,1)} %attn.1) | copy-start | bytes 1572868
  80.0 1.9 collective-permute-start.12
  80.0 32.4 %collective-permute-start.16 = (bf16[40,384,128]{2,1,0:T(8,128)(2,1)}, bf16[40,384,128]{2,1,0:T(8,128)(2,1)}, u32[]{:S(2)}, u32[]{:S(2)}) collective-permute-start(bf16[40,384,128]{2,1,0:T(8,128)(2,1)} %constant_dynamic-slice_fusion.2), channel_id=1, source_target_pairs={{0,1},{1,0},{2,3},{3,2},{4,5},{5,4},{6,7},{7,6}} | collective-permute-start | bytes 11796488 | tf_op jit(solution)/shard_map/ppermute | solution.py:373
  80.5 31.9 %collective-permute-start.17 = (bf16[40,384,128]{2,1,0:T(8,128)(2,1)}, bf16[40,384,128]{2,1,0:T(8,128)(2,1)}, u32[]{:S(2)}, u32[]{:S(2)}) collective-permute-start(bf16[40,384,128]{2,1,0:T(8,128)(2,1)} %constant_dynamic-slice_fusion.1), channel_id=1, source_target_pairs={{0,1},{1,0},{2,3},{3,2},{4,5},{5,4},{6,7},{7,6}} | collective-permute-start | bytes 11796488 | tf_op jit(solution)/shard_map/ppermute | solution.py:373
  84.7 15.4 %collective-permute-start.13 = (bf16[768,384]{1,0:T(8,128)(2,1)S(1)}, bf16[768,384]{1,0:T(8,128)(2,1)S(1)}, u32[]{:S(2)}, u32[]{:S(2)}) collective-permute-start(bf16[768,384]{1,0:T(8,128)(2,1)S(1)} %convolution_convert_fusion), channel_id=1, source_target_pairs={{0,4},{4,0},{1,5},{5,1},{2,6},{6,2},{3,7},{7,3}} | collective-permute-start | bytes 1769480 | tf_op jit(solution)/shard_map/ppermute | solution.py:379
  99.8 0.8 copy-start.17
  100.5 2.0 collective-permute-start.14
  100.5 6.2 %collective-permute-start.19 = (bf16[384,40]{0,1:T(8,128)(2,1)S(1)}, bf16[384,40]{0,1:T(8,128)(2,1)S(1)}, u32[]{:S(2)}, u32[]{:S(2)}) collective-permute-start(bf16[384,40]{0,1:T(8,128)(2,1)S(1)} %copy-done.17), channel_id=1, source_target_pairs={{0,1},{1,0},{2,3},{3,2},{4,5},{5,4},{6,7},{7,6}} | collective-permute-start | bytes 92168 | tf_op jit(solution)/shard_map/ppermute | solution.py:373
  102.7 3.6 %collective-permute-start.15 = (f32[768]{0:T(1024)S(1)}, f32[768]{0:T(1024)S(1)}, u32[]{:S(2)}, u32[]{:S(2)}) collective-permute-start(f32[768]{0:T(1024)S(1)} %add.87), channel_id=1, source_target_pairs={{0,2},{2,0},{1,3},{3,1},{4,6},{6,4},{5,7},{7,5}} | collective-permute-start | bytes 9224 | tf_op jit(solution)/shard_map/ppermute | solution.py:376
  105.1 63.0 %collective-permute-start.22 = (bf16[40,128,384]{2,1,0:T(8,128)(2,1)}, bf16[40,128,384]{2,1,0:T(8,128)(2,1)}, u32[]{:S(2)}, u32[]{:S(2)}) collective-permute-start(bf16[40,128,384]{2,1,0:T(8,128)(2,1)} %constant_dynamic-slice_fusion), channel_id=1, source_target_pairs={{0,1},{1,0},{2,3},{3,2},{4,5},{5,4},{6,7},{7,6}} | collective-permute-start | bytes 11796488 | tf_op jit(solution)/shard_map/ppermute | solution.py:373
  107.2 4.9 %collective-permute-start.20 = (f32[768,40]{0,1:T(8,128)S(1)}, f32[768,40]{0,1:T(8,128)S(1)}, u32[]{:S(2)}, u32[]{:S(2)}) collective-permute-start(f32[768,40]{0,1:T(8,128)S(1)} %fusion.10), channel_id=1, source_target_pairs={{0,2},{2,0},{1,3},{3,1},{4,6},{6,4},{5,7},{7,5}} | collective-permute-start | bytes 368648 | tf_op jit(solution)/shard_map/ppermute | solution.py:376
  128.3 37.1 %collective-permute-start.18 = (bf16[8,384,256]{2,1,0:T(8,128)(2,1)}, bf16[8,384,256]{2,1,0:T(8,128)(2,1)}, u32[]{:S(2)}, u32[]{:S(2)}) collective-permute-start(bf16[8,384,256]{2,1,0:T(8,128)(2,1)} %moe1.2), channel_id=1, source_target_pairs={{0,2},{2,0},{1,3},{3,1},{4,6},{6,4},{5,7},{7,5}} | collective-permute-start | bytes 4718600 | tf_op jit(solution)/shard_map/ppermute | solution.py:376
  145.8 19.6 %copy-start = (bf16[8,384,256]{2,1,0:T(8,128)(2,1)S(1)}, bf16[8,384,256]{2,1,0:T(8,128)(2,1)}, u32[]{:S(2)}) copy-start(bf16[8,384,256]{2,1,0:T(8,128)(2,1)} %moe1.3) | copy-start | bytes 4718596
  167.8 0.9 copy-start.1
  167.8 19.0 %collective-permute-start.21 = (bf16[8,384,128]{2,1,0:T(8,128)(2,1)S(1)}, bf16[8,384,128]{2,1,0:T(8,128)(2,1)S(1)}, u32[]{:S(2)}, u32[]{:S(2)}) collective-permute-start(bf16[8,384,128]{2,1,0:T(8,128)(2,1)S(1)} %fusion.u_ref), channel_id=1, source_target_pairs={{0,2},{2,0},{1,3},{3,1},{4,6},{6,4},{5,7},{7,5}} | collective-permute-start | bytes 2359304 | tf_op jit(solution)/shard_map/ppermute | solution.py:376
  179.4 7.3 %copy-start.10 = (f32[384,384]{1,0:T(8,128)S(1)}, f32[384,384]{1,0:T(8,128)}, u32[]{:S(2)}) copy-start(f32[384,384]{1,0:T(8,128)} %get-tuple-element.107) | copy-start | bytes 1769476
  179.4 7.3 %collective-permute-start.23 = (bf16[384,384]{1,0:T(8,128)(2,1)}, bf16[384,384]{1,0:T(8,128)(2,1)S(1)}, u32[]{:S(2)}, u32[]{:S(2)}) collective-permute-start(bf16[384,384]{1,0:T(8,128)(2,1)} %get-tuple-element.108), channel_id=1, source_target_pairs={{0,1},{1,0},{2,3},{3,2},{4,5},{5,4},{6,7},{7,6}} | collective-permute-start | bytes 884744 | tf_op jit(solution)/shard_map/ppermute | solution.py:373
  186.8 0.9 copy-start.7
  198.5 1.9 collective-permute-start.25
  198.8 11.3 %collective-permute-start.24 = (bf16[384,384]{1,0:T(8,128)(2,1)S(1)}, bf16[384,384]{1,0:T(8,128)(2,1)S(1)}, u32[]{:S(2)}, u32[]{:S(2)}) collective-permute-start(bf16[384,384]{1,0:T(8,128)(2,1)S(1)} %add_convert_fusion.2), channel_id=1, source_target_pairs={{0,4},{4,0},{1,5},{5,1},{2,6},{6,2},{3,7},{7,3}} | collective-permute-start | bytes 884744 | tf_op jit(solution)/shard_map/ppermute | solution.py:379
  201.5 12.7 %collective-permute-start.26 = (bf16[384,384]{1,0:T(8,128)(2,1)S(1)}, bf16[384,384]{1,0:T(8,128)(2,1)S(1)}, u32[]{:S(2)}, u32[]{:S(2)}) collective-permute-start(bf16[384,384]{1,0:T(8,128)(2,1)S(1)} %add_convert_fusion.1), channel_id=1, source_target_pairs={{0,4},{4,0},{1,5},{5,1},{2,6},{6,2},{3,7},{7,3}} | collective-permute-start | bytes 884744 | tf_op jit(solution)/shard_map/ppermute | solution.py:379
